TPU v7x, 32 devices: a whole 2x2x4 slice. The times are simulated.
32 devices in a mesh: blk: 16 (over z, y, core), rep: 2 (over x).
Axes of the slice: x: 2, y: 2, z: 4, core: 2. Of those that a mesh axis runs over, the one named last changes fastest.
Arguments:
- queries: bfloat16 [4096, 1024], P('blk'), may hold values from -20 to 20
- corpus: bfloat16 [2, 32768, 1024], P('rep', 'blk'), may hold values from -5 to 5
- attributions: bfloat16 [2, 32768, 1024], P('rep', 'blk'), may hold values from -6 to 6
Outputs:
- attributed: bfloat16 [4096, 1024], P('blk')
- log_total: float32 [4096], P('blk')
All inputs are finite; a program needn't handle non-finite values.
Results may differ from a plain program's by a relative error of at most 0.003.
Values may be sent and summed in bfloat16 or wider, within the bound.
No kernel may reach another device: no remote copies, remote signals or barrier semaphores. Data moves between devices by JAX's collectives and lax.ppermute only.
A program may use at most 64 MiB of HBM per device.

v0:
```python
import jax
import jax.numpy as jnp
from jax import lax
from jax.sharding import PartitionSpec as P

STEPS = 4


sharpness = 2.5


def from_behind(value, axis, by):
    devices = lax.axis_size(axis)
    return lax.ppermute(value, axis, [(i, (i + by) % devices) for i in range(devices)])


def joined_2(value, axis, combine):
    everything = jax.tree.map(lambda part: lax.all_gather(part, axis), value)
    initial = jax.tree.map(lambda part: part[0], everything)

    def hop(k, so_far):
        return combine(so_far, jax.tree.map(lambda part: part[k], everything))

    return lax.fori_loop(1, lax.axis_size(axis), hop, initial)


def partial_stats(block_queries, slab_keys, slab_values):
    scores = jnp.dot(block_queries, slab_keys.T, preferred_element_type=jnp.float32) * (
        sharpness / jnp.sqrt(jnp.float32(block_queries.shape[1]))
    )
    row_max = jnp.max(scores, axis=1)
    weights = jnp.exp(scores - row_max[:, None])
    row_sum = jnp.sum(weights, axis=1)
    weighted = jnp.dot(
        weights.astype(jnp.bfloat16), slab_values, preferred_element_type=jnp.float32
    )
    return (row_max, row_sum, weighted)


def combine(left_part, right_part):
    joined = jnp.maximum(left_part[0], right_part[0])
    left_factor = jnp.exp(left_part[0] - joined)
    right_factor = jnp.exp(right_part[0] - joined)
    row_sum = left_part[1] * left_factor + right_part[1] * right_factor
    weighted = left_part[2] * left_factor[:, None] + right_part[2] * right_factor[:, None]
    return (joined, row_sum, weighted)


def shards(queries, corpus, attributions):
    slab_keys = corpus[0]
    slab_values = attributions[0]
    running = partial_stats(queries, slab_keys, slab_values)
    visiting = queries
    for rounds in range(STEPS - 1):
        visiting = from_behind(visiting, "blk", 1)
        moved = from_behind((running[0], running[1], running[2]), "blk", 1)
        running = combine(moved, partial_stats(visiting, slab_keys, slab_values))
    running = from_behind((running[0], running[1], running[2]), "blk", 1 - STEPS)
    running = joined_2((running[0], running[1], running[2]), "rep", combine)
    attributed = (running[2] / running[1][:, None]).astype(jnp.bfloat16)
    log_total = running[0] + jnp.log(running[1])
    return (attributed, log_total)


def solution(mesh):
    return jax.shard_map(
        shards,
        mesh=mesh,
        in_specs=(P("blk", None), P("rep", "blk", None), P("rep", "blk", None)),
        out_specs=(P("blk", None), P("blk")),
        check_vma=False,
    )
```

profile of v0, /device:TPU:0, one launch (start us, length us, event | category | flops | bytes accessed | tf_op | source)
XLA Modules:
  0.0 140.8 jit_solution(2259220138937067912)
XLA Ops:
  7.2 0.5 collective-permute-start.2
  7.8 4.0 %fusion.52 = (f32[256]{0:T(256)S(1)}, f32[256,2048]{1,0:T(8,128)S(1)}) fusion(bf16[256,1024]{1,0:T(8,128)(2,1)} %param.3, bf16[1,2048,1024]{2,1,0:T(8,128)(2,1)} %param.4), kind=kOutput, calls=%fused_computation.62 | convolution fusion | flops 1074790144 | bytes 6816768 | tf_op jit(solution)/shard_map/dot_general | solution.py:28
  11.8 1.4 fusion.6
  13.2 2.4 %collective-permute-start = (f32[256,1024]{1,0:T(8,128)S(1)}, f32[256,1024]{1,0:T(8,128)S(1)}, u32[]{:S(2)}, u32[]{:S(2)}) collective-permute-start(f32[256,1024]{1,0:T(8,128)S(1)} %fusion.6), channel_id=1, source_target_pairs={{0,2},{2,4},{4,6},{6,8},{8,10},{10,12},{12,14},{14,16},{16,18},{18... | collective-permute-start | bytes 3145736 | tf_op jit(solution)/shard_map/ppermute | solution.py:14
  15.7 0.4 fusion.28
  16.1 1.5 %collective-permute-start.11 = (f32[256]{0:T(256)S(1)}, f32[256]{0:T(256)S(1)}, u32[]{:S(2)}, u32[]{:S(2)}) collective-permute-start(f32[256]{0:T(256)S(1)} %fusion.28), channel_id=1, source_target_pairs={{0,2},{2,4},{4,6},{6,8},{8,10},{10,12},{12,14},{14,16},{16,18},{18... | collective-permute-start | bytes 3080 | tf_op jit(solution)/shard_map/ppermute | solution.py:14
  17.7 2.2 %collective-permute-done.2 = bf16[256,1024]{1,0:T(8,128)(2,1)S(1)} collective-permute-done((bf16[256,1024]{1,0:T(8,128)(2,1)}, bf16[256,1024]{1,0:T(8,128)(2,1)S(1)}, u32[]{:S(2)}, u32[]{:S(2)}) %collective-permute-start.2) | collective-permute-done | bytes 524320 | tf_op jit(solution)/shard_map/ppermute | solution.py:14
  19.8 1.4 fusion.51
  21.2 0.4 fusion.30
  21.6 9.5 %collective-permute-done.11 = f32[256]{0:T(256)S(1)} collective-permute-done((f32[256]{0:T(256)S(1)}, f32[256]{0:T(256)S(1)}, u32[]{:S(2)}, u32[]{:S(2)}) %collective-permute-start.11) | collective-permute-done | bytes 1056 | tf_op jit(solution)/shard_map/ppermute | solution.py:14
  31.3 1.4 %multiply_add_fusion.2 = f32[256,1024]{1,0:T(8,128)S(1)} fusion(f32[256,1024]{1,0:T(8,128)S(1)} %collective-permute-done, f32[256]{0:T(256)S(1)} %get-tuple-element.40, f32[256]{0:T(256)S(1)} %get-tuple-element.39, bf16[1,2048,1024]{2,1,0:T(8,128)(2,1)S(1)} %copy-done.2, f32[256,2048]{1,0:T(8,128)S(1)} %get-tuple-element.51, f32[256]{0:T(256)S(1)} %get-tuple-element.50), kind=kOutput, calls=%fused_computation.40 | convolution fusion | flops 1075576832 | bytes 8391680 | tf_op jit(solution)/shard_map/dot_general | solution.py:34
  32.8 1.8 %collective-permute-start.3 = (f32[256,1024]{1,0:T(8,128)S(1)}, f32[256,1024]{1,0:T(8,128)S(1)}, u32[]{:S(2)}, u32[]{:S(2)}) collective-permute-start(f32[256,1024]{1,0:T(8,128)S(1)} %multiply_add_fusion.2), channel_id=1, source_target_pairs={{0,2},{2,4},{4,6},{6,8},{8,10},{10,12},{12,14},{14,16},{16,18},{18... | collective-permute-start | bytes 3145736 | tf_op jit(solution)/shard_map/ppermute | solution.py:14
  34.6 8.0 %collective-permute-done.5 = bf16[256,1024]{1,0:T(8,128)(2,1)S(1)} collective-permute-done((bf16[256,1024]{1,0:T(8,128)(2,1)S(1)}, bf16[256,1024]{1,0:T(8,128)(2,1)S(1)}, u32[]{:S(2)}, u32[]{:S(2)}) %collective-permute-start.5) | collective-permute-done | bytes 524320 | tf_op jit(solution)/shard_map/ppermute | solution.py:14
  42.6 1.4 fusion.50
  44.0 1.3 fusion.2
  45.3 0.4 fusion.32
  46.0 7.9 %collective-permute-done.3 = f32[256,1024]{1,0:T(8,128)S(1)} collective-permute-done((f32[256,1024]{1,0:T(8,128)S(1)}, f32[256,1024]{1,0:T(8,128)S(1)}, u32[]{:S(2)}, u32[]{:S(2)}) %collective-permute-start.3) | collective-permute-done | bytes 1048608 | tf_op jit(solution)/shard_map/ppermute | solution.py:14
  54.1 5.4 %collective-permute-done.8 = bf16[256,1024]{1,0:T(8,128)(2,1)S(1)} collective-permute-done((bf16[256,1024]{1,0:T(8,128)(2,1)S(1)}, bf16[256,1024]{1,0:T(8,128)(2,1)S(1)}, u32[]{:S(2)}, u32[]{:S(2)}) %collective-permute-start.8) | collective-permute-done | bytes 524320 | tf_op jit(solution)/shard_map/ppermute | solution.py:14
  59.5 1.4 fusion.49
  60.9 0.4 fusion.34
  61.3 1.4 fusion
  62.7 8.3 %collective-permute-done.6 = f32[256,1024]{1,0:T(8,128)S(1)} collective-permute-done((f32[256,1024]{1,0:T(8,128)S(1)}, f32[256,1024]{1,0:T(8,128)S(1)}, u32[]{:S(2)}, u32[]{:S(2)}) %collective-permute-start.6) | collective-permute-done | bytes 1048608 | tf_op jit(solution)/shard_map/ppermute | solution.py:14
  71.0 0.2 multiply_add_fusion
  71.3 22.4 %collective-permute-done.9 = f32[256,1024]{1,0:T(8,128)S(1)} collective-permute-done((f32[256,1024]{1,0:T(8,128)S(1)}, f32[256,1024]{1,0:T(8,128)S(1)}, u32[]{:S(2)}, u32[]{:S(2)}) %collective-permute-start.9) | collective-permute-done | bytes 1048608 | tf_op jit(solution)/shard_map/ppermute | solution.py:14
  93.7 1.0 copy-done
  94.7 3.8 %collective-permute-start.14 = (f32[256]{0:T(256)S(1)}, f32[256]{0:T(256)S(1)}, u32[]{:S(2)}, u32[]{:S(2)}) collective-permute-start(f32[256]{0:T(256)S(1)} %get-tuple-element.22), channel_id=1, source_target_pairs={{0,26},{2,28},{4,30},{6,0},{8,2},{10,4},{12,6},{14,8},{16,10},{18,... | collective-permute-start | bytes 3080 | tf_op jit(solution)/shard_map/ppermute | solution.py:14
  98.5 1.3 collective-permute-start.10
  99.8 4.2 %all-gather.4 = f32[2,1,256]{2,1,0:T(1,128)S(1)} all-gather(f32[1,1,256]{2,1,0:T(1,128)S(1)} %bitcast.51), channel_id=4, replica_groups=mesh['blk'=16,'rep'=2] {'rep'}, dimensions={0}, use_global_device_ids=true | all-gather | bytes 3072 | tf_op jit(solution)/shard_map/all_gather | solution.py:18
  104.0 4.2 %all-gather.3 = f32[2,1,256]{2,1,0:T(1,128)S(1)} all-gather(f32[1,1,256]{2,1,0:T(1,128)S(1)} %bitcast.50), channel_id=3, replica_groups=mesh['blk'=16,'rep'=2] {'rep'}, dimensions={0}, use_global_device_ids=true | all-gather | bytes 3072 | tf_op jit(solution)/shard_map/all_gather | solution.py:18
  108.2 0.6 log_add_fusion
  108.8 22.6 %all-gather.7.cloned.1.call-done = f32[512,1024]{1,0:T(8,128)} async-done(((f32[256,1024]{1,0:T(8,128)}), f32[512,1024]{1,0:T(8,128)}) %all-gather.7.cloned.1.call-update) | async-done | bytes 2097168 | tf_op jit(solution)/shard_map/all_gather | solution.py:18
  131.4 2.6 %fusion.46 = bf16[256,1024]{1,0:T(8,128)(2,1)} fusion(f32[512,1024]{1,0:T(8,128)} %all-gather.7.cloned.1.call-done, f32[256]{0:T(256)S(1)} %get-tuple-element.19, f32[256]{0:T(256)S(1)} %get-tuple-element.21, f32[256]{0:T(256)S(1)} %get-tuple-element.20), kind=kLoop, calls=%fused_computation.43 | loop fusion | flops 1310720 | bytes 2624512 | tf_op jit(solution)/shard_map/convert_element_type | solution.py:60
  (30 shorter events, 0.9 us)
Async XLA Ops:
  7.2 124.2 %all-gather.7.cloned.1.call-start = ((), (), s32[]{:S(2)}) async-start(), calls=%async_computation | async-start | bytes 3145728 | tf_op jit(solution)/shard_map/all_gather | solution.py:18
  7.2 4.5 %copy-start.2 = (bf16[1,2048,1024]{2,1,0:T(8,128)(2,1)S(1)}, bf16[1,2048,1024]{2,1,0:T(8,128)(2,1)}, u32[]{:S(2)}) copy-start(bf16[1,2048,1024]{2,1,0:T(8,128)(2,1)} %param.5) | copy-start | bytes 12582916
  7.2 12.6 %collective-permute-start.2 = (bf16[256,1024]{1,0:T(8,128)(2,1)}, bf16[256,1024]{1,0:T(8,128)(2,1)S(1)}, u32[]{:S(2)}, u32[]{:S(2)}) collective-permute-start(bf16[256,1024]{1,0:T(8,128)(2,1)} %param.3), channel_id=1, source_target_pairs={{0,2},{2,4},{4,6},{6,8},{8,10},{10,12},{12,14},{14,16},{16,18},{18... | collective-permute-start | bytes 1572872 | tf_op jit(solution)/shard_map/ppermute | solution.py:14
  11.8 8.1 %copy-start.1 = (bf16[1,2048,1024]{2,1,0:T(8,128)(2,1)S(1)}, bf16[1,2048,1024]{2,1,0:T(8,128)(2,1)}, u32[]{:S(2)}) copy-start(bf16[1,2048,1024]{2,1,0:T(8,128)(2,1)} %param.4) | copy-start | bytes 12582916
  13.2 18.2 %collective-permute-start = (f32[256,1024]{1,0:T(8,128)S(1)}, f32[256,1024]{1,0:T(8,128)S(1)}, u32[]{:S(2)}, u32[]{:S(2)}) collective-permute-start(f32[256,1024]{1,0:T(8,128)S(1)} %fusion.6), channel_id=1, source_target_pairs={{0,2},{2,4},{4,6},{6,8},{8,10},{10,12},{12,14},{14,16},{16,18},{18... | collective-permute-start | bytes 3145736 | tf_op jit(solution)/shard_map/ppermute | solution.py:14
  15.5 15.6 %collective-permute-start.1 = (f32[256]{0:T(256)S(1)}, f32[256]{0:T(256)S(1)}, u32[]{:S(2)}, u32[]{:S(2)}) collective-permute-start(f32[256]{0:T(256)S(1)} %get-tuple-element.52), channel_id=1, source_target_pairs={{0,2},{2,4},{4,6},{6,8},{8,10},{10,12},{12,14},{14,16},{16,18},{18... | collective-permute-start | bytes 3080 | tf_op jit(solution)/shard_map/ppermute | solution.py:14
  16.1 15.0 %collective-permute-start.11 = (f32[256]{0:T(256)S(1)}, f32[256]{0:T(256)S(1)}, u32[]{:S(2)}, u32[]{:S(2)}) collective-permute-start(f32[256]{0:T(256)S(1)} %fusion.28), channel_id=1, source_target_pairs={{0,2},{2,4},{4,6},{6,8},{8,10},{10,12},{12,14},{14,16},{16,18},{18... | collective-permute-start | bytes 3080 | tf_op jit(solution)/shard_map/ppermute | solution.py:14
  31.1 14.7 %collective-permute-start.12 = (f32[256]{0:T(256)S(1)}, f32[256]{0:T(256)S(1)}, u32[]{:S(2)}, u32[]{:S(2)}) collective-permute-start(f32[256]{0:T(256)S(1)} %get-tuple-element.38), channel_id=1, source_target_pairs={{0,2},{2,4},{4,6},{6,8},{8,10},{10,12},{12,14},{14,16},{16,18},{18... | collective-permute-start | bytes 3080 | tf_op jit(solution)/shard_map/ppermute | solution.py:14
  31.2 14.6 %collective-permute-start.4 = (f32[256]{0:T(256)S(1)}, f32[256]{0:T(256)S(1)}, u32[]{:S(2)}, u32[]{:S(2)}) collective-permute-start(f32[256]{0:T(256)S(1)} %get-tuple-element.41), channel_id=1, source_target_pairs={{0,2},{2,4},{4,6},{6,8},{8,10},{10,12},{12,14},{14,16},{16,18},{18... | collective-permute-start | bytes 3080 | tf_op jit(solution)/shard_map/ppermute | solution.py:14
  31.3 11.4 %collective-permute-start.5 = (bf16[256,1024]{1,0:T(8,128)(2,1)S(1)}, bf16[256,1024]{1,0:T(8,128)(2,1)S(1)}, u32[]{:S(2)}, u32[]{:S(2)}) collective-permute-start(bf16[256,1024]{1,0:T(8,128)(2,1)S(1)} %collective-permute-done.2), channel_id=1, source_target_pairs={{0,2},{2,4},{4,6},{6,8},{8,10},{10,12},{12,14},{14,16},{16,18},{18... | collective-permute-start | bytes 1572872 | tf_op jit(solution)/shard_map/ppermute | solution.py:14
  32.8 21.1 %collective-permute-start.3 = (f32[256,1024]{1,0:T(8,128)S(1)}, f32[256,1024]{1,0:T(8,128)S(1)}, u32[]{:S(2)}, u32[]{:S(2)}) collective-permute-start(f32[256,1024]{1,0:T(8,128)S(1)} %multiply_add_fusion.2), channel_id=1, source_target_pairs={{0,2},{2,4},{4,6},{6,8},{8,10},{10,12},{12,14},{14,16},{16,18},{18... | collective-permute-start | bytes 3145736 | tf_op jit(solution)/shard_map/ppermute | solution.py:14
  45.8 13.7 %collective-permute-start.8 = (bf16[256,1024]{1,0:T(8,128)(2,1)S(1)}, bf16[256,1024]{1,0:T(8,128)(2,1)S(1)}, u32[]{:S(2)}, u32[]{:S(2)}) collective-permute-start(bf16[256,1024]{1,0:T(8,128)(2,1)S(1)} %collective-permute-done.5), channel_id=1, source_target_pairs={{0,2},{2,4},{4,6},{6,8},{8,10},{10,12},{12,14},{14,16},{16,18},{18... | collective-permute-start | bytes 1572872 | tf_op jit(solution)/shard_map/ppermute | solution.py:14
  45.9 15.4 %collective-permute-start.13 = (f32[256]{0:T(256)S(1)}, f32[256]{0:T(256)S(1)}, u32[]{:S(2)}, u32[]{:S(2)}) collective-permute-start(f32[256]{0:T(256)S(1)} %get-tuple-element.34), channel_id=1, source_target_pairs={{0,2},{2,4},{4,6},{6,8},{8,10},{10,12},{12,14},{14,16},{16,18},{18... | collective-permute-start | bytes 3080 | tf_op jit(solution)/shard_map/ppermute | solution.py:14
  45.9 15.4 %collective-permute-start.7 = (f32[256]{0:T(256)S(1)}, f32[256]{0:T(256)S(1)}, u32[]{:S(2)}, u32[]{:S(2)}) collective-permute-start(f32[256]{0:T(256)S(1)} %get-tuple-element.37), channel_id=1, source_target_pairs={{0,2},{2,4},{4,6},{6,8},{8,10},{10,12},{12,14},{14,16},{16,18},{18... | collective-permute-start | bytes 3080 | tf_op jit(solution)/shard_map/ppermute | solution.py:14
  54.0 17.0 %collective-permute-start.6 = (f32[256,1024]{1,0:T(8,128)S(1)}, f32[256,1024]{1,0:T(8,128)S(1)}, u32[]{:S(2)}, u32[]{:S(2)}) collective-permute-start(f32[256,1024]{1,0:T(8,128)S(1)} %multiply_add_fusion.1), channel_id=1, source_target_pairs={{0,2},{2,4},{4,6},{6,8},{8,10},{10,12},{12,14},{14,16},{16,18},{18... | collective-permute-start | bytes 3145736 | tf_op jit(solution)/shard_map/ppermute | solution.py:14
  71.2 22.5 %collective-permute-start.9 = (f32[256,1024]{1,0:T(8,128)S(1)}, f32[256,1024]{1,0:T(8,128)S(1)}, u32[]{:S(2)}, u32[]{:S(2)}) collective-permute-start(f32[256,1024]{1,0:T(8,128)S(1)} %multiply_add_fusion), channel_id=1, source_target_pairs={{0,26},{2,28},{4,30},{6,0},{8,2},{10,4},{12,6},{14,8},{16,10},{18,... | collective-permute-start | bytes 3145736 | tf_op jit(solution)/shard_map/ppermute | solution.py:14
  93.7 1.0 copy-start
  94.7 5.1 %collective-permute-start.14 = (f32[256]{0:T(256)S(1)}, f32[256]{0:T(256)S(1)}, u32[]{:S(2)}, u32[]{:S(2)}) collective-permute-start(f32[256]{0:T(256)S(1)} %get-tuple-element.22), channel_id=1, source_target_pairs={{0,26},{2,28},{4,30},{6,0},{8,2},{10,4},{12,6},{14,8},{16,10},{18,... | collective-permute-start | bytes 3080 | tf_op jit(solution)/shard_map/ppermute | solution.py:14
  98.5 5.5 %collective-permute-start.10 = (f32[256]{0:T(256)S(1)}, f32[256]{0:T(256)S(1)}, u32[]{:S(2)}, u32[]{:S(2)}) collective-permute-start(f32[256]{0:T(256)S(1)} %get-tuple-element.33), channel_id=1, source_target_pairs={{0,26},{2,28},{4,30},{6,0},{8,2},{10,4},{12,6},{14,8},{16,10},{18,... | collective-permute-start | bytes 3080 | tf_op jit(solution)/shard_map/ppermute | solution.py:14
Sparse Core Ops, SparseCore 0:
  94.8 36.5 all-gather.6
where the time goes:
time: 141 us
  waiting for transfers between devices  86.2 us (61%)
  between operations  14.2 us (10%)
  matrix products  13.6 us (10%)
  starting transfers between devices  12 us (9%)
  blocking collectives  8.46 us (6%)
  other arithmetic  5.29 us (4%)
    ppermute x15, waiting for transfers between devices, from_behind(): lax.ppermute(value, axis, [(i, (i + by) % devices) for i in range(devices)])  63.6 us
    all_gather x1, waiting for transfers between devices, joined_2(): everything = jax.tree.map(lambda part: lax.all_gather(part, axis), value)  22.6 us
    ppermute x15, starting transfers between devices, from_behind(): lax.ppermute(value, axis, [(i, (i + by) % devices) for i in range(devices)])  12 us
    all_gather x2, blocking collectives, joined_2(): everything = jax.tree.map(lambda part: lax.all_gather(part, axis), value)  8.46 us
    dot_general x4, matrix products, partial_stats(): jnp.dot(block_queries, slab_keys.T, preferred_element_type=jnp.float32)  8.12 us
    dot_general x4, matrix products, partial_stats(): jnp.dot(weights.astype(jnp.bfloat16), slab_values, preferred_element_type...  5.49 us
  transfers between devices with their start and end apart: 16, of which 8 were waited for; matrix products, arithmetic and copies ran while one was open for 11% of the time, Pallas kernels for 0%

commit v1 on v0

v1 whole, which is shorter than its diff:
```python
import jax
import jax.numpy as jnp
from jax import lax
from jax.sharding import PartitionSpec as P

sharpness = 2.5


def partial_stats(block_queries, slab_keys, slab_values):
    scores = jnp.dot(block_queries, slab_keys.T, preferred_element_type=jnp.float32) * (
        sharpness / jnp.sqrt(jnp.float32(block_queries.shape[1]))
    )
    row_max = jnp.max(scores, axis=1, keepdims=True)
    weights = jnp.exp(scores - row_max)
    row_sum = jnp.sum(weights, axis=1, keepdims=True)
    weighted = jnp.dot(
        weights.astype(jnp.bfloat16), slab_values, preferred_element_type=jnp.float32
    )
    return weighted / row_sum, row_max + jnp.log(row_sum)


def joined(parts):
    top = parts[0][1]
    for _, level in parts[1:]:
        top = jnp.maximum(top, level)
    total = 0.0
    mean = 0.0
    for value, level in parts:
        share = jnp.exp(level - top)
        total = total + share
        mean = mean + value.astype(jnp.float32) * share
    return mean / total, top + jnp.log(total)


def packed(part):
    return part[0].astype(jnp.float16), part[1]


def shards(queries, corpus, attributions):
    keys = corpus[0]
    values = attributions[0]
    n = lax.axis_size("blk")
    two = [(b, (b + 2) % n) for b in range(n)]
    two_back = [(d, s) for s, d in two]
    fourth = [(b, (b + (3 if b % 2 else 1)) % n) for b in range(n)]
    fourth_back = [(d, s) for s, d in fourth]
    pair = [(b, b ^ 1) for b in range(n)]

    def move(tree, pairs, axis="blk"):
        return jax.tree.map(lambda x: lax.ppermute(x, axis, pairs), tree)

    near = move(queries, two)
    other = move(queries, fourth)
    far = move(near, pair)
    own = partial_stats(queries, keys, values)
    near_part = partial_stats(near, keys, values)
    far_part = packed(partial_stats(far, keys, values))
    other_part = packed(partial_stats(other, keys, values))
    other_back = move(other_part, fourth_back)
    far_back = move(far_part, pair)
    near_back = move(packed(joined([near_part, far_back])), two_back)
    mine = packed(joined([own, other_back, near_back]))
    theirs = move(mine, [(0, 1), (1, 0)], "rep")
    first = lax.axis_index("rep") == 0
    a = jax.tree.map(lambda x, y: jnp.where(first, x, y), mine, theirs)
    b = jax.tree.map(lambda x, y: jnp.where(first, y, x), mine, theirs)
    attributed, log_total = joined([a, b])
    return attributed.astype(jnp.bfloat16), log_total[:, 0]


def solution(mesh):
    return jax.shard_map(
        shards,
        mesh=mesh,
        in_specs=(P("blk", None), P("rep", "blk", None), P("rep", "blk", None)),
        out_specs=(P("blk", None), P("blk")),
        check_vma=False,
    )
```

time: 141 us -> 67.2 us (0.48)
  waiting for transfers between devices: 86.2 us -> 32.2 us
  between operations: 14.2 us -> 0.73 us
  blocking collectives: 8.46 us -> 0 us
  starting transfers between devices: 12 us -> 16.5 us
    ppermute x15 -> x11, waiting for transfers between devices: 63.6 us -> 32.2 us  [move(): return jax.tree.map(lambda x: lax.ppermute(x, axis, pairs), tree)]
    all_gather x1 -> x0, waiting for transfers between devices: 22.6 us -> none  [joined_2(): everything = jax.tree.map(lambda part: lax.all_gather(part, axis), value)]
    all_gather x2 -> x0, blocking collectives: 8.46 us -> none  [joined_2(): everything = jax.tree.map(lambda part: lax.all_gather(part, axis), value)]
    ppermute x15 -> x11, starting transfers between devices: 12 us -> 16.5 us  [move(): return jax.tree.map(lambda x: lax.ppermute(x, axis, pairs), tree)]
  transfers between devices with their start and end apart: 16 -> 11, of which waited for: 8 -> 5; matrix products, arithmetic and copies ran while one was open for 11% -> 24% of each run, Pallas kernels for 0% -> 0%
where the time goes in v1:
time: 67.2 us; the launch traced here: 67.1 us
  waiting for transfers between devices  32.2 us (48%)
  starting transfers between devices  16.5 us (25%)
  matrix products  13.6 us (20%)
  other arithmetic  3.91 us (6%)
  between operations  0.73 us (1%)
    ppermute x11, waiting for transfers between devices, move(): return jax.tree.map(lambda x: lax.ppermute(x, axis, pairs), tree)  32.2 us
    ppermute x11, starting transfers between devices, move(): return jax.tree.map(lambda x: lax.ppermute(x, axis, pairs), tree)  16.5 us
    dot_general x4, matrix products, partial_stats(): jnp.dot(block_queries, slab_keys.T, preferred_element_type=jnp.float32)  8.07 us
    dot_general x4, matrix products, partial_stats(): jnp.dot(weights.astype(jnp.bfloat16), slab_values, preferred_element_type...  5.57 us
    reduce_sum x4, other arithmetic, partial_stats(): row_sum = jnp.sum(weights, axis=1, keepdims=True)  1.75 us
  transfers between devices with their start and end apart: 11, of which 5 were waited for; matrix products, arithmetic and copies ran while one was open for 24% of the time, Pallas kernels for 0%

profile of v1, /device:TPU:0, one launch (start us, length us, event | category | flops | bytes accessed | tf_op | source)
XLA Modules:
  0.0 67.1 jit_solution(1881559490123630483)
XLA Ops:
  0.6 3.0 %collective-permute-start.2 = (bf16[256,1024]{1,0:T(8,128)(2,1)}, bf16[256,1024]{1,0:T(8,128)(2,1)S(1)}, u32[]{:S(2)}, u32[]{:S(2)}) collective-permute-start(bf16[256,1024]{1,0:T(8,128)(2,1)} %param.3), channel_id=1, source_target_pairs={{0,4},{2,6},{4,8},{6,10},{8,12},{10,14},{12,16},{14,18},{16,20},{1... | collective-permute-start | bytes 1572872 | tf_op jit(solution)/shard_map/ppermute | solution.py:50
  3.7 0.0 collective-permute-start
  3.7 3.9 %fusion.50 = (f32[256]{0:T(256)S(1)}, f32[256,2048]{1,0:T(8,128)S(1)}) fusion(bf16[256,1024]{1,0:T(8,128)(2,1)} %param.3, bf16[1,2048,1024]{2,1,0:T(8,128)(2,1)} %param.4), kind=kOutput, calls=%fused_computation.63 | convolution fusion | flops 1074790144 | bytes 6816768 | tf_op jit(solution)/shard_map/dot_general | solution.py:10
  7.5 0.4 fusion.28
  8.0 0.0 copy-start
  8.0 1.4 %fusion.36 = f32[256,1024]{1,0:T(8,128)S(1)} fusion(bf16[1,2048,1024]{2,1,0:T(8,128)(2,1)S(1)} %copy-done.1, f32[256,2048]{1,0:T(8,128)S(1)} %get-tuple-element.20, f32[256]{0:T(256)S(1)} %get-tuple-element.19, f32[256]{0:T(256)S(1)} %fusion.28), kind=kOutput, calls=%fused_computation.32 | convolution fusion | flops 1075052544 | bytes 7342080 | tf_op jit(solution)/shard_map/dot_general | solution.py:16
  9.4 4.9 %collective-permute-done = bf16[256,1024]{1,0:T(8,128)(2,1)S(1)} collective-permute-done((bf16[256,1024]{1,0:T(8,128)(2,1)}, bf16[256,1024]{1,0:T(8,128)(2,1)S(1)}, u32[]{:S(2)}, u32[]{:S(2)}) %collective-permute-start) | collective-permute-done | bytes 524320 | tf_op jit(solution)/shard_map/ppermute | solution.py:50
  14.3 1.4 %fusion.51 = (f32[256]{0:T(256)S(1)}, f32[256,2048]{1,0:T(8,128)S(1)}) fusion(bf16[256,1024]{1,0:T(8,128)(2,1)S(1)} %collective-permute-done, bf16[1,2048,1024]{2,1,0:T(8,128)(2,1)S(1)} %copy-done), kind=kOutput, calls=%fused_computation.64 | convolution fusion | flops 1074790144 | bytes 6816768 | tf_op jit(solution)/shard_map/dot_general | solution.py:10
  15.7 0.4 fusion.31
  16.2 1.4 %divide_convert_fusion.4 = f16[256,1024]{1,0:T(8,128)(2,1)S(1)} fusion(f32[256]{0:T(256)S(1)} %fusion.31, bf16[1,2048,1024]{2,1,0:T(8,128)(2,1)S(1)} %copy-done.1, f32[256,2048]{1,0:T(8,128)S(1)} %get-tuple-element.22, f32[256]{0:T(256)S(1)} %get-tuple-element.21), kind=kOutput, calls=%fused_computation.37 | convolution fusion | flops 1075314688 | bytes 6817792 | tf_op jit(solution)/shard_map/dot_general | solution.py:16
  17.5 0.1 collective-permute-start.6
  17.6 2.1 %collective-permute-done.2 = bf16[256,1024]{1,0:T(8,128)(2,1)S(1)} collective-permute-done((bf16[256,1024]{1,0:T(8,128)(2,1)}, bf16[256,1024]{1,0:T(8,128)(2,1)S(1)}, u32[]{:S(2)}, u32[]{:S(2)}) %collective-permute-start.2) | collective-permute-done | bytes 524320 | tf_op jit(solution)/shard_map/ppermute | solution.py:50
  19.7 1.4 %fusion.48 = (f32[256]{0:T(256)S(1)}, f32[256,2048]{1,0:T(8,128)S(1)}) fusion(bf16[256,1024]{1,0:T(8,128)(2,1)S(1)} %collective-permute-done.2, bf16[1,2048,1024]{2,1,0:T(8,128)(2,1)S(1)} %copy-done), kind=kOutput, calls=%fused_computation.61 | convolution fusion | flops 1074790144 | bytes 6816768 | tf_op jit(solution)/shard_map/dot_general | solution.py:10
  21.1 0.4 fusion.33
  21.6 0.0 collective-permute-done.3
  21.6 1.4 %fusion.49 = (f32[256]{0:T(256)S(1)}, f32[256,2048]{1,0:T(8,128)S(1)}) fusion(bf16[256,1024]{1,0:T(8,128)(2,1)S(1)} %collective-permute-done.3, bf16[1,2048,1024]{2,1,0:T(8,128)(2,1)S(1)} %copy-done), kind=kOutput, calls=%fused_computation.62 | convolution fusion | flops 1074790144 | bytes 6816768 | tf_op jit(solution)/shard_map/dot_general | solution.py:10
  23.0 0.4 fusion.35
  23.4 1.4 %divide_convert_fusion.3 = f16[256,1024]{1,0:T(8,128)(2,1)S(1)} fusion(f32[256]{0:T(256)S(1)} %fusion.35, bf16[1,2048,1024]{2,1,0:T(8,128)(2,1)S(1)} %copy-done.1, f32[256,2048]{1,0:T(8,128)S(1)} %get-tuple-element.18, f32[256]{0:T(256)S(1)} %get-tuple-element.17), kind=kOutput, calls=%fused_computation.36 | convolution fusion | flops 1075314688 | bytes 6817792 | tf_op jit(solution)/shard_map/dot_general | solution.py:16
  24.8 0.5 collective-permute-start.7
  25.3 0.1 collective-permute-start.4
  25.4 1.4 %collective-permute-done.4 = f32[256,1]{0,1:T(1,128)S(1)} collective-permute-done((f32[256,1]{0,1:T(1,128)S(1)}, f32[256,1]{0,1:T(1,128)S(1)}, u32[]{:S(2)}, u32[]{:S(2)}) %collective-permute-start.4) | collective-permute-done | bytes 1056 | tf_op jit(solution)/shard_map/ppermute | solution.py:50
  26.9 1.5 %divide_convert_fusion.2 = f16[256,1024]{1,0:T(8,128)(2,1)S(1)} fusion(f16[256,1024]{1,0:T(8,128)(2,1)S(1)} %collective-permute-done.7, f32[256]{0:T(256)S(1)} %bitcast.73, f32[256]{0:T(256)S(1)} %bitcast.74, f32[256]{0:T(256)S(1)} %bitcast.75, f32[256]{0:T(256)S(1)} %fusion.33, bf16[1,2048,1024]{2,1,0:T(8,128)(2,1)S(1)} %copy-done.1, ...), kind=kOutput, calls=%fused_computation.35 | convolution fusion | flops 1076625408 | bytes 7345152 | tf_op jit(solution)/shard_map/dot_general | solution.py:16
  28.4 10.4 %collective-permute-start.8 = (f16[256,1024]{1,0:T(8,128)(2,1)S(1)}, f16[256,1024]{1,0:T(8,128)(2,1)S(1)}, u32[]{:S(2)}, u32[]{:S(2)}) collective-permute-start(f16[256,1024]{1,0:T(8,128)(2,1)S(1)} %divide_convert_fusion.2), channel_id=1, source_target_pairs={{4,0},{6,2},{8,4},{10,6},{12,8},{14,10},{16,12},{18,14},{20,16},{2... | collective-permute-start | bytes 1572872 | tf_op jit(solution)/shard_map/ppermute | solution.py:50
  38.8 0.3 collective-permute-start.5
  39.1 11.2 %collective-permute-done.1 = f32[256,1]{0,1:T(1,128)S(1)} collective-permute-done((f32[256,1]{0,1:T(1,128)S(1)}, f32[256,1]{0,1:T(1,128)S(1)}, u32[]{:S(2)}, u32[]{:S(2)}) %collective-permute-start.1) | collective-permute-done | bytes 1056 | tf_op jit(solution)/shard_map/ppermute | solution.py:50
  50.3 0.0 collective-permute-done.5
  50.4 0.4 divide_convert_fusion.1
  50.8 1.6 %collective-permute-start.9 = (f16[256,1024]{1,0:T(8,128)(2,1)S(1)}, f16[256,1024]{1,0:T(8,128)(2,1)S(1)}, u32[]{:S(2)}, u32[]{:S(2)}) collective-permute-start(f16[256,1024]{1,0:T(8,128)(2,1)S(1)} %divide_convert_fusion.1), channel_id=1, source_target_pairs={{0,1},{1,0},{2,3},{3,2},{4,5},{5,4},{6,7},{7,6},{8,9},{9,8},{10,11... | collective-permute-start | bytes 1572872 | tf_op jit(solution)/shard_map/ppermute | solution.py:50
  52.4 0.5 collective-permute-start.10
  52.9 12.5 %collective-permute-done.10 = f32[256,1]{0,1:T(1,128)S(1)} collective-permute-done((f32[256,1]{0,1:T(1,128)S(1)}, f32[256,1]{0,1:T(1,128)S(1)}, u32[]{:S(2)}, u32[]{:S(2)}) %collective-permute-start.10) | collective-permute-done | bytes 1056 | tf_op jit(solution)/shard_map/ppermute | solution.py:50
  65.4 0.6 log_add_fusion
  66.0 1.1 %divide_convert_fusion = bf16[256,1024]{1,0:T(8,128)(2,1)} fusion(f32[256]{0:T(256)S(1)} %bitcast.65, f32[256]{0:T(256)S(1)} %bitcast.66, f16[256,1024]{1,0:T(8,128)(2,1)S(1)} %collective-permute-done.9, f16[256,1024]{1,0:T(8,128)(2,1)S(1)} %divide_convert_fusion.1, f32[256]{0:T(256)S(1)} %bitcast.67, pred[]{:T(512)S(6)} %eq.3), kind=kLoop, calls=%fused_computation.33 | loop fusion | flops 2359296 | bytes 1575937 | tf_op jit(solution)/shard_map/convert_element_type | solution.py:68
  (15 shorter events, 0.1 us)
Async XLA Ops:
  0.6 19.1 %collective-permute-start.2 = (bf16[256,1024]{1,0:T(8,128)(2,1)}, bf16[256,1024]{1,0:T(8,128)(2,1)S(1)}, u32[]{:S(2)}, u32[]{:S(2)}) collective-permute-start(bf16[256,1024]{1,0:T(8,128)(2,1)} %param.3), channel_id=1, source_target_pairs={{0,4},{2,6},{4,8},{6,10},{8,12},{10,14},{12,16},{14,18},{16,20},{1... | collective-permute-start | bytes 1572872 | tf_op jit(solution)/shard_map/ppermute | solution.py:50
  3.7 10.6 %collective-permute-start = (bf16[256,1024]{1,0:T(8,128)(2,1)}, bf16[256,1024]{1,0:T(8,128)(2,1)S(1)}, u32[]{:S(2)}, u32[]{:S(2)}) collective-permute-start(bf16[256,1024]{1,0:T(8,128)(2,1)} %param.3), channel_id=1, source_target_pairs={{0,2},{2,8},{4,6},{6,12},{8,10},{10,16},{12,14},{14,20},{16,18},{1... | collective-permute-start | bytes 1572872 | tf_op jit(solution)/shard_map/ppermute | solution.py:50
  3.7 4.3 %copy-start.1 = (bf16[1,2048,1024]{2,1,0:T(8,128)(2,1)S(1)}, bf16[1,2048,1024]{2,1,0:T(8,128)(2,1)}, u32[]{:S(2)}) copy-start(bf16[1,2048,1024]{2,1,0:T(8,128)(2,1)} %param.5) | copy-start | bytes 12582916
  8.0 6.3 %copy-start = (bf16[1,2048,1024]{2,1,0:T(8,128)(2,1)S(1)}, bf16[1,2048,1024]{2,1,0:T(8,128)(2,1)}, u32[]{:S(2)}) copy-start(bf16[1,2048,1024]{2,1,0:T(8,128)(2,1)} %param.4) | copy-start | bytes 12582916
  17.5 32.9 %collective-permute-start.6 = (f16[256,1024]{1,0:T(8,128)(2,1)S(1)}, f16[256,1024]{1,0:T(8,128)(2,1)S(1)}, u32[]{:S(2)}, u32[]{:S(2)}) collective-permute-start(f16[256,1024]{1,0:T(8,128)(2,1)S(1)} %divide_convert_fusion.4), channel_id=1, source_target_pairs={{2,0},{8,2},{6,4},{12,6},{10,8},{16,10},{14,12},{20,14},{18,16},{2... | collective-permute-start | bytes 1572872 | tf_op jit(solution)/shard_map/ppermute | solution.py:50
  19.7 1.9 %collective-permute-start.3 = (bf16[256,1024]{1,0:T(8,128)(2,1)S(1)}, bf16[256,1024]{1,0:T(8,128)(2,1)S(1)}, u32[]{:S(2)}, u32[]{:S(2)}) collective-permute-start(bf16[256,1024]{1,0:T(8,128)(2,1)S(1)} %collective-permute-done.2), channel_id=1, source_target_pairs={{0,2},{2,0},{4,6},{6,4},{8,10},{10,8},{12,14},{14,12},{16,18},{18,... | collective-permute-start | bytes 1572872 | tf_op jit(solution)/shard_map/ppermute | solution.py:50
  24.8 2.1 %collective-permute-start.7 = (f16[256,1024]{1,0:T(8,128)(2,1)S(1)}, f16[256,1024]{1,0:T(8,128)(2,1)S(1)}, u32[]{:S(2)}, u32[]{:S(2)}) collective-permute-start(f16[256,1024]{1,0:T(8,128)(2,1)S(1)} %divide_convert_fusion.3), channel_id=1, source_target_pairs={{0,2},{2,0},{4,6},{6,4},{8,10},{10,8},{12,14},{14,12},{16,18},{18,... | collective-permute-start | bytes 1572872 | tf_op jit(solution)/shard_map/ppermute | solution.py:50
  25.3 1.5 %collective-permute-start.4 = (f32[256,1]{0,1:T(1,128)S(1)}, f32[256,1]{0,1:T(1,128)S(1)}, u32[]{:S(2)}, u32[]{:S(2)}) collective-permute-start(f32[256,1]{0,1:T(1,128)S(1)} %bitcast.71), channel_id=1, source_target_pairs={{0,2},{2,0},{4,6},{6,4},{8,10},{10,8},{12,14},{14,12},{16,18},{18,... | collective-permute-start | bytes 3080 | tf_op jit(solution)/shard_map/ppermute | solution.py:50
  28.4 22.0 %collective-permute-start.8 = (f16[256,1024]{1,0:T(8,128)(2,1)S(1)}, f16[256,1024]{1,0:T(8,128)(2,1)S(1)}, u32[]{:S(2)}, u32[]{:S(2)}) collective-permute-start(f16[256,1024]{1,0:T(8,128)(2,1)S(1)} %divide_convert_fusion.2), channel_id=1, source_target_pairs={{4,0},{6,2},{8,4},{10,6},{12,8},{14,10},{16,12},{18,14},{20,16},{2... | collective-permute-start | bytes 1572872 | tf_op jit(solution)/shard_map/ppermute | solution.py:50
  38.8 11.5 %collective-permute-start.1 = (f32[256,1]{0,1:T(1,128)S(1)}, f32[256,1]{0,1:T(1,128)S(1)}, u32[]{:S(2)}, u32[]{:S(2)}) collective-permute-start(f32[256,1]{0,1:T(1,128)S(1)} %bitcast.70), channel_id=1, source_target_pairs={{2,0},{8,2},{6,4},{12,6},{10,8},{16,10},{14,12},{20,14},{18,16},{2... | collective-permute-start | bytes 3080 | tf_op jit(solution)/shard_map/ppermute | solution.py:50
  38.8 11.5 %collective-permute-start.5 = (f32[256,1]{0,1:T(1,128)S(1)}, f32[256,1]{0,1:T(1,128)S(1)}, u32[]{:S(2)}, u32[]{:S(2)}) collective-permute-start(f32[256,1]{0,1:T(1,128)S(1)} %get-tuple-element.11), channel_id=1, source_target_pairs={{4,0},{6,2},{8,4},{10,6},{12,8},{14,10},{16,12},{18,14},{20,16},{2... | collective-permute-start | bytes 3080 | tf_op jit(solution)/shard_map/ppermute | solution.py:50
  50.8 15.1 %collective-permute-start.9 = (f16[256,1024]{1,0:T(8,128)(2,1)S(1)}, f16[256,1024]{1,0:T(8,128)(2,1)S(1)}, u32[]{:S(2)}, u32[]{:S(2)}) collective-permute-start(f16[256,1024]{1,0:T(8,128)(2,1)S(1)} %divide_convert_fusion.1), channel_id=1, source_target_pairs={{0,1},{1,0},{2,3},{3,2},{4,5},{5,4},{6,7},{7,6},{8,9},{9,8},{10,11... | collective-permute-start | bytes 1572872 | tf_op jit(solution)/shard_map/ppermute | solution.py:50
  52.4 13.0 %collective-permute-start.10 = (f32[256,1]{0,1:T(1,128)S(1)}, f32[256,1]{0,1:T(1,128)S(1)}, u32[]{:S(2)}, u32[]{:S(2)}) collective-permute-start(f32[256,1]{0,1:T(1,128)S(1)} %get-tuple-element.6), channel_id=1, source_target_pairs={{0,1},{1,0},{2,3},{3,2},{4,5},{5,4},{6,7},{7,6},{8,9},{9,8},{10,11... | collective-permute-start | bytes 3080 | tf_op jit(solution)/shard_map/ppermute | solution.py:50

commit v2 on v1

v2 whole, which is shorter than its diff:
```python
import jax
import jax.numpy as jnp
from jax import lax
from jax.sharding import PartitionSpec as P


sharpness = 2.5
SPLIT = (1, 1)


def after(value, *earlier):
    return lax.optimization_barrier((value, earlier))[0]


def plain_part(block_queries, keys, values):
    scores = (sharpness / block_queries.shape[1] ** 0.5) * jnp.dot(
        block_queries, keys.T, preferred_element_type=jnp.float32
    )
    top = jnp.max(scores, axis=1, keepdims=True)
    weights = jnp.exp(scores - top)
    total = jnp.sum(weights, axis=1, keepdims=True)
    weighted = jnp.dot(weights.astype(jnp.bfloat16), values, preferred_element_type=jnp.float32)
    return weighted / total, top + jnp.log(total)


def joined(all_parts):
    top = all_parts[0][1]
    for _, level in all_parts[1:]:
        top = jnp.maximum(top, level)
    total = 0.0
    mean = 0.0
    for value, level in all_parts:
        share = jnp.exp(level - top)
        total = total + share
        mean = mean + value.astype(jnp.float32) * share
    return mean / total, top + jnp.log(total)


def packed(part):
    return part[0].astype(jnp.float16), part[1]


def program(queries, corpus, attributions):
    n = lax.axis_size("blk")
    two = [(b, (b + 2) % n) for b in range(n)]
    two_back = [(d, s) for s, d in two]
    fourth = [(b, (b + (3 if b % 2 else 1)) % n) for b in range(n)]
    fourth_back = [(d, s) for s, d in fourth]
    pair = [(b, b ^ 1) for b in range(n)]
    first = lax.axis_index("rep") == 0

    def move(value, pairs, axis="blk"):
        return lax.ppermute(value, axis, pairs)

    def move_part(part, pairs, axis="blk"):
        mean, level = part
        return move(mean, pairs, axis), move(after(level, mean), pairs, axis)

    def edges(c):
        rows = queries.shape[0]
        return rows * sum(SPLIT[:c]) // sum(SPLIT), rows * sum(SPLIT[: c + 1]) // sum(SPLIT)

    def cut(tree, c):
        lo, hi = edges(c)
        return jax.tree.map(lambda a: a[lo:hi], tree)

    near_1 = move(cut(queries, 0), two)
    other = move(queries, fourth)
    near_2 = move(cut(queries, 1), two)
    keys, values = corpus[0], attributions[0]
    own = plain_part(queries, keys, values)

    def window(near):
        far = move(near, pair)
        both = plain_part(jnp.concatenate([near, far]), keys, values)
        near_part, far_part = (jax.tree.map(lambda a: a[at], both) for at in (slice(near.shape[0]), slice(near.shape[0], None)))
        far_back = move_part(packed(far_part), pair)
        mine = packed(joined([near_part, far_back]))
        return mine, move_part(mine, two_back)

    def exchange(all_parts):
        mine = packed(joined(all_parts))
        return mine, move_part(mine, [(0, 1), (1, 0)], "rep")

    def finish(outs, mine, theirs, c):
        a = jax.tree.map(lambda x, y: jnp.where(first, x, y), mine, theirs)
        b = jax.tree.map(lambda x, y: jnp.where(first, y, x), mine, theirs)
        attributed, log_total = joined([a, b])
        at = edges(c)[0]
        return (
            lax.dynamic_update_slice(outs[0], attributed.astype(jnp.bfloat16), (at, 0)),
            lax.dynamic_update_slice(outs[1], log_total[:, 0], (at,)),
        )

    mine_1, back_1 = window(after(near_1, own))
    other_part = plain_part(after(other, mine_1), keys, values)
    other_part = packed(other_part)
    other_back = move_part(other_part, fourth_back)
    mine_2, back_2 = window(after(near_2, other_part))
    own_1, theirs_1 = exchange([cut(own, 0), cut(other_back, 0), after(back_1, mine_2)])
    own_2, theirs_2 = exchange([cut(own, 1), cut(other_back, 1), after(back_2, own_1)])
    outs = (jnp.zeros(queries.shape, jnp.bfloat16), jnp.zeros(queries.shape[:1], jnp.float32))
    outs = finish(outs, own_1, after(theirs_1, own_2), 0)
    outs = finish(outs, own_2, theirs_2, 1)
    return outs


def solution(mesh):
    return jax.shard_map(
        program,
        mesh=mesh,
        in_specs=(P("blk", None), P("rep", "blk", None), P("rep", "blk", None)),
        out_specs=(P("blk", None), P("blk")),
        check_vma=False,
    )
```

time: 67.2 us -> 69.3 us (1.031)
  matrix products: 13.6 us -> 15.7 us
  waiting for transfers between devices: 32.2 us -> 30.8 us
  local copies, waits for them, and re-layouts: 0.01 us -> 1.09 us
    dot_general x8, matrix products: 13.6 us -> 15.7 us  [the longest x4 10.3 us: plain_part(): jnp.dot(block_queries, keys.T, preferred_element_type=jnp.float32)]
    ppermute x11 -> x19, waiting for transfers between devices: 32.2 us -> 30.8 us  [move(): return lax.ppermute(value, axis, pairs)]
    dynamic_update_slice x0 -> x2, other arithmetic: none -> 1.41 us  [the longest x1 0.83 us: finish(): lax.dynamic_update_slice(outs[0], attributed.astype(jnp.bfloat16), (at, 0))]
    slice x0 -> x3, local copies, waits for them, and re-layouts: none -> 1.07 us  [the longest x1 1.07 us: cut(): return jax.tree.map(lambda a: a[lo:hi], tree)]
    convert_element_type x1 -> x2, other arithmetic: 1.11 us -> 0.34 us  [finish(): attributed.astype(jnp.bfloat16)]
    ppermute x11 -> x19, starting transfers between devices: 16.5 us -> 16.1 us  [move(): return lax.ppermute(value, axis, pairs)]
  transfers between devices with their start and end apart: 11 -> 19, of which waited for: 5 -> 9; matrix products, arithmetic and copies ran while one was open for 24% -> 20% of each run, Pallas kernels for 0% -> 0%
where the time goes in v2:
time: 69.3 us; the launch traced here: 69.1 us
  waiting for transfers between devices  30.8 us (44%)
  starting transfers between devices  16.1 us (23%)
  matrix products  15.7 us (23%)
  other arithmetic  4.53 us (7%)
  local copies, waits for them, and re-layouts  1.09 us (2%)
  between operations  0.85 us (1%)
    ppermute x19, waiting for transfers between devices, move(): return lax.ppermute(value, axis, pairs)  30.8 us
    ppermute x19, starting transfers between devices, move(): return lax.ppermute(value, axis, pairs)  16.1 us
    dot_general x4, matrix products, plain_part(): jnp.dot(block_queries, keys.T, preferred_element_type=jnp.float32)  10.3 us
    dot_general x4, matrix products, plain_part(): jnp.dot(weights.astype(jnp.bfloat16), values, preferred_element_type=jnp....  5.42 us
    reduce_sum x4, other arithmetic, plain_part(): total = jnp.sum(weights, axis=1, keepdims=True)  1.75 us
  transfers between devices with their start and end apart: 19, of which 9 were waited for; matrix products, arithmetic and copies ran while one was open for 20% of the time, Pallas kernels for 0%

profile of v2, /device:TPU:0, one launch (start us, length us, event | category | flops | bytes accessed | tf_op | source)
XLA Modules:
  0.0 69.1 jit_solution(1877020493238504445)
XLA Ops:
  0.6 1.1 %fusion.97 = (bf16[128,1024]{1,0:T(8,128)(2,1)S(1)}, bf16[128,1024]{1,0:T(8,128)(2,1)S(1)}) fusion(bf16[256,1024]{1,0:T(8,128)(2,1)} %param.3), kind=kLoop, calls=%fused_computation.133 | loop fusion | bytes 1048576 | tf_op jit(solution)/shard_map/slice | solution.py:65
  1.7 3.0 %collective-permute-start.1 = (bf16[128,1024]{1,0:T(8,128)(2,1)S(1)}, bf16[128,1024]{1,0:T(8,128)(2,1)S(1)}, u32[]{:S(2)}, u32[]{:S(2)}) collective-permute-start(bf16[128,1024]{1,0:T(8,128)(2,1)S(1)} %get-tuple-element.47), channel_id=1, source_target_pairs={{0,4},{2,6},{4,8},{6,10},{8,12},{10,14},{12,16},{14,18},{16,20},{1... | collective-permute-start | bytes 786440 | tf_op jit(solution)/shard_map/ppermute | solution.py:53
  4.7 3.9 %fusion.98 = (f32[256]{0:T(256)S(1)}, f32[256,2048]{1,0:T(8,128)S(1)}) fusion(bf16[256,1024]{1,0:T(8,128)(2,1)} %param.3, bf16[1,2048,1024]{2,1,0:T(8,128)(2,1)} %param.4), kind=kOutput, calls=%fused_computation.134 | convolution fusion | flops 1074790144 | bytes 6816768 | tf_op jit(solution)/shard_map/dot_general | solution.py:16
  8.6 0.4 fusion.28
  9.1 1.4 %fusion.36 = f32[256,1024]{1,0:T(8,128)S(1)} fusion(bf16[1,2048,1024]{2,1,0:T(8,128)(2,1)S(1)} %copy-done.2, f32[256,2048]{1,0:T(8,128)S(1)} %get-tuple-element.69, f32[256]{0:T(256)S(1)} %get-tuple-element.68, f32[256]{0:T(256)S(1)} %fusion.28), kind=kOutput, calls=%fused_computation.32 | convolution fusion | flops 1075052544 | bytes 7342080 | tf_op jit(solution)/shard_map/dot_general | solution.py:22
  10.5 3.6 %collective-permute-done.1 = bf16[128,1024]{1,0:T(8,128)(2,1)S(1)} collective-permute-done((bf16[128,1024]{1,0:T(8,128)(2,1)S(1)}, bf16[128,1024]{1,0:T(8,128)(2,1)S(1)}, u32[]{:S(2)}, u32[]{:S(2)}) %collective-permute-start.1) | collective-permute-done | bytes 262176 | tf_op jit(solution)/shard_map/ppermute | solution.py:53
  14.1 0.5 collective-permute-start
  14.6 1.0 %collective-permute-done.2 = bf16[128,1024]{1,0:T(8,128)(2,1)S(1)} collective-permute-done((bf16[128,1024]{1,0:T(8,128)(2,1)S(1)}, bf16[128,1024]{1,0:T(8,128)(2,1)S(1)}, u32[]{:S(2)}, u32[]{:S(2)}) %collective-permute-start.2) | collective-permute-done | bytes 262176 | tf_op jit(solution)/shard_map/ppermute | solution.py:53
  15.6 1.4 %fusion.99 = (f32[256]{0:T(256)S(1)}, f32[256,2048]{1,0:T(8,128)S(1)}) fusion(bf16[1,2048,1024]{2,1,0:T(8,128)(2,1)S(1)} %copy-done.1, bf16[128,1024]{1,0:T(8,128)(2,1)S(1)} %collective-permute-done.2, bf16[128,1024]{1,0:T(8,128)(2,1)S(1)} %collective-permute-done.1), kind=kOutput, calls=%fused_computation.135 | convolution fusion | flops 1075838720 | bytes 6816768 | tf_op jit(solution)/shard_map/dot_general | solution.py:16
  17.0 0.4 fusion.30
  17.4 1.3 %broadcast_divide_fusion.1 = f32[256,1024]{1,0:T(8,128)S(1)} fusion(f32[256]{0:T(256)S(1)} %fusion.30, bf16[1,2048,1024]{2,1,0:T(8,128)(2,1)S(1)} %copy-done.2, f32[256,2048]{1,0:T(8,128)S(1)} %get-tuple-element.71, f32[256]{0:T(256)S(1)} %get-tuple-element.70), kind=kOutput, calls=%fused_computation.65 | convolution fusion | flops 1075052544 | bytes 7342080 | tf_op jit(solution)/shard_map/dot_general | solution.py:22
  19.4 1.0 %collective-permute-done.3 = f32[128,1]{0,1:T(1,128)S(1)} collective-permute-done((f32[128,1]{0,1:T(1,128)S(1)}, f32[128,1]{0,1:T(1,128)S(1)}, u32[]{:S(2)}, u32[]{:S(2)}) %collective-permute-start.3) | collective-permute-done | bytes 544 | tf_op jit(solution)/shard_map/ppermute | solution.py:53
  20.7 3.8 %collective-permute-done = bf16[256,1024]{1,0:T(8,128)(2,1)S(1)} collective-permute-done((bf16[256,1024]{1,0:T(8,128)(2,1)S(1)}, bf16[256,1024]{1,0:T(8,128)(2,1)S(1)}, u32[]{:S(2)}, u32[]{:S(2)}) %collective-permute-start) | collective-permute-done | bytes 524320 | tf_op jit(solution)/shard_map/ppermute | solution.py:53
  24.5 1.4 %fusion.100 = (f32[256]{0:T(256)S(1)}, f32[256,2048]{1,0:T(8,128)S(1)}) fusion(bf16[256,1024]{1,0:T(8,128)(2,1)S(1)} %collective-permute-done, bf16[1,2048,1024]{2,1,0:T(8,128)(2,1)S(1)} %copy-done.1), kind=kOutput, calls=%fused_computation.136 | convolution fusion | flops 1074790144 | bytes 6816768 | tf_op jit(solution)/shard_map/dot_general | solution.py:16
  25.9 0.4 fusion.33
  26.3 1.4 %fusion.42 = f16[256,1024]{1,0:T(8,128)(2,1)S(1)} fusion(bf16[1,2048,1024]{2,1,0:T(8,128)(2,1)S(1)} %copy-done.2, f32[256,2048]{1,0:T(8,128)S(1)} %get-tuple-element.73, f32[256]{0:T(256)S(1)} %get-tuple-element.72, f32[256]{0:T(256)S(1)} %fusion.33), kind=kOutput, calls=%fused_computation.34 | convolution fusion | flops 1075314688 | bytes 6817792 | tf_op jit(solution)/shard_map/dot_general | solution.py:22
  27.7 2.7 %collective-permute-done.8 = bf16[128,1024]{1,0:T(8,128)(2,1)S(1)} collective-permute-done((bf16[128,1024]{1,0:T(8,128)(2,1)S(1)}, bf16[128,1024]{1,0:T(8,128)(2,1)S(1)}, u32[]{:S(2)}, u32[]{:S(2)}) %collective-permute-start.8) | collective-permute-done | bytes 262176 | tf_op jit(solution)/shard_map/ppermute | solution.py:53
  30.5 1.5 %collective-permute-done.9 = bf16[128,1024]{1,0:T(8,128)(2,1)S(1)} collective-permute-done((bf16[128,1024]{1,0:T(8,128)(2,1)S(1)}, bf16[128,1024]{1,0:T(8,128)(2,1)S(1)}, u32[]{:S(2)}, u32[]{:S(2)}) %collective-permute-start.9) | collective-permute-done | bytes 262176 | tf_op jit(solution)/shard_map/ppermute | solution.py:53
  32.0 3.7 %fusion.101 = (f32[256]{0:T(256)S(1)}, f32[256,2048]{1,0:T(8,128)S(1)}) fusion(bf16[1,2048,1024]{2,1,0:T(8,128)(2,1)} %param.4, bf16[128,1024]{1,0:T(8,128)(2,1)S(1)} %collective-permute-done.9, bf16[128,1024]{1,0:T(8,128)(2,1)S(1)} %collective-permute-done.8), kind=kOutput, calls=%fused_computation.137 | convolution fusion | flops 1075838720 | bytes 6816768 | tf_op jit(solution)/shard_map/dot_general | solution.py:16
  35.7 0.4 fusion.34
  36.2 1.3 %broadcast_divide_fusion = f32[256,1024]{1,0:T(8,128)S(1)} fusion(f32[256]{0:T(256)S(1)} %fusion.34, bf16[1,2048,1024]{2,1,0:T(8,128)(2,1)S(1)} %copy-done.3, f32[256,2048]{1,0:T(8,128)S(1)} %get-tuple-element.75, f32[256]{0:T(256)S(1)} %get-tuple-element.74), kind=kOutput, calls=%fused_computation.64 | convolution fusion | flops 1075052544 | bytes 7342080 | tf_op jit(solution)/shard_map/dot_general | solution.py:22
  38.3 1.7 %collective-permute-start.7 = (f32[128,1]{0,1:T(1,128)S(1)}, f32[128,1]{0,1:T(1,128)S(1)}, u32[]{:S(2)}, u32[]{:S(2)}) collective-permute-start(f32[128,1]{0,1:T(1,128)S(1)} %get-tuple-element.22), channel_id=1, source_target_pairs={{4,0},{6,2},{8,4},{10,6},{12,8},{14,10},{16,12},{18,14},{20,16},{2... | collective-permute-start | bytes 1544 | tf_op jit(solution)/shard_map/ppermute | solution.py:53
  40.4 12.3 %collective-permute-done.7 = f32[128,1]{0,1:T(1,128)S(1)} collective-permute-done((f32[128,1]{0,1:T(1,128)S(1)}, f32[128,1]{0,1:T(1,128)S(1)}, u32[]{:S(2)}, u32[]{:S(2)}) %collective-permute-start.7) | collective-permute-done | bytes 544 | tf_op jit(solution)/shard_map/ppermute | solution.py:53
  52.7 5.1 %collective-permute-start.16 = (f32[128,1]{0,1:T(1,128)S(1)}, f32[128,1]{0,1:T(1,128)S(1)}, u32[]{:S(2)}, u32[]{:S(2)}) collective-permute-start(f32[128,1]{0,1:T(1,128)S(1)} %get-tuple-element.28), channel_id=1, source_target_pairs={{4,0},{6,2},{8,4},{10,6},{12,8},{14,10},{16,12},{18,14},{20,16},{2... | collective-permute-start | bytes 1544 | tf_op jit(solution)/shard_map/ppermute | solution.py:53
  58.2 1.6 %collective-permute-start.13 = (f16[128,1024]{1,0:T(8,128)(2,1)S(1)}, f16[128,1024]{1,0:T(8,128)(2,1)S(1)}, u32[]{:S(2)}, u32[]{:S(2)}) collective-permute-start(f16[128,1024]{1,0:T(8,128)(2,1)S(1)} %fusion.71), channel_id=1, source_target_pairs={{0,1},{1,0},{2,3},{3,2},{4,5},{5,4},{6,7},{7,6},{8,9},{9,8},{10,11... | collective-permute-start | bytes 786440 | tf_op jit(solution)/shard_map/ppermute | solution.py:53
  59.7 0.5 collective-permute-start.14
  60.5 1.6 %collective-permute-start.17 = (f16[128,1024]{1,0:T(8,128)(2,1)S(1)}, f16[128,1024]{1,0:T(8,128)(2,1)S(1)}, u32[]{:S(2)}, u32[]{:S(2)}) collective-permute-start(f16[128,1024]{1,0:T(8,128)(2,1)S(1)} %fusion.72), channel_id=1, source_target_pairs={{0,1},{1,0},{2,3},{3,2},{4,5},{5,4},{6,7},{7,6},{8,9},{9,8},{10,11... | collective-permute-start | bytes 786440 | tf_op jit(solution)/shard_map/ppermute | solution.py:53
  62.1 0.5 collective-permute-start.18
  62.6 2.1 %collective-permute-done.14 = f32[128,1]{0,1:T(1,128)S(1)} collective-permute-done((f32[128,1]{0,1:T(1,128)S(1)}, f32[128,1]{0,1:T(1,128)S(1)}, u32[]{:S(2)}, u32[]{:S(2)}) %collective-permute-start.14) | collective-permute-done | bytes 544 | tf_op jit(solution)/shard_map/ppermute | solution.py:53
  64.9 2.6 %collective-permute-done.18 = f32[128,1]{0,1:T(1,128)S(1)} collective-permute-done((f32[128,1]{0,1:T(1,128)S(1)}, f32[128,1]{0,1:T(1,128)S(1)}, u32[]{:S(2)}, u32[]{:S(2)}) %collective-permute-start.18) | collective-permute-done | bytes 544 | tf_op jit(solution)/shard_map/ppermute | solution.py:53
  67.5 0.6 pad_maximum_fusion.1
  68.3 0.8 %pad_maximum_fusion = bf16[256,1024]{1,0:T(8,128)(2,1)} fusion(bf16[128,1024]{1,0:T(8,128)(2,1)S(1)} %divide_convert_fusion, bf16[128,1024]{1,0:T(8,128)(2,1)S(1)} %divide_convert_fusion.1), kind=kLoop, calls=%fused_computation.61 | loop fusion | flops 1048576 | bytes 1048576 | tf_op jit(solution)/shard_map/dynamic_update_slice | solution.py:91
  (53 shorter events, 2.9 us)
Async XLA Ops:
  1.7 12.4 %collective-permute-start.1 = (bf16[128,1024]{1,0:T(8,128)(2,1)S(1)}, bf16[128,1024]{1,0:T(8,128)(2,1)S(1)}, u32[]{:S(2)}, u32[]{:S(2)}) collective-permute-start(bf16[128,1024]{1,0:T(8,128)(2,1)S(1)} %get-tuple-element.47), channel_id=1, source_target_pairs={{0,4},{2,6},{4,8},{6,10},{8,12},{10,14},{12,16},{14,18},{16,20},{1... | collective-permute-start | bytes 786440 | tf_op jit(solution)/shard_map/ppermute | solution.py:53
  4.7 4.3 %copy-start.2 = (bf16[1,2048,1024]{2,1,0:T(8,128)(2,1)S(1)}, bf16[1,2048,1024]{2,1,0:T(8,128)(2,1)}, u32[]{:S(2)}) copy-start(bf16[1,2048,1024]{2,1,0:T(8,128)(2,1)} %param.5) | copy-start | bytes 12582916
  9.1 5.0 %copy-start = (bf16[256,1024]{1,0:T(8,128)(2,1)S(1)}, bf16[256,1024]{1,0:T(8,128)(2,1)}, u32[]{:S(2)}) copy-start(bf16[256,1024]{1,0:T(8,128)(2,1)} %param.3) | copy-start | bytes 1572868
  9.1 6.6 %copy-start.1 = (bf16[1,2048,1024]{2,1,0:T(8,128)(2,1)S(1)}, bf16[1,2048,1024]{2,1,0:T(8,128)(2,1)}, u32[]{:S(2)}) copy-start(bf16[1,2048,1024]{2,1,0:T(8,128)(2,1)} %param.4) | copy-start | bytes 12582916
  14.1 1.5 %collective-permute-start.2 = (bf16[128,1024]{1,0:T(8,128)(2,1)S(1)}, bf16[128,1024]{1,0:T(8,128)(2,1)S(1)}, u32[]{:S(2)}, u32[]{:S(2)}) collective-permute-start(bf16[128,1024]{1,0:T(8,128)(2,1)S(1)} %collective-permute-done.1), channel_id=1, source_target_pairs={{0,2},{2,0},{4,6},{6,4},{8,10},{10,8},{12,14},{14,12},{16,18},{18,... | collective-permute-start | bytes 786440 | tf_op jit(solution)/shard_map/ppermute | solution.py:53
  14.1 10.4 %collective-permute-start = (bf16[256,1024]{1,0:T(8,128)(2,1)S(1)}, bf16[256,1024]{1,0:T(8,128)(2,1)S(1)}, u32[]{:S(2)}, u32[]{:S(2)}) collective-permute-start(bf16[256,1024]{1,0:T(8,128)(2,1)S(1)} %copy-done), channel_id=1, source_target_pairs={{0,2},{2,8},{4,6},{6,12},{8,10},{10,16},{12,14},{14,20},{16,18},{1... | collective-permute-start | bytes 1572872 | tf_op jit(solution)/shard_map/ppermute | solution.py:53
  18.8 1.6 %collective-permute-start.4 = (f16[128,1024]{1,0:T(8,128)(2,1)S(1)}, f16[128,1024]{1,0:T(8,128)(2,1)S(1)}, u32[]{:S(2)}, u32[]{:S(2)}) collective-permute-start(f16[128,1024]{1,0:T(8,128)(2,1)S(1)} %slice_convert_fusion.1), channel_id=1, source_target_pairs={{0,2},{2,0},{4,6},{6,4},{8,10},{10,8},{12,14},{14,12},{16,18},{18,... | collective-permute-start | bytes 786440 | tf_op jit(solution)/shard_map/ppermute | solution.py:53
  19.0 1.4 %collective-permute-start.3 = (f32[128,1]{0,1:T(1,128)S(1)}, f32[128,1]{0,1:T(1,128)S(1)}, u32[]{:S(2)}, u32[]{:S(2)}) collective-permute-start(f32[128,1]{0,1:T(1,128)S(1)} %slice_bitcast_fusion.1), channel_id=1, source_target_pairs={{0,2},{2,0},{4,6},{6,4},{8,10},{10,8},{12,14},{14,12},{16,18},{18,... | collective-permute-start | bytes 1544 | tf_op jit(solution)/shard_map/ppermute | solution.py:53
  19.4 11.0 %collective-permute-start.8 = (bf16[128,1024]{1,0:T(8,128)(2,1)S(1)}, bf16[128,1024]{1,0:T(8,128)(2,1)S(1)}, u32[]{:S(2)}, u32[]{:S(2)}) collective-permute-start(bf16[128,1024]{1,0:T(8,128)(2,1)S(1)} %get-tuple-element.48), channel_id=1, source_target_pairs={{0,4},{2,6},{4,8},{6,10},{8,12},{10,14},{12,16},{14,18},{16,20},{1... | collective-permute-start | bytes 786440 | tf_op jit(solution)/shard_map/ppermute | solution.py:53
  30.5 1.5 %collective-permute-start.9 = (bf16[128,1024]{1,0:T(8,128)(2,1)S(1)}, bf16[128,1024]{1,0:T(8,128)(2,1)S(1)}, u32[]{:S(2)}, u32[]{:S(2)}) collective-permute-start(bf16[128,1024]{1,0:T(8,128)(2,1)S(1)} %collective-permute-done.8), channel_id=1, source_target_pairs={{0,2},{2,0},{4,6},{6,4},{8,10},{10,8},{12,14},{14,12},{16,18},{18,... | collective-permute-start | bytes 786440 | tf_op jit(solution)/shard_map/ppermute | solution.py:53
  32.0 4.2 %copy-start.3 = (bf16[1,2048,1024]{2,1,0:T(8,128)(2,1)S(1)}, bf16[1,2048,1024]{2,1,0:T(8,128)(2,1)}, u32[]{:S(2)}) copy-start(bf16[1,2048,1024]{2,1,0:T(8,128)(2,1)} %param.5) | copy-start | bytes 12582916
  37.5 2.5 %collective-permute-start.11 = (f16[128,1024]{1,0:T(8,128)(2,1)S(1)}, f16[128,1024]{1,0:T(8,128)(2,1)S(1)}, u32[]{:S(2)}, u32[]{:S(2)}) collective-permute-start(f16[128,1024]{1,0:T(8,128)(2,1)S(1)} %slice_convert_fusion), channel_id=1, source_target_pairs={{0,2},{2,0},{4,6},{6,4},{8,10},{10,8},{12,14},{14,12},{16,18},{18,... | collective-permute-start | bytes 786440 | tf_op jit(solution)/shard_map/ppermute | solution.py:53
  37.7 2.3 %collective-permute-start.10 = (f32[128,1]{0,1:T(1,128)S(1)}, f32[128,1]{0,1:T(1,128)S(1)}, u32[]{:S(2)}, u32[]{:S(2)}) collective-permute-start(f32[128,1]{0,1:T(1,128)S(1)} %slice_bitcast_fusion), channel_id=1, source_target_pairs={{0,2},{2,0},{4,6},{6,4},{8,10},{10,8},{12,14},{14,12},{16,18},{18,... | collective-permute-start | bytes 1544 | tf_op jit(solution)/shard_map/ppermute | solution.py:53
  38.1 19.8 %collective-permute-start.6 = (f16[128,1024]{1,0:T(8,128)(2,1)S(1)}, f16[128,1024]{1,0:T(8,128)(2,1)S(1)}, u32[]{:S(2)}, u32[]{:S(2)}) collective-permute-start(f16[128,1024]{1,0:T(8,128)(2,1)S(1)} %fusion.69), channel_id=1, source_target_pairs={{4,0},{6,2},{8,4},{10,6},{12,8},{14,10},{16,12},{18,14},{20,16},{2... | collective-permute-start | bytes 786440 | tf_op jit(solution)/shard_map/ppermute | solution.py:53
  38.1 19.8 %collective-permute-start.12 = (f16[256,1024]{1,0:T(8,128)(2,1)S(1)}, f16[256,1024]{1,0:T(8,128)(2,1)S(1)}, u32[]{:S(2)}, u32[]{:S(2)}) collective-permute-start(f16[256,1024]{1,0:T(8,128)(2,1)S(1)} %fusion.42), channel_id=1, source_target_pairs={{2,0},{8,2},{6,4},{12,6},{10,8},{16,10},{14,12},{20,14},{18,16},{2... | collective-permute-start | bytes 1572872 | tf_op jit(solution)/shard_map/ppermute | solution.py:53
  38.3 14.4 %collective-permute-start.7 = (f32[128,1]{0,1:T(1,128)S(1)}, f32[128,1]{0,1:T(1,128)S(1)}, u32[]{:S(2)}, u32[]{:S(2)}) collective-permute-start(f32[128,1]{0,1:T(1,128)S(1)} %get-tuple-element.22), channel_id=1, source_target_pairs={{4,0},{6,2},{8,4},{10,6},{12,8},{14,10},{16,12},{18,14},{20,16},{2... | collective-permute-start | bytes 1544 | tf_op jit(solution)/shard_map/ppermute | solution.py:53
  40.1 17.8 %collective-permute-start.5 = (f32[256,1]{0,1:T(1,128)S(1)}, f32[256,1]{0,1:T(1,128)S(1)}, u32[]{:S(2)}, u32[]{:S(2)}) collective-permute-start(f32[256,1]{0,1:T(1,128)S(1)} %bitcast.159), channel_id=1, source_target_pairs={{2,0},{8,2},{6,4},{12,6},{10,8},{16,10},{14,12},{20,14},{18,16},{2... | collective-permute-start | bytes 3080 | tf_op jit(solution)/shard_map/ppermute | solution.py:53
  40.3 20.0 %collective-permute-start.15 = (f16[128,1024]{1,0:T(8,128)(2,1)S(1)}, f16[128,1024]{1,0:T(8,128)(2,1)S(1)}, u32[]{:S(2)}, u32[]{:S(2)}) collective-permute-start(f16[128,1024]{1,0:T(8,128)(2,1)S(1)} %fusion.70), channel_id=1, source_target_pairs={{4,0},{6,2},{8,4},{10,6},{12,8},{14,10},{16,12},{18,14},{20,16},{2... | collective-permute-start | bytes 786440 | tf_op jit(solution)/shard_map/ppermute | solution.py:53
  52.7 7.5 %collective-permute-start.16 = (f32[128,1]{0,1:T(1,128)S(1)}, f32[128,1]{0,1:T(1,128)S(1)}, u32[]{:S(2)}, u32[]{:S(2)}) collective-permute-start(f32[128,1]{0,1:T(1,128)S(1)} %get-tuple-element.28), channel_id=1, source_target_pairs={{4,0},{6,2},{8,4},{10,6},{12,8},{14,10},{16,12},{18,14},{20,16},{2... | collective-permute-start | bytes 1544 | tf_op jit(solution)/shard_map/ppermute | solution.py:53
  58.2 6.5 %collective-permute-start.13 = (f16[128,1024]{1,0:T(8,128)(2,1)S(1)}, f16[128,1024]{1,0:T(8,128)(2,1)S(1)}, u32[]{:S(2)}, u32[]{:S(2)}) collective-permute-start(f16[128,1024]{1,0:T(8,128)(2,1)S(1)} %fusion.71), channel_id=1, source_target_pairs={{0,1},{1,0},{2,3},{3,2},{4,5},{5,4},{6,7},{7,6},{8,9},{9,8},{10,11... | collective-permute-start | bytes 786440 | tf_op jit(solution)/shard_map/ppermute | solution.py:53
  59.7 5.0 %collective-permute-start.14 = (f32[128,1]{0,1:T(1,128)S(1)}, f32[128,1]{0,1:T(1,128)S(1)}, u32[]{:S(2)}, u32[]{:S(2)}) collective-permute-start(f32[128,1]{0,1:T(1,128)S(1)} %get-tuple-element.27), channel_id=1, source_target_pairs={{0,1},{1,0},{2,3},{3,2},{4,5},{5,4},{6,7},{7,6},{8,9},{9,8},{10,11... | collective-permute-start | bytes 1544 | tf_op jit(solution)/shard_map/ppermute | solution.py:53
  60.5 7.6 %collective-permute-start.17 = (f16[128,1024]{1,0:T(8,128)(2,1)S(1)}, f16[128,1024]{1,0:T(8,128)(2,1)S(1)}, u32[]{:S(2)}, u32[]{:S(2)}) collective-permute-start(f16[128,1024]{1,0:T(8,128)(2,1)S(1)} %fusion.72), channel_id=1, source_target_pairs={{0,1},{1,0},{2,3},{3,2},{4,5},{5,4},{6,7},{7,6},{8,9},{9,8},{10,11... | collective-permute-start | bytes 786440 | tf_op jit(solution)/shard_map/ppermute | solution.py:53
  62.1 5.4 %collective-permute-start.18 = (f32[128,1]{0,1:T(1,128)S(1)}, f32[128,1]{0,1:T(1,128)S(1)}, u32[]{:S(2)}, u32[]{:S(2)}) collective-permute-start(f32[128,1]{0,1:T(1,128)S(1)} %get-tuple-element.33), channel_id=1, source_target_pairs={{0,1},{1,0},{2,3},{3,2},{4,5},{5,4},{6,7},{7,6},{8,9},{9,8},{10,11... | collective-permute-start | bytes 1544 | tf_op jit(solution)/shard_map/ppermute | solution.py:53

commit v3 on v2

--- a/solution.py
+++ b/solution.py
@@ -47,14 +47,14 @@
     fourth = [(b, (b + (3 if b % 2 else 1)) % n) for b in range(n)]
     fourth_back = [(d, s) for s, d in fourth]
     pair = [(b, b ^ 1) for b in range(n)]
-    first = lax.axis_index("rep") == 0
 
     def move(value, pairs, axis="blk"):
         return lax.ppermute(value, axis, pairs)
 
     def move_part(part, pairs, axis="blk"):
         mean, level = part
-        return move(mean, pairs, axis), move(after(level, mean), pairs, axis)
+        mean_there = move(mean, pairs, axis)
+        return mean_there, move(after(level[:, 0], mean), pairs, axis)[:, None]
 
     def edges(c):
         rows = queries.shape[0]
@@ -83,9 +83,7 @@
         return mine, move_part(mine, [(0, 1), (1, 0)], "rep")
 
     def finish(outs, mine, theirs, c):
-        a = jax.tree.map(lambda x, y: jnp.where(first, x, y), mine, theirs)
-        b = jax.tree.map(lambda x, y: jnp.where(first, y, x), mine, theirs)
-        attributed, log_total = joined([a, b])
+        attributed, log_total = joined([mine, theirs])
         at = edges(c)[0]
         return (
             lax.dynamic_update_slice(outs[0], attributed.astype(jnp.bfloat16), (at, 0)),
@@ -99,7 +97,7 @@
     mine_2, back_2 = window(after(near_2, other_part))
     own_1, theirs_1 = exchange([cut(own, 0), cut(other_back, 0), after(back_1, mine_2)])
     own_2, theirs_2 = exchange([cut(own, 1), cut(other_back, 1), after(back_2, own_1)])
-    outs = (jnp.zeros(queries.shape, jnp.bfloat16), jnp.zeros(queries.shape[:1], jnp.float32))
+    outs = (queries, own[1][:, 0])
     outs = finish(outs, own_1, after(theirs_1, own_2), 0)
     outs = finish(outs, own_2, theirs_2, 1)
     return outs

time: 69.3 us -> 64.2 us (0.926)
  waiting for transfers between devices: 30.8 us -> 27.8 us
  matrix products: 15.7 us -> 13.3 us
  other arithmetic: 4.53 us -> 3.18 us
  local copies, waits for them, and re-layouts: 1.09 us -> 2.24 us
    ppermute x19, waiting for transfers between devices: 30.8 us -> 27.8 us  [move(): return lax.ppermute(value, axis, pairs)]
    dot_general x4, matrix products: 10.3 us -> 7.83 us  [plain_part(): jnp.dot(block_queries, keys.T, preferred_element_type=jnp.float32)]
    unnamed x8 -> x9, local copies, waits for them, and re-layouts: 0.02 us -> 2.19 us
    slice x1, local copies, waits for them, and re-layouts: 1.07 us -> 0.03 us  [cut(): return jax.tree.map(lambda a: a[lo:hi], tree)]
  transfers between devices with their start and end apart: 19 -> 19, of which waited for: 9 -> 10; matrix products, arithmetic and copies ran while one was open for 20% -> 26% of each run, Pallas kernels for 0% -> 0%
where the time goes in v3:
time: 64.2 us; the launch traced here: 64 us
  waiting for transfers between devices  27.8 us (43%)
  starting transfers between devices  16.6 us (26%)
  matrix products  13.3 us (21%)
  other arithmetic  3.18 us (5%)
  local copies, waits for them, and re-layouts  2.24 us (3%)
  between operations  0.84 us (1%)
    ppermute x19, waiting for transfers between devices, move(): return lax.ppermute(value, axis, pairs)  27.8 us
    ppermute x19, starting transfers between devices, move(): return lax.ppermute(value, axis, pairs)  16.6 us
    dot_general x4, matrix products, plain_part(): jnp.dot(block_queries, keys.T, preferred_element_type=jnp.float32)  7.83 us
    dot_general x4, matrix products, plain_part(): jnp.dot(weights.astype(jnp.bfloat16), values, preferred_element_type=jnp....  5.51 us
    unnamed x9, local copies, waits for them, and re-layouts  2.19 us
    reduce_sum x4, other arithmetic, plain_part(): total = jnp.sum(weights, axis=1, keepdims=True)  1.75 us
  transfers between devices with their start and end apart: 19, of which 10 were waited for; matrix products, arithmetic and copies ran while one was open for 26% of the time, Pallas kernels for 0%

profile of v3, /device:TPU:0, one launch (start us, length us, event | category | flops | bytes accessed | tf_op | source)
XLA Modules:
  0.0 64.0 jit_solution(742312832427068243)
XLA Ops:
  0.6 1.0 %copy.10 = bf16[256,1024]{1,0:T(8,128)(2,1)S(1)} copy(bf16[256,1024]{1,0:T(8,128)(2,1)} %param.3) | data formatting | bytes 1048576
  1.7 3.0 %collective-permute-start.1 = (bf16[128,1024]{1,0:T(8,128)(2,1)S(1)}, bf16[128,1024]{1,0:T(8,128)(2,1)S(1)}, u32[]{:S(2)}, u32[]{:S(2)}) collective-permute-start(bf16[128,1024]{1,0:T(8,128)(2,1)S(1)} %get-tuple-element.41), channel_id=1, source_target_pairs={{0,4},{2,6},{4,8},{6,10},{8,12},{10,14},{12,16},{14,18},{16,20},{1... | collective-permute-start | bytes 786440 | tf_op jit(solution)/shard_map/ppermute | solution.py:52
  4.8 3.7 %fusion.105 = (f32[256]{0:T(256)S(1)}, f32[256,2048]{1,0:T(8,128)S(1)}) fusion(bf16[256,1024]{1,0:T(8,128)(2,1)S(1)} %copy.10, bf16[1,2048,1024]{2,1,0:T(8,128)(2,1)} %param.4), kind=kOutput, calls=%fused_computation.134 | convolution fusion | flops 1074790144 | bytes 6816768 | tf_op jit(solution)/shard_map/dot_general | solution.py:16
  8.5 0.4 fusion.28
  8.9 1.4 %fusion.36 = f32[256,1024]{1,0:T(8,128)S(1)} fusion(bf16[1,2048,1024]{2,1,0:T(8,128)(2,1)S(1)} %copy-done.3, f32[256,2048]{1,0:T(8,128)S(1)} %get-tuple-element.63, f32[256]{0:T(256)S(1)} %get-tuple-element.62, f32[256]{0:T(256)S(1)} %fusion.28), kind=kOutput, calls=%fused_computation.32 | convolution fusion | flops 1075052544 | bytes 7342080 | tf_op jit(solution)/shard_map/dot_general | solution.py:22
  10.3 3.8 %collective-permute-done.1 = bf16[128,1024]{1,0:T(8,128)(2,1)S(1)} collective-permute-done((bf16[128,1024]{1,0:T(8,128)(2,1)S(1)}, bf16[128,1024]{1,0:T(8,128)(2,1)S(1)}, u32[]{:S(2)}, u32[]{:S(2)}) %collective-permute-start.1) | collective-permute-done | bytes 262176 | tf_op jit(solution)/shard_map/ppermute | solution.py:52
  14.1 0.5 collective-permute-start
  14.6 1.0 %collective-permute-done.2 = bf16[128,1024]{1,0:T(8,128)(2,1)S(1)} collective-permute-done((bf16[128,1024]{1,0:T(8,128)(2,1)S(1)}, bf16[128,1024]{1,0:T(8,128)(2,1)S(1)}, u32[]{:S(2)}, u32[]{:S(2)}) %collective-permute-start.2) | collective-permute-done | bytes 262176 | tf_op jit(solution)/shard_map/ppermute | solution.py:52
  15.6 1.4 %fusion.106 = (f32[256]{0:T(256)S(1)}, f32[256,2048]{1,0:T(8,128)S(1)}) fusion(bf16[1,2048,1024]{2,1,0:T(8,128)(2,1)S(1)} %copy-done.2, bf16[128,1024]{1,0:T(8,128)(2,1)S(1)} %collective-permute-done.2, bf16[128,1024]{1,0:T(8,128)(2,1)S(1)} %collective-permute-done.1), kind=kOutput, calls=%fused_computation.135 | convolution fusion | flops 1075838720 | bytes 6816768 | tf_op jit(solution)/shard_map/dot_general | solution.py:16
  17.0 0.4 fusion.30
  17.5 1.4 %broadcast_divide_fusion.1 = f32[256,1024]{1,0:T(8,128)S(1)} fusion(f32[256]{0:T(256)S(1)} %fusion.30, bf16[1,2048,1024]{2,1,0:T(8,128)(2,1)S(1)} %copy-done.3, f32[256,2048]{1,0:T(8,128)S(1)} %get-tuple-element.65, f32[256]{0:T(256)S(1)} %get-tuple-element.64), kind=kOutput, calls=%fused_computation.64 | convolution fusion | flops 1075052544 | bytes 7342080 | tf_op jit(solution)/shard_map/dot_general | solution.py:22
  19.5 1.0 %collective-permute-done.3 = f32[128]{0:T(128)S(1)} collective-permute-done((f32[128]{0:T(128)S(1)}, f32[128]{0:T(128)S(1)}, u32[]{:S(2)}, u32[]{:S(2)}) %collective-permute-start.3) | collective-permute-done | bytes 544 | tf_op jit(solution)/shard_map/ppermute | solution.py:52
  20.7 3.8 %collective-permute-done = bf16[256,1024]{1,0:T(8,128)(2,1)S(1)} collective-permute-done((bf16[256,1024]{1,0:T(8,128)(2,1)S(1)}, bf16[256,1024]{1,0:T(8,128)(2,1)S(1)}, u32[]{:S(2)}, u32[]{:S(2)}) %collective-permute-start) | collective-permute-done | bytes 524320 | tf_op jit(solution)/shard_map/ppermute | solution.py:52
  24.5 1.4 %fusion.107 = (f32[256]{0:T(256)S(1)}, f32[256,2048]{1,0:T(8,128)S(1)}) fusion(bf16[256,1024]{1,0:T(8,128)(2,1)S(1)} %collective-permute-done, bf16[1,2048,1024]{2,1,0:T(8,128)(2,1)S(1)} %copy-done.2), kind=kOutput, calls=%fused_computation.136 | convolution fusion | flops 1074790144 | bytes 6816768 | tf_op jit(solution)/shard_map/dot_general | solution.py:16
  25.9 0.4 fusion.33
  26.3 1.4 %fusion.42 = f16[256,1024]{1,0:T(8,128)(2,1)S(1)} fusion(bf16[1,2048,1024]{2,1,0:T(8,128)(2,1)S(1)} %copy-done.3, f32[256,2048]{1,0:T(8,128)S(1)} %get-tuple-element.67, f32[256]{0:T(256)S(1)} %get-tuple-element.66, f32[256]{0:T(256)S(1)} %fusion.33), kind=kOutput, calls=%fused_computation.34 | convolution fusion | flops 1075314688 | bytes 6817792 | tf_op jit(solution)/shard_map/dot_general | solution.py:22
  27.7 2.8 %collective-permute-done.8 = bf16[128,1024]{1,0:T(8,128)(2,1)S(1)} collective-permute-done((bf16[128,1024]{1,0:T(8,128)(2,1)S(1)}, bf16[128,1024]{1,0:T(8,128)(2,1)S(1)}, u32[]{:S(2)}, u32[]{:S(2)}) %collective-permute-start.8) | collective-permute-done | bytes 262176 | tf_op jit(solution)/shard_map/ppermute | solution.py:52
  30.6 1.5 %collective-permute-done.9 = bf16[128,1024]{1,0:T(8,128)(2,1)S(1)} collective-permute-done((bf16[128,1024]{1,0:T(8,128)(2,1)S(1)}, bf16[128,1024]{1,0:T(8,128)(2,1)S(1)}, u32[]{:S(2)}, u32[]{:S(2)}) %collective-permute-start.9) | collective-permute-done | bytes 262176 | tf_op jit(solution)/shard_map/ppermute | solution.py:52
  32.1 1.4 %fusion.108 = (f32[256]{0:T(256)S(1)}, f32[256,2048]{1,0:T(8,128)S(1)}) fusion(bf16[1,2048,1024]{2,1,0:T(8,128)(2,1)S(1)} %copy-done.2, bf16[128,1024]{1,0:T(8,128)(2,1)S(1)} %collective-permute-done.9, bf16[128,1024]{1,0:T(8,128)(2,1)S(1)} %collective-permute-done.8), kind=kOutput, calls=%fused_computation.137 | convolution fusion | flops 1075838720 | bytes 6816768 | tf_op jit(solution)/shard_map/dot_general | solution.py:16
  33.5 0.4 fusion.34
  33.9 1.4 %broadcast_divide_fusion = f32[256,1024]{1,0:T(8,128)S(1)} fusion(f32[256]{0:T(256)S(1)} %fusion.34, bf16[1,2048,1024]{2,1,0:T(8,128)(2,1)S(1)} %copy-done.3, f32[256,2048]{1,0:T(8,128)S(1)} %get-tuple-element.69, f32[256]{0:T(256)S(1)} %get-tuple-element.68), kind=kOutput, calls=%fused_computation.63 | convolution fusion | flops 1075052544 | bytes 7342080 | tf_op jit(solution)/shard_map/dot_general | solution.py:22
  36.4 0.5 collective-permute-done.10
  37.4 0.8 %collective-permute-start.15 = (f16[128,1024]{1,0:T(8,128)(2,1)S(1)}, f16[128,1024]{1,0:T(8,128)(2,1)S(1)}, u32[]{:S(2)}, u32[]{:S(2)}) collective-permute-start(f16[128,1024]{1,0:T(8,128)(2,1)S(1)} %fusion.70), channel_id=1, source_target_pairs={{4,0},{6,2},{8,4},{10,6},{12,8},{14,10},{16,12},{18,14},{20,16},{2... | collective-permute-start | bytes 786440 | tf_op jit(solution)/shard_map/ppermute | solution.py:52
  38.2 7.6 %collective-permute-done.7 = f32[128]{0:T(128)S(1)} collective-permute-done((f32[128]{0:T(128)S(1)}, f32[128]{0:T(128)S(1)}, u32[]{:S(2)}, u32[]{:S(2)}) %collective-permute-start.7) | collective-permute-done | bytes 544 | tf_op jit(solution)/shard_map/ppermute | solution.py:52
  45.7 5.1 %collective-permute-start.16 = (f32[128]{0:T(128)S(1)}, f32[128]{0:T(128)S(1)}, u32[]{:S(2)}, u32[]{:S(2)}) collective-permute-start(f32[128]{0:T(128)S(1)} %bitcast.253), channel_id=1, source_target_pairs={{4,0},{6,2},{8,4},{10,6},{12,8},{14,10},{16,12},{18,14},{20,16},{2... | collective-permute-start | bytes 1544 | tf_op jit(solution)/shard_map/ppermute | solution.py:52
  51.1 1.6 %collective-permute-start.13 = (f16[128,1024]{1,0:T(8,128)(2,1)S(1)}, f16[128,1024]{1,0:T(8,128)(2,1)S(1)}, u32[]{:S(2)}, u32[]{:S(2)}) collective-permute-start(f16[128,1024]{1,0:T(8,128)(2,1)S(1)} %fusion.71), channel_id=1, source_target_pairs={{0,1},{1,0},{2,3},{3,2},{4,5},{5,4},{6,7},{7,6},{8,9},{9,8},{10,11... | collective-permute-start | bytes 786440 | tf_op jit(solution)/shard_map/ppermute | solution.py:52
  52.7 0.5 collective-permute-start.14
  53.5 1.6 %collective-permute-start.18 = (f16[128,1024]{1,0:T(8,128)(2,1)S(1)}, f16[128,1024]{1,0:T(8,128)(2,1)S(1)}, u32[]{:S(2)}, u32[]{:S(2)}) collective-permute-start(f16[128,1024]{1,0:T(8,128)(2,1)S(1)} %fusion.72), channel_id=1, source_target_pairs={{0,1},{1,0},{2,3},{3,2},{4,5},{5,4},{6,7},{7,6},{8,9},{9,8},{10,11... | collective-permute-start | bytes 786440 | tf_op jit(solution)/shard_map/ppermute | solution.py:52
  55.1 3.9 %collective-permute-done.14 = f32[128]{0:T(128)S(1)} collective-permute-done((f32[128]{0:T(128)S(1)}, f32[128]{0:T(128)S(1)}, u32[]{:S(2)}, u32[]{:S(2)}) %collective-permute-start.14) | collective-permute-done | bytes 544 | tf_op jit(solution)/shard_map/ppermute | solution.py:52
  59.0 1.6 %collective-permute-start.17 = (f32[128]{0:T(128)S(1)}, f32[128]{0:T(128)S(1)}, u32[]{:S(2)}, u32[]{:S(2)}) collective-permute-start(f32[128]{0:T(128)S(1)} %bitcast.245), channel_id=1, source_target_pairs={{0,1},{1,0},{2,3},{3,2},{4,5},{5,4},{6,7},{7,6},{8,9},{9,8},{10,11... | collective-permute-start | bytes 1544 | tf_op jit(solution)/shard_map/ppermute | solution.py:52
  60.8 1.9 %collective-permute-done.17 = f32[128]{0:T(128)S(1)} collective-permute-done((f32[128]{0:T(128)S(1)}, f32[128]{0:T(128)S(1)}, u32[]{:S(2)}, u32[]{:S(2)}) %collective-permute-start.17) | collective-permute-done | bytes 544 | tf_op jit(solution)/shard_map/ppermute | solution.py:52
  63.3 0.8 %copy-done = bf16[256,1024]{1,0:T(8,128)(2,1)} copy-done((bf16[256,1024]{1,0:T(8,128)(2,1)}, bf16[256,1024]{1,0:T(8,128)(2,1)S(1)}, u32[]{:S(2)}) %copy-start) | copy-done | bytes 524312
  (52 shorter events, 3.8 us)
Async XLA Ops:
  1.7 12.4 %collective-permute-start.1 = (bf16[128,1024]{1,0:T(8,128)(2,1)S(1)}, bf16[128,1024]{1,0:T(8,128)(2,1)S(1)}, u32[]{:S(2)}, u32[]{:S(2)}) collective-permute-start(bf16[128,1024]{1,0:T(8,128)(2,1)S(1)} %get-tuple-element.41), channel_id=1, source_target_pairs={{0,4},{2,6},{4,8},{6,10},{8,12},{10,14},{12,16},{14,18},{16,20},{1... | collective-permute-start | bytes 786440 | tf_op jit(solution)/shard_map/ppermute | solution.py:52
  4.8 4.1 %copy-start.3 = (bf16[1,2048,1024]{2,1,0:T(8,128)(2,1)S(1)}, bf16[1,2048,1024]{2,1,0:T(8,128)(2,1)}, u32[]{:S(2)}) copy-start(bf16[1,2048,1024]{2,1,0:T(8,128)(2,1)} %param.5) | copy-start | bytes 12582916
  8.9 6.7 %copy-start.2 = (bf16[1,2048,1024]{2,1,0:T(8,128)(2,1)S(1)}, bf16[1,2048,1024]{2,1,0:T(8,128)(2,1)}, u32[]{:S(2)}) copy-start(bf16[1,2048,1024]{2,1,0:T(8,128)(2,1)} %param.4) | copy-start | bytes 12582916
  14.1 1.5 %collective-permute-start.2 = (bf16[128,1024]{1,0:T(8,128)(2,1)S(1)}, bf16[128,1024]{1,0:T(8,128)(2,1)S(1)}, u32[]{:S(2)}, u32[]{:S(2)}) collective-permute-start(bf16[128,1024]{1,0:T(8,128)(2,1)S(1)} %collective-permute-done.1), channel_id=1, source_target_pairs={{0,2},{2,0},{4,6},{6,4},{8,10},{10,8},{12,14},{14,12},{16,18},{18,... | collective-permute-start | bytes 786440 | tf_op jit(solution)/shard_map/ppermute | solution.py:52
  14.1 10.4 %collective-permute-start = (bf16[256,1024]{1,0:T(8,128)(2,1)S(1)}, bf16[256,1024]{1,0:T(8,128)(2,1)S(1)}, u32[]{:S(2)}, u32[]{:S(2)}) collective-permute-start(bf16[256,1024]{1,0:T(8,128)(2,1)S(1)} %copy.10), channel_id=1, source_target_pairs={{0,2},{2,8},{4,6},{6,12},{8,10},{10,16},{12,14},{14,20},{16,18},{1... | collective-permute-start | bytes 1572872 | tf_op jit(solution)/shard_map/ppermute | solution.py:52
  18.9 1.6 %collective-permute-start.4 = (f16[128,1024]{1,0:T(8,128)(2,1)S(1)}, f16[128,1024]{1,0:T(8,128)(2,1)S(1)}, u32[]{:S(2)}, u32[]{:S(2)}) collective-permute-start(f16[128,1024]{1,0:T(8,128)(2,1)S(1)} %slice_convert_fusion.1), channel_id=1, source_target_pairs={{0,2},{2,0},{4,6},{6,4},{8,10},{10,8},{12,14},{14,12},{16,18},{18,... | collective-permute-start | bytes 786440 | tf_op jit(solution)/shard_map/ppermute | solution.py:52
  19.1 1.4 %collective-permute-start.3 = (f32[128]{0:T(128)S(1)}, f32[128]{0:T(128)S(1)}, u32[]{:S(2)}, u32[]{:S(2)}) collective-permute-start(f32[128]{0:T(128)S(1)} %slice.83), channel_id=1, source_target_pairs={{0,2},{2,0},{4,6},{6,4},{8,10},{10,8},{12,14},{14,12},{16,18},{18,... | collective-permute-start | bytes 1544 | tf_op jit(solution)/shard_map/ppermute | solution.py:52
  19.5 11.0 %collective-permute-start.8 = (bf16[128,1024]{1,0:T(8,128)(2,1)S(1)}, bf16[128,1024]{1,0:T(8,128)(2,1)S(1)}, u32[]{:S(2)}, u32[]{:S(2)}) collective-permute-start(bf16[128,1024]{1,0:T(8,128)(2,1)S(1)} %get-tuple-element.40), channel_id=1, source_target_pairs={{0,4},{2,6},{4,8},{6,10},{8,12},{10,14},{12,16},{14,18},{16,20},{1... | collective-permute-start | bytes 786440 | tf_op jit(solution)/shard_map/ppermute | solution.py:52
  30.6 1.5 %collective-permute-start.9 = (bf16[128,1024]{1,0:T(8,128)(2,1)S(1)}, bf16[128,1024]{1,0:T(8,128)(2,1)S(1)}, u32[]{:S(2)}, u32[]{:S(2)}) collective-permute-start(bf16[128,1024]{1,0:T(8,128)(2,1)S(1)} %collective-permute-done.8), channel_id=1, source_target_pairs={{0,2},{2,0},{4,6},{6,4},{8,10},{10,8},{12,14},{14,12},{16,18},{18,... | collective-permute-start | bytes 786440 | tf_op jit(solution)/shard_map/ppermute | solution.py:52
  30.6 15.1 %collective-permute-start.6 = (f16[128,1024]{1,0:T(8,128)(2,1)S(1)}, f16[128,1024]{1,0:T(8,128)(2,1)S(1)}, u32[]{:S(2)}, u32[]{:S(2)}) collective-permute-start(f16[128,1024]{1,0:T(8,128)(2,1)S(1)} %fusion.69), channel_id=1, source_target_pairs={{4,0},{6,2},{8,4},{10,6},{12,8},{14,10},{16,12},{18,14},{20,16},{2... | collective-permute-start | bytes 786440 | tf_op jit(solution)/shard_map/ppermute | solution.py:52
  35.3 1.8 %collective-permute-start.11 = (f16[128,1024]{1,0:T(8,128)(2,1)S(1)}, f16[128,1024]{1,0:T(8,128)(2,1)S(1)}, u32[]{:S(2)}, u32[]{:S(2)}) collective-permute-start(f16[128,1024]{1,0:T(8,128)(2,1)S(1)} %slice_convert_fusion), channel_id=1, source_target_pairs={{0,2},{2,0},{4,6},{6,4},{8,10},{10,8},{12,14},{14,12},{16,18},{18,... | collective-permute-start | bytes 786440 | tf_op jit(solution)/shard_map/ppermute | solution.py:52
  35.5 1.4 %collective-permute-start.10 = (f32[128]{0:T(128)S(1)}, f32[128]{0:T(128)S(1)}, u32[]{:S(2)}, u32[]{:S(2)}) collective-permute-start(f32[128]{0:T(128)S(1)} %slice.91), channel_id=1, source_target_pairs={{0,2},{2,0},{4,6},{6,4},{8,10},{10,8},{12,14},{14,12},{16,18},{18,... | collective-permute-start | bytes 1544 | tf_op jit(solution)/shard_map/ppermute | solution.py:52
  35.9 15.0 %collective-permute-start.12 = (f16[256,1024]{1,0:T(8,128)(2,1)S(1)}, f16[256,1024]{1,0:T(8,128)(2,1)S(1)}, u32[]{:S(2)}, u32[]{:S(2)}) collective-permute-start(f16[256,1024]{1,0:T(8,128)(2,1)S(1)} %fusion.42), channel_id=1, source_target_pairs={{2,0},{8,2},{6,4},{12,6},{10,8},{16,10},{14,12},{20,14},{18,16},{2... | collective-permute-start | bytes 1572872 | tf_op jit(solution)/shard_map/ppermute | solution.py:52
  36.2 9.6 %collective-permute-start.7 = (f32[128]{0:T(128)S(1)}, f32[128]{0:T(128)S(1)}, u32[]{:S(2)}, u32[]{:S(2)}) collective-permute-start(f32[128]{0:T(128)S(1)} %bitcast.252), channel_id=1, source_target_pairs={{4,0},{6,2},{8,4},{10,6},{12,8},{14,10},{16,12},{18,14},{20,16},{2... | collective-permute-start | bytes 1544 | tf_op jit(solution)/shard_map/ppermute | solution.py:52
  36.9 13.9 %collective-permute-start.5 = (f32[256]{0:T(256)S(1)}, f32[256]{0:T(256)S(1)}, u32[]{:S(2)}, u32[]{:S(2)}) collective-permute-start(f32[256]{0:T(256)S(1)} %log_add_fusion.1), channel_id=1, source_target_pairs={{2,0},{8,2},{6,4},{12,6},{10,8},{16,10},{14,12},{20,14},{18,16},{2... | collective-permute-start | bytes 3080 | tf_op jit(solution)/shard_map/ppermute | solution.py:52
  37.4 15.8 %collective-permute-start.15 = (f16[128,1024]{1,0:T(8,128)(2,1)S(1)}, f16[128,1024]{1,0:T(8,128)(2,1)S(1)}, u32[]{:S(2)}, u32[]{:S(2)}) collective-permute-start(f16[128,1024]{1,0:T(8,128)(2,1)S(1)} %fusion.70), channel_id=1, source_target_pairs={{4,0},{6,2},{8,4},{10,6},{12,8},{14,10},{16,12},{18,14},{20,16},{2... | collective-permute-start | bytes 786440 | tf_op jit(solution)/shard_map/ppermute | solution.py:52
  45.7 7.5 %collective-permute-start.16 = (f32[128]{0:T(128)S(1)}, f32[128]{0:T(128)S(1)}, u32[]{:S(2)}, u32[]{:S(2)}) collective-permute-start(f32[128]{0:T(128)S(1)} %bitcast.253), channel_id=1, source_target_pairs={{4,0},{6,2},{8,4},{10,6},{12,8},{14,10},{16,12},{18,14},{20,16},{2... | collective-permute-start | bytes 1544 | tf_op jit(solution)/shard_map/ppermute | solution.py:52
  51.1 7.9 %collective-permute-start.13 = (f16[128,1024]{1,0:T(8,128)(2,1)S(1)}, f16[128,1024]{1,0:T(8,128)(2,1)S(1)}, u32[]{:S(2)}, u32[]{:S(2)}) collective-permute-start(f16[128,1024]{1,0:T(8,128)(2,1)S(1)} %fusion.71), channel_id=1, source_target_pairs={{0,1},{1,0},{2,3},{3,2},{4,5},{5,4},{6,7},{7,6},{8,9},{9,8},{10,11... | collective-permute-start | bytes 786440 | tf_op jit(solution)/shard_map/ppermute | solution.py:52
  52.7 6.3 %collective-permute-start.14 = (f32[128]{0:T(128)S(1)}, f32[128]{0:T(128)S(1)}, u32[]{:S(2)}, u32[]{:S(2)}) collective-permute-start(f32[128]{0:T(128)S(1)} %bitcast.244), channel_id=1, source_target_pairs={{0,1},{1,0},{2,3},{3,2},{4,5},{5,4},{6,7},{7,6},{8,9},{9,8},{10,11... | collective-permute-start | bytes 1544 | tf_op jit(solution)/shard_map/ppermute | solution.py:52
  53.5 9.2 %collective-permute-start.18 = (f16[128,1024]{1,0:T(8,128)(2,1)S(1)}, f16[128,1024]{1,0:T(8,128)(2,1)S(1)}, u32[]{:S(2)}, u32[]{:S(2)}) collective-permute-start(f16[128,1024]{1,0:T(8,128)(2,1)S(1)} %fusion.72), channel_id=1, source_target_pairs={{0,1},{1,0},{2,3},{3,2},{4,5},{5,4},{6,7},{7,6},{8,9},{9,8},{10,11... | collective-permute-start | bytes 786440 | tf_op jit(solution)/shard_map/ppermute | solution.py:52
  59.0 3.6 %collective-permute-start.17 = (f32[128]{0:T(128)S(1)}, f32[128]{0:T(128)S(1)}, u32[]{:S(2)}, u32[]{:S(2)}) collective-permute-start(f32[128]{0:T(128)S(1)} %bitcast.245), channel_id=1, source_target_pairs={{0,1},{1,0},{2,3},{3,2},{4,5},{5,4},{6,7},{7,6},{8,9},{9,8},{10,11... | collective-permute-start | bytes 1544 | tf_op jit(solution)/shard_map/ppermute | solution.py:52
  62.7 0.6 copy-start.1
  63.3 0.8 %copy-start = (bf16[256,1024]{1,0:T(8,128)(2,1)}, bf16[256,1024]{1,0:T(8,128)(2,1)S(1)}, u32[]{:S(2)}) copy-start(bf16[256,1024]{1,0:T(8,128)(2,1)S(1)} %fusion.74) | copy-start | bytes 1572868

commit v4 on v3

--- a/solution.py
+++ b/solution.py
@@ -1,10 +1,14 @@
 import jax
 import jax.numpy as jnp
 from jax import lax
+from jax.experimental import pallas as pl
+from jax.experimental.pallas import tpu as pltpu
 from jax.sharding import PartitionSpec as P
 
 
 sharpness = 2.5
+PIECES = 8
+GRANT = 4 * 2**20
 SPLIT = (1, 1)
 
 
@@ -21,6 +25,65 @@
     total = jnp.sum(weights, axis=1, keepdims=True)
     weighted = jnp.dot(weights.astype(jnp.bfloat16), values, preferred_element_type=jnp.float32)
     return weighted / total, top + jnp.log(total)
+
+
+def parts_kernel(*refs):
+    count = (len(refs) - 3) // 3
+    queries, (keys_ref, values_ref), outs, scores_ref = (
+        refs[:count],
+        refs[count : count + 2],
+        refs[count + 2 : -1],
+        refs[-1],
+    )
+    block = jnp.concatenate([q[...] for q in queries]) if count > 1 else queries[0][...]
+    scale = sharpness / block.shape[1] ** 0.5
+    step = keys_ref.shape[0] // PIECES
+    top = None
+    for j in range(PIECES):
+        at = slice(j * step, (j + 1) * step)
+        scores = scale * lax.dot_general(
+            block, keys_ref[at, :], (((1,), (1,)), ((), ())), preferred_element_type=jnp.float32
+        )
+        scores_ref[:, at] = scores
+        highest = jnp.max(scores, axis=1, keepdims=True)
+        top = highest if top is None else jnp.maximum(top, highest)
+    total = 0.0
+    weighted = 0.0
+    for j in range(PIECES):
+        at = slice(j * step, (j + 1) * step)
+        weights = jnp.exp(scores_ref[:, at] - top)
+        total = total + jnp.sum(weights, axis=1, keepdims=True)
+        weighted = weighted + jnp.dot(
+            weights.astype(jnp.bfloat16), values_ref[at, :], preferred_element_type=jnp.float32
+        )
+    mean = weighted / total
+    level = jnp.transpose(jnp.broadcast_to(top + jnp.log(total), (block.shape[0], 128)))
+    row = 0
+    for k, q in enumerate(queries):
+        rows = slice(row, row + q.shape[0])
+        outs[2 * k][...] = mean[rows]
+        outs[2 * k + 1][...] = level[0:8, rows]
+        row = rows.stop
+
+
+def parts(queries, keys, values):
+    shapes = [
+        jax.ShapeDtypeStruct(shape, jnp.float32)
+        for q in queries
+        for shape in ((q.shape[0], values.shape[1]), (8, q.shape[0]))
+    ]
+    rows = sum(q.shape[0] for q in queries)
+    vmem = pl.BlockSpec(memory_space=pltpu.VMEM)
+    out = pl.pallas_call(
+        parts_kernel,
+        out_shape=tuple(shapes),
+        in_specs=[vmem] * (len(queries) + 2),
+        out_specs=(vmem,) * len(shapes),
+        scratch_shapes=[pltpu.VMEM((rows, keys.shape[0]), jnp.float32)],
+        compiler_params=pltpu.CompilerParams(vmem_limit_bytes=GRANT),
+        name="parts",
+    )(*queries, keys, values)
+    return [(out[2 * k], out[2 * k + 1][0][:, None]) for k in range(len(queries))]
 
 
 def joined(all_parts):
@@ -68,12 +131,13 @@
     other = move(queries, fourth)
     near_2 = move(cut(queries, 1), two)
     keys, values = corpus[0], attributions[0]
+    keys_1 = pltpu.with_memory_space_constraint(keys, pltpu.VMEM)
+    values_1 = pltpu.with_memory_space_constraint(values, pltpu.VMEM)
     own = plain_part(queries, keys, values)
 
     def window(near):
         far = move(near, pair)
-        both = plain_part(jnp.concatenate([near, far]), keys, values)
-        near_part, far_part = (jax.tree.map(lambda a: a[at], both) for at in (slice(near.shape[0]), slice(near.shape[0], None)))
+        near_part, far_part = parts([near, far], keys_1, values_1)
         far_back = move_part(packed(far_part), pair)
         mine = packed(joined([near_part, far_back]))
         return mine, move_part(mine, two_back)
@@ -91,7 +155,7 @@
         )
 
     mine_1, back_1 = window(after(near_1, own))
-    other_part = plain_part(after(other, mine_1), keys, values)
+    (other_part,) = parts([after(other, mine_1)], keys_1, values_1)
     other_part = packed(other_part)
     other_back = move_part(other_part, fourth_back)
     mine_2, back_2 = window(after(near_2, other_part))

time: 64.2 us -> 62.2 us (0.969)
  matrix products: 13.3 us -> 5.04 us
  Pallas kernels: 0 us -> 8.2 us
  waiting for transfers between devices: 27.8 us -> 26 us
  other arithmetic: 3.18 us -> 1.94 us
  starting transfers between devices: 16.6 us -> 17.8 us
    pallas_call x0 -> x3, Pallas kernels: none -> 8.2 us  [parts(): pl.pallas_call(parts_kernel, out_shape=tuple(shapes), in_specs=[vmem] * (...]
    dot_general x4 -> x1, matrix products: 5.51 us -> 1.33 us  [plain_part(): jnp.dot(weights.astype(jnp.bfloat16), values, preferred_element_type=jnp....]
    dot_general x4 -> x1, matrix products: 7.83 us -> 3.71 us  [plain_part(): jnp.dot(block_queries, keys.T, preferred_element_type=jnp.float32)]
    ppermute x19, waiting for transfers between devices: 27.8 us -> 26 us  [move(): return lax.ppermute(value, axis, pairs)]
    reduce_sum x4 -> x1, other arithmetic: 1.75 us -> 0.44 us  [plain_part(): total = jnp.sum(weights, axis=1, keepdims=True)]
    ppermute x19, starting transfers between devices: 16.6 us -> 17.8 us  [move(): return lax.ppermute(value, axis, pairs)]
  transfers between devices with their start and end apart: 19 -> 19, of which waited for: 10 -> 10; matrix products, arithmetic and copies ran while one was open for 26% -> 11% of each run, Pallas kernels for 0% -> 13%
where the time goes in v4:
time: 62.2 us; the launch traced here: 62 us
  waiting for transfers between devices  26 us (42%)
  starting transfers between devices  17.8 us (29%)
  Pallas kernels  8.2 us (13%)
  matrix products  5.04 us (8%)
  local copies, waits for them, and re-layouts  2.23 us (4%)
  other arithmetic  1.94 us (3%)
  between operations  0.83 us (1%)
    ppermute x19, waiting for transfers between devices, move(): return lax.ppermute(value, axis, pairs)  26 us
    ppermute x19, starting transfers between devices, move(): return lax.ppermute(value, axis, pairs)  17.8 us
    pallas_call x3, Pallas kernels, parts(): pl.pallas_call(parts_kernel, out_shape=tuple(shapes), in_specs=[vmem] * (...  8.2 us
    dot_general x1, matrix products, plain_part(): jnp.dot(block_queries, keys.T, preferred_element_type=jnp.float32)  3.71 us
    unnamed x9, local copies, waits for them, and re-layouts  2.19 us
    dot_general x1, matrix products, plain_part(): jnp.dot(weights.astype(jnp.bfloat16), values, preferred_element_type=jnp....  1.33 us
  transfers between devices with their start and end apart: 19, of which 10 were waited for; matrix products, arithmetic and copies ran while one was open for 11% of the time, Pallas kernels for 13%

profile of v4, /device:TPU:0, one launch (start us, length us, event | category | flops | bytes accessed | tf_op | source)
XLA Modules:
  0.0 62.0 jit_solution(12842114992630199084)
XLA Ops:
  0.6 1.0 %copy.10 = bf16[256,1024]{1,0:T(8,128)(2,1)S(1)} copy(bf16[256,1024]{1,0:T(8,128)(2,1)} %param.3) | data formatting | bytes 1048576
  1.7 3.0 %collective-permute-start.1 = (bf16[128,1024]{1,0:T(8,128)(2,1)S(1)}, bf16[128,1024]{1,0:T(8,128)(2,1)S(1)}, u32[]{:S(2)}, u32[]{:S(2)}) collective-permute-start(bf16[128,1024]{1,0:T(8,128)(2,1)S(1)} %get-tuple-element.69), channel_id=1, source_target_pairs={{0,4},{2,6},{4,8},{6,10},{8,12},{10,14},{12,16},{14,18},{16,20},{1... | collective-permute-start | bytes 786440 | tf_op jit(solution)/shard_map/ppermute | solution.py:115
  4.8 3.7 %fusion.40 = (f32[256]{0:T(256)S(1)}, f32[256,2048]{1,0:T(8,128)S(1)}) fusion(bf16[256,1024]{1,0:T(8,128)(2,1)S(1)} %copy.10, bf16[1,2048,1024]{2,1,0:T(8,128)(2,1)} %param.4), kind=kOutput, calls=%fused_computation.76 | convolution fusion | flops 1074790144 | bytes 6816768 | tf_op jit(solution)/shard_map/dot_general | solution.py:20
  8.5 0.4 fusion
  8.9 1.3 %convolution_divide_fusion = f32[256,1024]{1,0:T(8,128)S(1)} fusion(f32[256,2048]{1,0:T(8,128)S(1)} %get-tuple-element.83, f32[256]{0:T(256)S(1)} %get-tuple-element.82, f32[256]{0:T(256)S(1)} %fusion, bf16[1,2048,1024]{2,1,0:T(8,128)(2,1)S(1)} %copy-done.1), kind=kOutput, calls=%fused_computation.4 | convolution fusion | flops 1075052544 | bytes 7342080 | tf_op jit(solution)/shard_map/dot_general | solution.py:26
  10.3 3.8 %collective-permute-done.1.refs_0_ = bf16[128,1024]{1,0:T(8,128)(2,1)S(1)} collective-permute-done((bf16[128,1024]{1,0:T(8,128)(2,1)S(1)}, bf16[128,1024]{1,0:T(8,128)(2,1)S(1)}, u32[]{:S(2)}, u32[]{:S(2)}) %collective-permute-start.1) | collective-permute-done | bytes 262176 | tf_op jit(solution)/shard_map/ppermute | solution.py:115
  14.1 0.5 collective-permute-start
  14.6 1.0 %collective-permute-done.2.refs_1_ = bf16[128,1024]{1,0:T(8,128)(2,1)S(1)} collective-permute-done((bf16[128,1024]{1,0:T(8,128)(2,1)S(1)}, bf16[128,1024]{1,0:T(8,128)(2,1)S(1)}, u32[]{:S(2)}, u32[]{:S(2)}) %collective-permute-start.2) | collective-permute-done | bytes 262176 | tf_op jit(solution)/shard_map/ppermute | solution.py:115
  15.6 2.7 %parts.3 = (f32[128,1024]{1,0:T(8,128)S(1)}, f32[8,128]{1,0:T(8,128)S(1)}, f32[128,1024]{1,0:T(8,128)S(1)}, f32[8,128]{1,0:T(8,128)S(1)}) custom-call(bf16[128,1024]{1,0:T(8,128)(2,1)S(1)} %collective-permute-done.1.refs_0_, bf16[128,1024]{1,0:T(8,128)(2,1)S(1)} %collective-permute-done.2.refs_1_, bf16[2048,1024]{1,0:T(8,128)(2,1)S(1)} %bitcast.146, ...), custom_call_target="tpu_custom_call" | custom-call | tf_op jit(solution)/shard_map/parts/pallas_call | solution.py:77
  18.6 0.4 collective-permute-start.3
  19.0 1.0 %collective-permute-done.3 = f32[128]{0:T(128)S(1)} collective-permute-done((f32[128]{0:T(128)S(1)}, f32[128]{0:T(128)S(1)}, u32[]{:S(2)}, u32[]{:S(2)}) %collective-permute-start.3) | collective-permute-done | bytes 544 | tf_op jit(solution)/shard_map/ppermute | solution.py:115
  20.2 4.3 %collective-permute-done.refs_0_ = bf16[256,1024]{1,0:T(8,128)(2,1)S(1)} collective-permute-done((bf16[256,1024]{1,0:T(8,128)(2,1)S(1)}, bf16[256,1024]{1,0:T(8,128)(2,1)S(1)}, u32[]{:S(2)}, u32[]{:S(2)}) %collective-permute-start) | collective-permute-done | bytes 524320 | tf_op jit(solution)/shard_map/ppermute | solution.py:115
  24.5 2.7 %parts.4 = (f32[256,1024]{1,0:T(8,128)S(1)}, f32[8,256]{1,0:T(8,128)S(1)}) custom-call(bf16[256,1024]{1,0:T(8,128)(2,1)S(1)} %collective-permute-done.refs_0_, bf16[2048,1024]{1,0:T(8,128)(2,1)S(1)} %bitcast.147, bf16[2048,1024]{1,0:T(8,128)(2,1)S(1)} %bitcast.150), custom_call_target="tpu_custom_call" | custom-call | tf_op jit(solution)/shard_map/parts/pallas_call | solution.py:77
  27.3 2.7 %collective-permute-done.8.refs_0_ = bf16[128,1024]{1,0:T(8,128)(2,1)S(1)} collective-permute-done((bf16[128,1024]{1,0:T(8,128)(2,1)S(1)}, bf16[128,1024]{1,0:T(8,128)(2,1)S(1)}, u32[]{:S(2)}, u32[]{:S(2)}) %collective-permute-start.8) | collective-permute-done | bytes 262176 | tf_op jit(solution)/shard_map/ppermute | solution.py:115
  30.1 0.5 collective-permute-start.12
  30.7 0.9 %collective-permute-done.9.refs_1_ = bf16[128,1024]{1,0:T(8,128)(2,1)S(1)} collective-permute-done((bf16[128,1024]{1,0:T(8,128)(2,1)S(1)}, bf16[128,1024]{1,0:T(8,128)(2,1)S(1)}, u32[]{:S(2)}, u32[]{:S(2)}) %collective-permute-start.9) | collective-permute-done | bytes 262176 | tf_op jit(solution)/shard_map/ppermute | solution.py:115
  31.6 2.7 %parts.5 = (f32[128,1024]{1,0:T(8,128)S(1)}, f32[8,128]{1,0:T(8,128)S(1)}, f32[128,1024]{1,0:T(8,128)S(1)}, f32[8,128]{1,0:T(8,128)S(1)}) custom-call(bf16[128,1024]{1,0:T(8,128)(2,1)S(1)} %collective-permute-done.8.refs_0_, bf16[128,1024]{1,0:T(8,128)(2,1)S(1)} %collective-permute-done.9.refs_1_, bf16[2048,1024]{1,0:T(8,128)(2,1)S(1)} %bitcast.148, ...), custom_call_target="tpu_custom_call" | custom-call | tf_op jit(solution)/shard_map/parts/pallas_call | solution.py:77
  34.6 0.4 collective-permute-start.10
  35.2 0.8 %collective-permute-done.10 = f32[128]{0:T(128)S(1)} collective-permute-done((f32[128]{0:T(128)S(1)}, f32[128]{0:T(128)S(1)}, u32[]{:S(2)}, u32[]{:S(2)}) %collective-permute-start.10) | collective-permute-done | bytes 544 | tf_op jit(solution)/shard_map/ppermute | solution.py:115
  36.0 0.6 collective-permute-start.7
  36.8 1.4 %collective-permute-start.15 = (f16[128,1024]{1,0:T(8,128)(2,1)S(1)}, f16[128,1024]{1,0:T(8,128)(2,1)S(1)}, u32[]{:S(2)}, u32[]{:S(2)}) collective-permute-start(f16[128,1024]{1,0:T(8,128)(2,1)S(1)} %divide_convert_fusion.2), channel_id=1, source_target_pairs={{4,0},{6,2},{8,4},{10,6},{12,8},{14,10},{16,12},{18,14},{20,16},{2... | collective-permute-start | bytes 786440 | tf_op jit(solution)/shard_map/ppermute | solution.py:115
  38.2 6.9 %collective-permute-done.7 = f32[128]{0:T(128)S(1)} collective-permute-done((f32[128]{0:T(128)S(1)}, f32[128]{0:T(128)S(1)}, u32[]{:S(2)}, u32[]{:S(2)}) %collective-permute-start.7) | collective-permute-done | bytes 544 | tf_op jit(solution)/shard_map/ppermute | solution.py:115
  45.1 5.1 %collective-permute-start.16 = (f32[128]{0:T(128)S(1)}, f32[128]{0:T(128)S(1)}, u32[]{:S(2)}, u32[]{:S(2)}) collective-permute-start(f32[128]{0:T(128)S(1)} %get-tuple-element.48), channel_id=1, source_target_pairs={{4,0},{6,2},{8,4},{10,6},{12,8},{14,10},{16,12},{18,14},{20,16},{2... | collective-permute-start | bytes 1544 | tf_op jit(solution)/shard_map/ppermute | solution.py:115
  50.5 1.6 %collective-permute-start.13 = (f16[128,1024]{1,0:T(8,128)(2,1)S(1)}, f16[128,1024]{1,0:T(8,128)(2,1)S(1)}, u32[]{:S(2)}, u32[]{:S(2)}) collective-permute-start(f16[128,1024]{1,0:T(8,128)(2,1)S(1)} %fusion.10), channel_id=1, source_target_pairs={{0,1},{1,0},{2,3},{3,2},{4,5},{5,4},{6,7},{7,6},{8,9},{9,8},{10,11... | collective-permute-start | bytes 786440 | tf_op jit(solution)/shard_map/ppermute | solution.py:115
  52.1 0.5 collective-permute-start.14
  52.6 0.2 fusion.11
  52.9 1.6 %collective-permute-start.18 = (f16[128,1024]{1,0:T(8,128)(2,1)S(1)}, f16[128,1024]{1,0:T(8,128)(2,1)S(1)}, u32[]{:S(2)}, u32[]{:S(2)}) collective-permute-start(f16[128,1024]{1,0:T(8,128)(2,1)S(1)} %fusion.11), channel_id=1, source_target_pairs={{0,1},{1,0},{2,3},{3,2},{4,5},{5,4},{6,7},{7,6},{8,9},{9,8},{10,11... | collective-permute-start | bytes 786440 | tf_op jit(solution)/shard_map/ppermute | solution.py:115
  54.4 2.6 %collective-permute-done.14 = f32[128]{0:T(128)S(1)} collective-permute-done((f32[128]{0:T(128)S(1)}, f32[128]{0:T(128)S(1)}, u32[]{:S(2)}, u32[]{:S(2)}) %collective-permute-start.14) | collective-permute-done | bytes 544 | tf_op jit(solution)/shard_map/ppermute | solution.py:115
  57.0 1.5 %collective-permute-start.17 = (f32[128]{0:T(128)S(1)}, f32[128]{0:T(128)S(1)}, u32[]{:S(2)}, u32[]{:S(2)}) collective-permute-start(f32[128]{0:T(128)S(1)} %bitcast.155), channel_id=1, source_target_pairs={{0,1},{1,0},{2,3},{3,2},{4,5},{5,4},{6,7},{7,6},{8,9},{9,8},{10,11... | collective-permute-start | bytes 1544 | tf_op jit(solution)/shard_map/ppermute | solution.py:115
  58.8 1.9 %collective-permute-done.17 = f32[128]{0:T(128)S(1)} collective-permute-done((f32[128]{0:T(128)S(1)}, f32[128]{0:T(128)S(1)}, u32[]{:S(2)}, u32[]{:S(2)}) %collective-permute-start.17) | collective-permute-done | bytes 544 | tf_op jit(solution)/shard_map/ppermute | solution.py:115
  60.9 0.3 copy-done.3
  61.2 0.8 %copy-done.2 = bf16[256,1024]{1,0:T(8,128)(2,1)} copy-done((bf16[256,1024]{1,0:T(8,128)(2,1)}, bf16[256,1024]{1,0:T(8,128)(2,1)S(1)}, u32[]{:S(2)}) %copy-start.2) | copy-done | bytes 524312
  (45 shorter events, 2.0 us)
Async XLA Ops:
  1.7 12.4 %collective-permute-start.1 = (bf16[128,1024]{1,0:T(8,128)(2,1)S(1)}, bf16[128,1024]{1,0:T(8,128)(2,1)S(1)}, u32[]{:S(2)}, u32[]{:S(2)}) collective-permute-start(bf16[128,1024]{1,0:T(8,128)(2,1)S(1)} %get-tuple-element.69), channel_id=1, source_target_pairs={{0,4},{2,6},{4,8},{6,10},{8,12},{10,14},{12,16},{14,18},{16,20},{1... | collective-permute-start | bytes 786440 | tf_op jit(solution)/shard_map/ppermute | solution.py:115
  4.8 4.2 %copy-start.1 = (bf16[1,2048,1024]{2,1,0:T(8,128)(2,1)S(1)}, bf16[1,2048,1024]{2,1,0:T(8,128)(2,1)}, u32[]{:S(2)}) copy-start(bf16[1,2048,1024]{2,1,0:T(8,128)(2,1)} %param.5) | copy-start | bytes 12582916
  8.9 6.7 %copy-start = (bf16[1,2048,1024]{2,1,0:T(8,128)(2,1)S(1)}, bf16[1,2048,1024]{2,1,0:T(8,128)(2,1)}, u32[]{:S(2)}) copy-start(bf16[1,2048,1024]{2,1,0:T(8,128)(2,1)} %param.4) | copy-start | bytes 12582916
  14.1 1.5 %collective-permute-start.2 = (bf16[128,1024]{1,0:T(8,128)(2,1)S(1)}, bf16[128,1024]{1,0:T(8,128)(2,1)S(1)}, u32[]{:S(2)}, u32[]{:S(2)}) collective-permute-start(bf16[128,1024]{1,0:T(8,128)(2,1)S(1)} %collective-permute-done.1.refs_0_), channel_id=1, source_target_pairs={{0,2},{2,0},{4,6},{6,4},{8,10},{10,8},{12,14},{14,12},{16,18},{18,... | collective-permute-start | bytes 786440 | tf_op jit(solution)/shard_map/ppermute | solution.py:115
  14.1 10.4 %collective-permute-start = (bf16[256,1024]{1,0:T(8,128)(2,1)S(1)}, bf16[256,1024]{1,0:T(8,128)(2,1)S(1)}, u32[]{:S(2)}, u32[]{:S(2)}) collective-permute-start(bf16[256,1024]{1,0:T(8,128)(2,1)S(1)} %copy.10), channel_id=1, source_target_pairs={{0,2},{2,8},{4,6},{6,12},{8,10},{10,16},{12,14},{14,20},{16,18},{1... | collective-permute-start | bytes 1572872 | tf_op jit(solution)/shard_map/ppermute | solution.py:115
  18.4 1.6 %collective-permute-start.4 = (f16[128,1024]{1,0:T(8,128)(2,1)S(1)}, f16[128,1024]{1,0:T(8,128)(2,1)S(1)}, u32[]{:S(2)}, u32[]{:S(2)}) collective-permute-start(f16[128,1024]{1,0:T(8,128)(2,1)S(1)} %convert_element_type.61), channel_id=1, source_target_pairs={{0,2},{2,0},{4,6},{6,4},{8,10},{10,8},{12,14},{14,12},{16,18},{18,... | collective-permute-start | bytes 786440 | tf_op jit(solution)/shard_map/ppermute | solution.py:115
  18.6 1.4 %collective-permute-start.3 = (f32[128]{0:T(128)S(1)}, f32[128]{0:T(128)S(1)}, u32[]{:S(2)}, u32[]{:S(2)}) collective-permute-start(f32[128]{0:T(128)S(1)} %slice_bitcast_fusion.1), channel_id=1, source_target_pairs={{0,2},{2,0},{4,6},{6,4},{8,10},{10,8},{12,14},{14,12},{16,18},{18,... | collective-permute-start | bytes 1544 | tf_op jit(solution)/shard_map/ppermute | solution.py:115
  19.0 11.0 %collective-permute-start.8 = (bf16[128,1024]{1,0:T(8,128)(2,1)S(1)}, bf16[128,1024]{1,0:T(8,128)(2,1)S(1)}, u32[]{:S(2)}, u32[]{:S(2)}) collective-permute-start(bf16[128,1024]{1,0:T(8,128)(2,1)S(1)} %get-tuple-element.68), channel_id=1, source_target_pairs={{0,4},{2,6},{4,8},{6,10},{8,12},{10,14},{12,16},{14,18},{16,20},{1... | collective-permute-start | bytes 786440 | tf_op jit(solution)/shard_map/ppermute | solution.py:115
  30.0 1.5 %collective-permute-start.9 = (bf16[128,1024]{1,0:T(8,128)(2,1)S(1)}, bf16[128,1024]{1,0:T(8,128)(2,1)S(1)}, u32[]{:S(2)}, u32[]{:S(2)}) collective-permute-start(bf16[128,1024]{1,0:T(8,128)(2,1)S(1)} %collective-permute-done.8.refs_0_), channel_id=1, source_target_pairs={{0,2},{2,0},{4,6},{6,4},{8,10},{10,8},{12,14},{14,12},{16,18},{18,... | collective-permute-start | bytes 786440 | tf_op jit(solution)/shard_map/ppermute | solution.py:115
  30.1 20.2 %collective-permute-start.6 = (f16[128,1024]{1,0:T(8,128)(2,1)S(1)}, f16[128,1024]{1,0:T(8,128)(2,1)S(1)}, u32[]{:S(2)}, u32[]{:S(2)}) collective-permute-start(f16[128,1024]{1,0:T(8,128)(2,1)S(1)} %divide_convert_fusion.3), channel_id=1, source_target_pairs={{4,0},{6,2},{8,4},{10,6},{12,8},{14,10},{16,12},{18,14},{20,16},{2... | collective-permute-start | bytes 786440 | tf_op jit(solution)/shard_map/ppermute | solution.py:115
  30.1 20.1 %collective-permute-start.12 = (f16[256,1024]{1,0:T(8,128)(2,1)S(1)}, f16[256,1024]{1,0:T(8,128)(2,1)S(1)}, u32[]{:S(2)}, u32[]{:S(2)}) collective-permute-start(f16[256,1024]{1,0:T(8,128)(2,1)S(1)} %convert_element_type.64), channel_id=1, source_target_pairs={{2,0},{8,2},{6,4},{12,6},{10,8},{16,10},{14,12},{20,14},{18,16},{2... | collective-permute-start | bytes 1572872 | tf_op jit(solution)/shard_map/ppermute | solution.py:115
  34.4 2.2 %collective-permute-start.11 = (f16[128,1024]{1,0:T(8,128)(2,1)S(1)}, f16[128,1024]{1,0:T(8,128)(2,1)S(1)}, u32[]{:S(2)}, u32[]{:S(2)}) collective-permute-start(f16[128,1024]{1,0:T(8,128)(2,1)S(1)} %convert_element_type.65), channel_id=1, source_target_pairs={{0,2},{2,0},{4,6},{6,4},{8,10},{10,8},{12,14},{14,12},{16,18},{18,... | collective-permute-start | bytes 786440 | tf_op jit(solution)/shard_map/ppermute | solution.py:115
  34.6 1.4 %collective-permute-start.10 = (f32[128]{0:T(128)S(1)}, f32[128]{0:T(128)S(1)}, u32[]{:S(2)}, u32[]{:S(2)}) collective-permute-start(f32[128]{0:T(128)S(1)} %slice_bitcast_fusion), channel_id=1, source_target_pairs={{0,2},{2,0},{4,6},{6,4},{8,10},{10,8},{12,14},{14,12},{16,18},{18,... | collective-permute-start | bytes 1544 | tf_op jit(solution)/shard_map/ppermute | solution.py:115
  34.9 15.3 %collective-permute-start.5 = (f32[256]{0:T(256)S(1)}, f32[256]{0:T(256)S(1)}, u32[]{:S(2)}, u32[]{:S(2)}) collective-permute-start(f32[256]{0:T(256)S(1)} %bitcast.160), channel_id=1, source_target_pairs={{2,0},{8,2},{6,4},{12,6},{10,8},{16,10},{14,12},{20,14},{18,16},{2... | collective-permute-start | bytes 3080 | tf_op jit(solution)/shard_map/ppermute | solution.py:115
  36.0 9.1 %collective-permute-start.7 = (f32[128]{0:T(128)S(1)}, f32[128]{0:T(128)S(1)}, u32[]{:S(2)}, u32[]{:S(2)}) collective-permute-start(f32[128]{0:T(128)S(1)} %get-tuple-element.38), channel_id=1, source_target_pairs={{4,0},{6,2},{8,4},{10,6},{12,8},{14,10},{16,12},{18,14},{20,16},{2... | collective-permute-start | bytes 1544 | tf_op jit(solution)/shard_map/ppermute | solution.py:115
  36.8 15.8 %collective-permute-start.15 = (f16[128,1024]{1,0:T(8,128)(2,1)S(1)}, f16[128,1024]{1,0:T(8,128)(2,1)S(1)}, u32[]{:S(2)}, u32[]{:S(2)}) collective-permute-start(f16[128,1024]{1,0:T(8,128)(2,1)S(1)} %divide_convert_fusion.2), channel_id=1, source_target_pairs={{4,0},{6,2},{8,4},{10,6},{12,8},{14,10},{16,12},{18,14},{20,16},{2... | collective-permute-start | bytes 786440 | tf_op jit(solution)/shard_map/ppermute | solution.py:115
  45.1 7.5 %collective-permute-start.16 = (f32[128]{0:T(128)S(1)}, f32[128]{0:T(128)S(1)}, u32[]{:S(2)}, u32[]{:S(2)}) collective-permute-start(f32[128]{0:T(128)S(1)} %get-tuple-element.48), channel_id=1, source_target_pairs={{4,0},{6,2},{8,4},{10,6},{12,8},{14,10},{16,12},{18,14},{20,16},{2... | collective-permute-start | bytes 1544 | tf_op jit(solution)/shard_map/ppermute | solution.py:115
  50.5 6.5 %collective-permute-start.13 = (f16[128,1024]{1,0:T(8,128)(2,1)S(1)}, f16[128,1024]{1,0:T(8,128)(2,1)S(1)}, u32[]{:S(2)}, u32[]{:S(2)}) collective-permute-start(f16[128,1024]{1,0:T(8,128)(2,1)S(1)} %fusion.10), channel_id=1, source_target_pairs={{0,1},{1,0},{2,3},{3,2},{4,5},{5,4},{6,7},{7,6},{8,9},{9,8},{10,11... | collective-permute-start | bytes 786440 | tf_op jit(solution)/shard_map/ppermute | solution.py:115
  52.1 5.0 %collective-permute-start.14 = (f32[128]{0:T(128)S(1)}, f32[128]{0:T(128)S(1)}, u32[]{:S(2)}, u32[]{:S(2)}) collective-permute-start(f32[128]{0:T(128)S(1)} %bitcast.154), channel_id=1, source_target_pairs={{0,1},{1,0},{2,3},{3,2},{4,5},{5,4},{6,7},{7,6},{8,9},{9,8},{10,11... | collective-permute-start | bytes 1544 | tf_op jit(solution)/shard_map/ppermute | solution.py:115
  52.9 7.8 %collective-permute-start.18 = (f16[128,1024]{1,0:T(8,128)(2,1)S(1)}, f16[128,1024]{1,0:T(8,128)(2,1)S(1)}, u32[]{:S(2)}, u32[]{:S(2)}) collective-permute-start(f16[128,1024]{1,0:T(8,128)(2,1)S(1)} %fusion.11), channel_id=1, source_target_pairs={{0,1},{1,0},{2,3},{3,2},{4,5},{5,4},{6,7},{7,6},{8,9},{9,8},{10,11... | collective-permute-start | bytes 786440 | tf_op jit(solution)/shard_map/ppermute | solution.py:115
  57.0 3.6 %collective-permute-start.17 = (f32[128]{0:T(128)S(1)}, f32[128]{0:T(128)S(1)}, u32[]{:S(2)}, u32[]{:S(2)}) collective-permute-start(f32[128]{0:T(128)S(1)} %bitcast.155), channel_id=1, source_target_pairs={{0,1},{1,0},{2,3},{3,2},{4,5},{5,4},{6,7},{7,6},{8,9},{9,8},{10,11... | collective-permute-start | bytes 1544 | tf_op jit(solution)/shard_map/ppermute | solution.py:115
  60.6 0.6 copy-start.3
  61.2 0.8 %copy-start.2 = (bf16[256,1024]{1,0:T(8,128)(2,1)}, bf16[256,1024]{1,0:T(8,128)(2,1)S(1)}, u32[]{:S(2)}) copy-start(bf16[256,1024]{1,0:T(8,128)(2,1)S(1)} %fusion.13) | copy-start | bytes 1572868

commit v5 on v4

--- a/solution.py
+++ b/solution.py
@@ -86,6 +86,37 @@
     return [(out[2 * k], out[2 * k + 1][0][:, None]) for k in range(len(queries))]
 
 
+def store(outs, shape, attributed, level, at):
+    rows = attributed.shape[0]
+
+    def kernel(attributed_ref, level_ref, *refs):
+        out_ref, level_out_ref, sems = refs[-3:]
+        copies = [
+            pltpu.make_async_copy(attributed_ref, out_ref.at[pl.ds(at, rows), :], sems.at[0]),
+            pltpu.make_async_copy(level_ref, level_out_ref.at[:, pl.ds(at, rows)], sems.at[1]),
+        ]
+        for copy in copies:
+            copy.start()
+        for copy in copies:
+            copy.wait()
+
+    vmem = pl.BlockSpec(memory_space=pltpu.VMEM)
+    hbm = pl.BlockSpec(memory_space=pltpu.HBM)
+    return pl.pallas_call(
+        kernel,
+        out_shape=(
+            jax.ShapeDtypeStruct(shape, attributed.dtype),
+            jax.ShapeDtypeStruct((1, shape[0]), level.dtype),
+        ),
+        in_specs=[vmem, vmem] + [hbm] * len(outs),
+        out_specs=(hbm, hbm),
+        scratch_shapes=[pltpu.SemaphoreType.DMA((2,))],
+        input_output_aliases={2 + k: k for k in range(len(outs))},
+        compiler_params=pltpu.CompilerParams(vmem_limit_bytes=GRANT),
+        name="store",
+    )(attributed, level, *outs)
+
+
 def joined(all_parts):
     top = all_parts[0][1]
     for _, level in all_parts[1:]:
@@ -149,10 +180,8 @@
     def finish(outs, mine, theirs, c):
         attributed, log_total = joined([mine, theirs])
         at = edges(c)[0]
-        return (
-            lax.dynamic_update_slice(outs[0], attributed.astype(jnp.bfloat16), (at, 0)),
-            lax.dynamic_update_slice(outs[1], log_total[:, 0], (at,)),
-        )
+        shape = (queries.shape[0], attributed.shape[1])
+        return store(outs, shape, attributed.astype(jnp.bfloat16), log_total[:, 0][None], at)
 
     mine_1, back_1 = window(after(near_1, own))
     (other_part,) = parts([after(other, mine_1)], keys_1, values_1)
@@ -161,10 +190,10 @@
     mine_2, back_2 = window(after(near_2, other_part))
     own_1, theirs_1 = exchange([cut(own, 0), cut(other_back, 0), after(back_1, mine_2)])
     own_2, theirs_2 = exchange([cut(own, 1), cut(other_back, 1), after(back_2, own_1)])
-    outs = (queries, own[1][:, 0])
+    outs = ()
     outs = finish(outs, own_1, after(theirs_1, own_2), 0)
     outs = finish(outs, own_2, theirs_2, 1)
-    return outs
+    return outs[0], outs[1][0]
 
 
 def solution(mesh):

time: 62.2 us -> 61.8 us (level)
  Pallas kernels: 8.2 us -> 9.65 us
  local copies, waits for them, and re-layouts: 2.23 us -> 1.09 us
  waiting for transfers between devices: 26 us -> 25.1 us
    unnamed x9 -> x6, local copies, waits for them, and re-layouts: 2.19 us -> 0.02 us
    pallas_call x0 -> x2, Pallas kernels: none -> 1.45 us  [store(): pl.pallas_call(kernel, out_shape=(jax.ShapeDtypeStruct(shape, attributed....]
    slice x1, local copies, waits for them, and re-layouts: 0.03 us -> 1.07 us  [cut(): return jax.tree.map(lambda a: a[lo:hi], tree)]
    ppermute x19, waiting for transfers between devices: 26 us -> 25.1 us  [move(): return lax.ppermute(value, axis, pairs)]
  transfers between devices with their start and end apart: 19 -> 19, of which waited for: 10 -> 10; matrix products, arithmetic and copies ran while one was open for 11% -> 11% of each run, Pallas kernels for 13% -> 14%
where the time goes in v5:
time: 61.8 us; the launch traced here: 61.6 us
  waiting for transfers between devices  25.1 us (41%)
  starting transfers between devices  17.9 us (29%)
  Pallas kernels  9.65 us (16%)
  matrix products  5.19 us (8%)
  other arithmetic  1.89 us (3%)
  local copies, waits for them, and re-layouts  1.09 us (2%)
  between operations  0.83 us (1%)
    ppermute x19, waiting for transfers between devices, move(): return lax.ppermute(value, axis, pairs)  25.1 us
    ppermute x19, starting transfers between devices, move(): return lax.ppermute(value, axis, pairs)  17.9 us
    pallas_call x3, Pallas kernels, parts(): pl.pallas_call(parts_kernel, out_shape=tuple(shapes), in_specs=[vmem] * (...  8.2 us
    dot_general x1, matrix products, plain_part(): jnp.dot(block_queries, keys.T, preferred_element_type=jnp.float32)  3.86 us
    pallas_call x2, Pallas kernels, store(): pl.pallas_call(kernel, out_shape=(jax.ShapeDtypeStruct(shape, attributed....  1.45 us
    dot_general x1, matrix products, plain_part(): jnp.dot(weights.astype(jnp.bfloat16), values, preferred_element_type=jnp....  1.33 us
  transfers between devices with their start and end apart: 19, of which 10 were waited for; matrix products, arithmetic and copies ran while one was open for 11% of the time, Pallas kernels for 14%

profile of v5, /device:TPU:0, one launch (start us, length us, event | category | flops | bytes accessed | tf_op | source)
XLA Modules:
  0.0 61.6 jit_solution(3020903043831599656)
XLA Ops:
  0.6 1.1 %fusion.37 = (bf16[128,1024]{1,0:T(8,128)(2,1)S(1)}, bf16[128,1024]{1,0:T(8,128)(2,1)S(1)}) fusion(bf16[256,1024]{1,0:T(8,128)(2,1)} %param.3), kind=kLoop, calls=%fused_computation.73 | loop fusion | bytes 1048576 | tf_op jit(solution)/shard_map/slice | solution.py:159
  1.7 3.0 %collective-permute-start.1 = (bf16[128,1024]{1,0:T(8,128)(2,1)S(1)}, bf16[128,1024]{1,0:T(8,128)(2,1)S(1)}, u32[]{:S(2)}, u32[]{:S(2)}) collective-permute-start(bf16[128,1024]{1,0:T(8,128)(2,1)S(1)} %get-tuple-element.76), channel_id=1, source_target_pairs={{0,4},{2,6},{4,8},{6,10},{8,12},{10,14},{12,16},{14,18},{16,20},{1... | collective-permute-start | bytes 786440 | tf_op jit(solution)/shard_map/ppermute | solution.py:146
  4.7 3.9 %fusion.38 = (f32[256]{0:T(256)S(1)}, f32[256,2048]{1,0:T(8,128)S(1)}) fusion(bf16[256,1024]{1,0:T(8,128)(2,1)} %param.3, bf16[1,2048,1024]{2,1,0:T(8,128)(2,1)} %param.4), kind=kOutput, calls=%fused_computation.74 | convolution fusion | flops 1074790144 | bytes 6816768 | tf_op jit(solution)/shard_map/dot_general | solution.py:20
  8.6 0.4 fusion
  9.1 1.3 %convolution_divide_fusion = f32[256,1024]{1,0:T(8,128)S(1)} fusion(f32[256,2048]{1,0:T(8,128)S(1)} %get-tuple-element.93, f32[256]{0:T(256)S(1)} %get-tuple-element.92, f32[256]{0:T(256)S(1)} %fusion, bf16[1,2048,1024]{2,1,0:T(8,128)(2,1)S(1)} %copy-done.1), kind=kOutput, calls=%fused_computation.4 | convolution fusion | flops 1075052544 | bytes 7342080 | tf_op jit(solution)/shard_map/dot_general | solution.py:26
  10.4 3.7 %collective-permute-done.1.refs_0_ = bf16[128,1024]{1,0:T(8,128)(2,1)S(1)} collective-permute-done((bf16[128,1024]{1,0:T(8,128)(2,1)S(1)}, bf16[128,1024]{1,0:T(8,128)(2,1)S(1)}, u32[]{:S(2)}, u32[]{:S(2)}) %collective-permute-start.1) | collective-permute-done | bytes 262176 | tf_op jit(solution)/shard_map/ppermute | solution.py:146
  14.1 0.5 collective-permute-start
  14.6 1.0 %collective-permute-done.2.refs_1_ = bf16[128,1024]{1,0:T(8,128)(2,1)S(1)} collective-permute-done((bf16[128,1024]{1,0:T(8,128)(2,1)S(1)}, bf16[128,1024]{1,0:T(8,128)(2,1)S(1)}, u32[]{:S(2)}, u32[]{:S(2)}) %collective-permute-start.2) | collective-permute-done | bytes 262176 | tf_op jit(solution)/shard_map/ppermute | solution.py:146
  15.6 2.7 %parts.3 = (f32[128,1024]{1,0:T(8,128)S(1)}, f32[8,128]{1,0:T(8,128)S(1)}, f32[128,1024]{1,0:T(8,128)S(1)}, f32[8,128]{1,0:T(8,128)S(1)}) custom-call(bf16[128,1024]{1,0:T(8,128)(2,1)S(1)} %collective-permute-done.1.refs_0_, bf16[128,1024]{1,0:T(8,128)(2,1)S(1)} %collective-permute-done.2.refs_1_, bf16[2048,1024]{1,0:T(8,128)(2,1)S(1)} %bitcast.147, ...), custom_call_target="tpu_custom_call" | custom-call | tf_op jit(solution)/shard_map/parts/pallas_call | solution.py:77
  18.6 0.4 collective-permute-start.3
  19.0 1.0 %collective-permute-done.3 = f32[128]{0:T(128)S(1)} collective-permute-done((f32[128]{0:T(128)S(1)}, f32[128]{0:T(128)S(1)}, u32[]{:S(2)}, u32[]{:S(2)}) %collective-permute-start.3) | collective-permute-done | bytes 544 | tf_op jit(solution)/shard_map/ppermute | solution.py:146
  20.2 4.3 %collective-permute-done.refs_0_ = bf16[256,1024]{1,0:T(8,128)(2,1)S(1)} collective-permute-done((bf16[256,1024]{1,0:T(8,128)(2,1)S(1)}, bf16[256,1024]{1,0:T(8,128)(2,1)S(1)}, u32[]{:S(2)}, u32[]{:S(2)}) %collective-permute-start) | collective-permute-done | bytes 524320 | tf_op jit(solution)/shard_map/ppermute | solution.py:146
  24.5 2.7 %parts.4 = (f32[256,1024]{1,0:T(8,128)S(1)}, f32[8,256]{1,0:T(8,128)S(1)}) custom-call(bf16[256,1024]{1,0:T(8,128)(2,1)S(1)} %collective-permute-done.refs_0_, bf16[2048,1024]{1,0:T(8,128)(2,1)S(1)} %bitcast.148, bf16[2048,1024]{1,0:T(8,128)(2,1)S(1)} %bitcast.151), custom_call_target="tpu_custom_call" | custom-call | tf_op jit(solution)/shard_map/parts/pallas_call | solution.py:77
  27.3 2.7 %collective-permute-done.6.refs_0_ = bf16[128,1024]{1,0:T(8,128)(2,1)S(1)} collective-permute-done((bf16[128,1024]{1,0:T(8,128)(2,1)S(1)}, bf16[128,1024]{1,0:T(8,128)(2,1)S(1)}, u32[]{:S(2)}, u32[]{:S(2)}) %collective-permute-start.6) | collective-permute-done | bytes 262176 | tf_op jit(solution)/shard_map/ppermute | solution.py:146
  30.1 0.5 collective-permute-start.14
  30.6 0.9 %collective-permute-done.7.refs_1_ = bf16[128,1024]{1,0:T(8,128)(2,1)S(1)} collective-permute-done((bf16[128,1024]{1,0:T(8,128)(2,1)S(1)}, bf16[128,1024]{1,0:T(8,128)(2,1)S(1)}, u32[]{:S(2)}, u32[]{:S(2)}) %collective-permute-start.7) | collective-permute-done | bytes 262176 | tf_op jit(solution)/shard_map/ppermute | solution.py:146
  31.6 2.7 %parts.5 = (f32[128,1024]{1,0:T(8,128)S(1)}, f32[8,128]{1,0:T(8,128)S(1)}, f32[128,1024]{1,0:T(8,128)S(1)}, f32[8,128]{1,0:T(8,128)S(1)}) custom-call(bf16[128,1024]{1,0:T(8,128)(2,1)S(1)} %collective-permute-done.6.refs_0_, bf16[128,1024]{1,0:T(8,128)(2,1)S(1)} %collective-permute-done.7.refs_1_, bf16[2048,1024]{1,0:T(8,128)(2,1)S(1)} %bitcast.149, ...), custom_call_target="tpu_custom_call" | custom-call | tf_op jit(solution)/shard_map/parts/pallas_call | solution.py:77
  34.6 0.4 collective-permute-start.8
  35.1 0.8 %collective-permute-done.8 = f32[128]{0:T(128)S(1)} collective-permute-done((f32[128]{0:T(128)S(1)}, f32[128]{0:T(128)S(1)}, u32[]{:S(2)}, u32[]{:S(2)}) %collective-permute-start.8) | collective-permute-done | bytes 544 | tf_op jit(solution)/shard_map/ppermute | solution.py:146
  35.9 0.6 collective-permute-start.13
  36.8 1.4 %collective-permute-start.10 = (f16[128,1024]{1,0:T(8,128)(2,1)S(1)}, f16[128,1024]{1,0:T(8,128)(2,1)S(1)}, u32[]{:S(2)}, u32[]{:S(2)}) collective-permute-start(f16[128,1024]{1,0:T(8,128)(2,1)S(1)} %divide_convert_fusion.2), channel_id=1, source_target_pairs={{4,0},{6,2},{8,4},{10,6},{12,8},{14,10},{16,12},{18,14},{20,16},{2... | collective-permute-start | bytes 786440 | tf_op jit(solution)/shard_map/ppermute | solution.py:146
  38.2 6.9 %collective-permute-done.13 = f32[128]{0:T(128)S(1)} collective-permute-done((f32[128]{0:T(128)S(1)}, f32[128]{0:T(128)S(1)}, u32[]{:S(2)}, u32[]{:S(2)}) %collective-permute-start.13) | collective-permute-done | bytes 544 | tf_op jit(solution)/shard_map/ppermute | solution.py:146
  45.1 5.1 %collective-permute-start.11 = (f32[128]{0:T(128)S(1)}, f32[128]{0:T(128)S(1)}, u32[]{:S(2)}, u32[]{:S(2)}) collective-permute-start(f32[128]{0:T(128)S(1)} %get-tuple-element.48), channel_id=1, source_target_pairs={{4,0},{6,2},{8,4},{10,6},{12,8},{14,10},{16,12},{18,14},{20,16},{2... | collective-permute-start | bytes 1544 | tf_op jit(solution)/shard_map/ppermute | solution.py:146
  50.5 1.6 %collective-permute-start.17 = (f16[128,1024]{1,0:T(8,128)(2,1)S(1)}, f16[128,1024]{1,0:T(8,128)(2,1)S(1)}, u32[]{:S(2)}, u32[]{:S(2)}) collective-permute-start(f16[128,1024]{1,0:T(8,128)(2,1)S(1)} %fusion.11), channel_id=1, source_target_pairs={{0,1},{1,0},{2,3},{3,2},{4,5},{5,4},{6,7},{7,6},{8,9},{9,8},{10,11... | collective-permute-start | bytes 786440 | tf_op jit(solution)/shard_map/ppermute | solution.py:146
  52.0 0.5 collective-permute-start.18
  52.6 0.2 fusion.10
  52.9 1.6 %collective-permute-start.16 = (f16[128,1024]{1,0:T(8,128)(2,1)S(1)}, f16[128,1024]{1,0:T(8,128)(2,1)S(1)}, u32[]{:S(2)}, u32[]{:S(2)}) collective-permute-start(f16[128,1024]{1,0:T(8,128)(2,1)S(1)} %fusion.10), channel_id=1, source_target_pairs={{0,1},{1,0},{2,3},{3,2},{4,5},{5,4},{6,7},{7,6},{8,9},{9,8},{10,11... | collective-permute-start | bytes 786440 | tf_op jit(solution)/shard_map/ppermute | solution.py:146
  54.4 2.6 %collective-permute-done.18 = f32[128]{0:T(128)S(1)} collective-permute-done((f32[128]{0:T(128)S(1)}, f32[128]{0:T(128)S(1)}, u32[]{:S(2)}, u32[]{:S(2)}) %collective-permute-start.18) | collective-permute-done | bytes 544 | tf_op jit(solution)/shard_map/ppermute | solution.py:146
  57.0 1.6 %collective-permute-start.15 = (f32[128]{0:T(128)S(1)}, f32[128]{0:T(128)S(1)}, u32[]{:S(2)}, u32[]{:S(2)}) collective-permute-start(f32[128]{0:T(128)S(1)} %bitcast.160), channel_id=1, source_target_pairs={{0,1},{1,0},{2,3},{3,2},{4,5},{5,4},{6,7},{7,6},{8,9},{9,8},{10,11... | collective-permute-start | bytes 1544 | tf_op jit(solution)/shard_map/ppermute | solution.py:146
  58.8 0.7 %store.2 = (bf16[256,1024]{1,0:T(8,128)(2,1)}, f32[1,256]{1,0:T(1,128)}) custom-call(bf16[128,1024]{1,0:T(8,128)(2,1)S(1)} %divide_convert_fusion.attributed_ref, f32[1,128]{1,0:T(1,128)S(1)} %get-tuple-element.78.level_ref), custom_call_target="tpu_custom_call" | custom-call | tf_op jit(solution)/shard_map/store/pallas_call | solution.py:105
  59.5 1.2 %collective-permute-done.15 = f32[128]{0:T(128)S(1)} collective-permute-done((f32[128]{0:T(128)S(1)}, f32[128]{0:T(128)S(1)}, u32[]{:S(2)}, u32[]{:S(2)}) %collective-permute-start.15) | collective-permute-done | bytes 544 | tf_op jit(solution)/shard_map/ppermute | solution.py:146
  60.9 0.7 %store.3 = (bf16[256,1024]{1,0:T(8,128)(2,1)}, f32[1,256]{1,0:T(1,128)}) custom-call(bf16[128,1024]{1,0:T(8,128)(2,1)S(1)} %divide_convert_fusion.1.attributed_ref, f32[1,128]{1,0:T(1,128)S(1)} %get-tuple-element.82.level_ref, bf16[256,1024]{1,0:T(8,128)(2,1)} %get-tuple-element.58.refs_0_, ...), custom_call_target="tpu_custom_call", output_to_operand_aliasing={{0}: (2, {}), {1}: (3, {})} | custom-call | tf_op jit(solution)/shard_map/store/pallas_call | solution.py:105
  (42 shorter events, 1.9 us)
Async XLA Ops:
  1.7 12.4 %collective-permute-start.1 = (bf16[128,1024]{1,0:T(8,128)(2,1)S(1)}, bf16[128,1024]{1,0:T(8,128)(2,1)S(1)}, u32[]{:S(2)}, u32[]{:S(2)}) collective-permute-start(bf16[128,1024]{1,0:T(8,128)(2,1)S(1)} %get-tuple-element.76), channel_id=1, source_target_pairs={{0,4},{2,6},{4,8},{6,10},{8,12},{10,14},{12,16},{14,18},{16,20},{1... | collective-permute-start | bytes 786440 | tf_op jit(solution)/shard_map/ppermute | solution.py:146
  4.7 4.3 %copy-start.1 = (bf16[1,2048,1024]{2,1,0:T(8,128)(2,1)S(1)}, bf16[1,2048,1024]{2,1,0:T(8,128)(2,1)}, u32[]{:S(2)}) copy-start(bf16[1,2048,1024]{2,1,0:T(8,128)(2,1)} %param.5) | copy-start | bytes 12582916
  9.1 5.0 %copy-start.2 = (bf16[256,1024]{1,0:T(8,128)(2,1)S(1)}, bf16[256,1024]{1,0:T(8,128)(2,1)}, u32[]{:S(2)}) copy-start(bf16[256,1024]{1,0:T(8,128)(2,1)} %param.3) | copy-start | bytes 1572868
  9.1 6.6 %copy-start = (bf16[1,2048,1024]{2,1,0:T(8,128)(2,1)S(1)}, bf16[1,2048,1024]{2,1,0:T(8,128)(2,1)}, u32[]{:S(2)}) copy-start(bf16[1,2048,1024]{2,1,0:T(8,128)(2,1)} %param.4) | copy-start | bytes 12582916
  14.1 1.5 %collective-permute-start.2 = (bf16[128,1024]{1,0:T(8,128)(2,1)S(1)}, bf16[128,1024]{1,0:T(8,128)(2,1)S(1)}, u32[]{:S(2)}, u32[]{:S(2)}) collective-permute-start(bf16[128,1024]{1,0:T(8,128)(2,1)S(1)} %collective-permute-done.1.refs_0_), channel_id=1, source_target_pairs={{0,2},{2,0},{4,6},{6,4},{8,10},{10,8},{12,14},{14,12},{16,18},{18,... | collective-permute-start | bytes 786440 | tf_op jit(solution)/shard_map/ppermute | solution.py:146
  14.1 10.4 %collective-permute-start = (bf16[256,1024]{1,0:T(8,128)(2,1)S(1)}, bf16[256,1024]{1,0:T(8,128)(2,1)S(1)}, u32[]{:S(2)}, u32[]{:S(2)}) collective-permute-start(bf16[256,1024]{1,0:T(8,128)(2,1)S(1)} %copy-done.2), channel_id=1, source_target_pairs={{0,2},{2,8},{4,6},{6,12},{8,10},{10,16},{12,14},{14,20},{16,18},{1... | collective-permute-start | bytes 1572872 | tf_op jit(solution)/shard_map/ppermute | solution.py:146
  18.4 1.6 %collective-permute-start.4 = (f16[128,1024]{1,0:T(8,128)(2,1)S(1)}, f16[128,1024]{1,0:T(8,128)(2,1)S(1)}, u32[]{:S(2)}, u32[]{:S(2)}) collective-permute-start(f16[128,1024]{1,0:T(8,128)(2,1)S(1)} %convert_element_type.61), channel_id=1, source_target_pairs={{0,2},{2,0},{4,6},{6,4},{8,10},{10,8},{12,14},{14,12},{16,18},{18,... | collective-permute-start | bytes 786440 | tf_op jit(solution)/shard_map/ppermute | solution.py:146
  18.6 1.4 %collective-permute-start.3 = (f32[128]{0:T(128)S(1)}, f32[128]{0:T(128)S(1)}, u32[]{:S(2)}, u32[]{:S(2)}) collective-permute-start(f32[128]{0:T(128)S(1)} %slice_bitcast_fusion.1), channel_id=1, source_target_pairs={{0,2},{2,0},{4,6},{6,4},{8,10},{10,8},{12,14},{14,12},{16,18},{18,... | collective-permute-start | bytes 1544 | tf_op jit(solution)/shard_map/ppermute | solution.py:146
  19.0 11.0 %collective-permute-start.6 = (bf16[128,1024]{1,0:T(8,128)(2,1)S(1)}, bf16[128,1024]{1,0:T(8,128)(2,1)S(1)}, u32[]{:S(2)}, u32[]{:S(2)}) collective-permute-start(bf16[128,1024]{1,0:T(8,128)(2,1)S(1)} %get-tuple-element.77), channel_id=1, source_target_pairs={{0,4},{2,6},{4,8},{6,10},{8,12},{10,14},{12,16},{14,18},{16,20},{1... | collective-permute-start | bytes 786440 | tf_op jit(solution)/shard_map/ppermute | solution.py:146
  30.0 1.5 %collective-permute-start.7 = (bf16[128,1024]{1,0:T(8,128)(2,1)S(1)}, bf16[128,1024]{1,0:T(8,128)(2,1)S(1)}, u32[]{:S(2)}, u32[]{:S(2)}) collective-permute-start(bf16[128,1024]{1,0:T(8,128)(2,1)S(1)} %collective-permute-done.6.refs_0_), channel_id=1, source_target_pairs={{0,2},{2,0},{4,6},{6,4},{8,10},{10,8},{12,14},{14,12},{16,18},{18,... | collective-permute-start | bytes 786440 | tf_op jit(solution)/shard_map/ppermute | solution.py:146
  30.0 15.0 %collective-permute-start.12 = (f16[128,1024]{1,0:T(8,128)(2,1)S(1)}, f16[128,1024]{1,0:T(8,128)(2,1)S(1)}, u32[]{:S(2)}, u32[]{:S(2)}) collective-permute-start(f16[128,1024]{1,0:T(8,128)(2,1)S(1)} %divide_convert_fusion.3), channel_id=1, source_target_pairs={{4,0},{6,2},{8,4},{10,6},{12,8},{14,10},{16,12},{18,14},{20,16},{2... | collective-permute-start | bytes 786440 | tf_op jit(solution)/shard_map/ppermute | solution.py:146
  30.1 20.1 %collective-permute-start.14 = (f16[256,1024]{1,0:T(8,128)(2,1)S(1)}, f16[256,1024]{1,0:T(8,128)(2,1)S(1)}, u32[]{:S(2)}, u32[]{:S(2)}) collective-permute-start(f16[256,1024]{1,0:T(8,128)(2,1)S(1)} %convert_element_type.64), channel_id=1, source_target_pairs={{2,0},{8,2},{6,4},{12,6},{10,8},{16,10},{14,12},{20,14},{18,16},{2... | collective-permute-start | bytes 1572872 | tf_op jit(solution)/shard_map/ppermute | solution.py:146
  34.3 2.2 %collective-permute-start.9 = (f16[128,1024]{1,0:T(8,128)(2,1)S(1)}, f16[128,1024]{1,0:T(8,128)(2,1)S(1)}, u32[]{:S(2)}, u32[]{:S(2)}) collective-permute-start(f16[128,1024]{1,0:T(8,128)(2,1)S(1)} %convert_element_type.65), channel_id=1, source_target_pairs={{0,2},{2,0},{4,6},{6,4},{8,10},{10,8},{12,14},{14,12},{16,18},{18,... | collective-permute-start | bytes 786440 | tf_op jit(solution)/shard_map/ppermute | solution.py:146
  34.6 1.4 %collective-permute-start.8 = (f32[128]{0:T(128)S(1)}, f32[128]{0:T(128)S(1)}, u32[]{:S(2)}, u32[]{:S(2)}) collective-permute-start(f32[128]{0:T(128)S(1)} %slice_bitcast_fusion), channel_id=1, source_target_pairs={{0,2},{2,0},{4,6},{6,4},{8,10},{10,8},{12,14},{14,12},{16,18},{18,... | collective-permute-start | bytes 1544 | tf_op jit(solution)/shard_map/ppermute | solution.py:146
  34.9 15.3 %collective-permute-start.5 = (f32[256]{0:T(256)S(1)}, f32[256]{0:T(256)S(1)}, u32[]{:S(2)}, u32[]{:S(2)}) collective-permute-start(f32[256]{0:T(256)S(1)} %bitcast.162), channel_id=1, source_target_pairs={{2,0},{8,2},{6,4},{12,6},{10,8},{16,10},{14,12},{20,14},{18,16},{2... | collective-permute-start | bytes 3080 | tf_op jit(solution)/shard_map/ppermute | solution.py:146
  35.9 9.1 %collective-permute-start.13 = (f32[128]{0:T(128)S(1)}, f32[128]{0:T(128)S(1)}, u32[]{:S(2)}, u32[]{:S(2)}) collective-permute-start(f32[128]{0:T(128)S(1)} %get-tuple-element.49), channel_id=1, source_target_pairs={{4,0},{6,2},{8,4},{10,6},{12,8},{14,10},{16,12},{18,14},{20,16},{2... | collective-permute-start | bytes 1544 | tf_op jit(solution)/shard_map/ppermute | solution.py:146
  36.8 15.8 %collective-permute-start.10 = (f16[128,1024]{1,0:T(8,128)(2,1)S(1)}, f16[128,1024]{1,0:T(8,128)(2,1)S(1)}, u32[]{:S(2)}, u32[]{:S(2)}) collective-permute-start(f16[128,1024]{1,0:T(8,128)(2,1)S(1)} %divide_convert_fusion.2), channel_id=1, source_target_pairs={{4,0},{6,2},{8,4},{10,6},{12,8},{14,10},{16,12},{18,14},{20,16},{2... | collective-permute-start | bytes 786440 | tf_op jit(solution)/shard_map/ppermute | solution.py:146
  45.1 7.5 %collective-permute-start.11 = (f32[128]{0:T(128)S(1)}, f32[128]{0:T(128)S(1)}, u32[]{:S(2)}, u32[]{:S(2)}) collective-permute-start(f32[128]{0:T(128)S(1)} %get-tuple-element.48), channel_id=1, source_target_pairs={{4,0},{6,2},{8,4},{10,6},{12,8},{14,10},{16,12},{18,14},{20,16},{2... | collective-permute-start | bytes 1544 | tf_op jit(solution)/shard_map/ppermute | solution.py:146
  50.5 6.5 %collective-permute-start.17 = (f16[128,1024]{1,0:T(8,128)(2,1)S(1)}, f16[128,1024]{1,0:T(8,128)(2,1)S(1)}, u32[]{:S(2)}, u32[]{:S(2)}) collective-permute-start(f16[128,1024]{1,0:T(8,128)(2,1)S(1)} %fusion.11), channel_id=1, source_target_pairs={{0,1},{1,0},{2,3},{3,2},{4,5},{5,4},{6,7},{7,6},{8,9},{9,8},{10,11... | collective-permute-start | bytes 786440 | tf_op jit(solution)/shard_map/ppermute | solution.py:146
  52.0 5.0 %collective-permute-start.18 = (f32[128]{0:T(128)S(1)}, f32[128]{0:T(128)S(1)}, u32[]{:S(2)}, u32[]{:S(2)}) collective-permute-start(f32[128]{0:T(128)S(1)} %bitcast.159), channel_id=1, source_target_pairs={{0,1},{1,0},{2,3},{3,2},{4,5},{5,4},{6,7},{7,6},{8,9},{9,8},{10,11... | collective-permute-start | bytes 1544 | tf_op jit(solution)/shard_map/ppermute | solution.py:146
  52.9 7.8 %collective-permute-start.16 = (f16[128,1024]{1,0:T(8,128)(2,1)S(1)}, f16[128,1024]{1,0:T(8,128)(2,1)S(1)}, u32[]{:S(2)}, u32[]{:S(2)}) collective-permute-start(f16[128,1024]{1,0:T(8,128)(2,1)S(1)} %fusion.10), channel_id=1, source_target_pairs={{0,1},{1,0},{2,3},{3,2},{4,5},{5,4},{6,7},{7,6},{8,9},{9,8},{10,11... | collective-permute-start | bytes 786440 | tf_op jit(solution)/shard_map/ppermute | solution.py:146
  57.0 3.6 %collective-permute-start.15 = (f32[128]{0:T(128)S(1)}, f32[128]{0:T(128)S(1)}, u32[]{:S(2)}, u32[]{:S(2)}) collective-permute-start(f32[128]{0:T(128)S(1)} %bitcast.160), channel_id=1, source_target_pairs={{0,1},{1,0},{2,3},{3,2},{4,5},{5,4},{6,7},{7,6},{8,9},{9,8},{10,11... | collective-permute-start | bytes 1544 | tf_op jit(solution)/shard_map/ppermute | solution.py:146

commit v6 on v5

--- a/solution.py
+++ b/solution.py
@@ -14,6 +14,11 @@
 
 def after(value, *earlier):
     return lax.optimization_barrier((value, earlier))[0]
+
+
+def power_of(mean):
+    peak = jnp.max(jnp.abs(mean), axis=1, keepdims=True)
+    return jnp.floor(jnp.log2(jnp.maximum(peak, 2.0**-100))) - 13.0
 
 
 def plain_part(block_queries, keys, values):
@@ -24,7 +29,8 @@
     weights = jnp.exp(scores - top)
     total = jnp.sum(weights, axis=1, keepdims=True)
     weighted = jnp.dot(weights.astype(jnp.bfloat16), values, preferred_element_type=jnp.float32)
-    return weighted / total, top + jnp.log(total)
+    mean = weighted / total
+    return mean, top + jnp.log(total), power_of(mean)
 
 
 def parts_kernel(*refs):
@@ -57,12 +63,16 @@
             weights.astype(jnp.bfloat16), values_ref[at, :], preferred_element_type=jnp.float32
         )
     mean = weighted / total
-    level = jnp.transpose(jnp.broadcast_to(top + jnp.log(total), (block.shape[0], 128)))
+    power = power_of(mean)
+    mean = mean * jnp.exp2(-power)
+    across = lambda column: jnp.transpose(jnp.broadcast_to(column, (block.shape[0], 128)))[0:8]
+    level, power = across(top + jnp.log(total)), across(power)
+    stats = jnp.where(lax.broadcasted_iota(jnp.int32, level.shape, 0) == 0, level, power)
     row = 0
     for k, q in enumerate(queries):
         rows = slice(row, row + q.shape[0])
         outs[2 * k][...] = mean[rows]
-        outs[2 * k + 1][...] = level[0:8, rows]
+        outs[2 * k + 1][...] = stats[:, rows]
         row = rows.stop
 
 
@@ -83,7 +93,7 @@
         compiler_params=pltpu.CompilerParams(vmem_limit_bytes=GRANT),
         name="parts",
     )(*queries, keys, values)
-    return [(out[2 * k], out[2 * k + 1][0][:, None]) for k in range(len(queries))]
+    return [(out[2 * k], out[2 * k + 1]) for k in range(len(queries))]
 
 
 def store(outs, shape, attributed, level, at):
@@ -117,21 +127,27 @@
     )(attributed, level, *outs)
 
 
-def joined(all_parts):
-    top = all_parts[0][1]
-    for _, level in all_parts[1:]:
-        top = jnp.maximum(top, level)
+def joined(all_parts, own=None):
+    everything = [(mean, stats[0][:, None], stats[1][:, None]) for mean, stats in all_parts]
+    everything += [own] if own else []
+    top = power = None
+    for _, level, part_power in everything:
+        top = level if top is None else jnp.maximum(top, level)
+        power = part_power if power is None else jnp.maximum(power, part_power)
     total = 0.0
     mean = 0.0
-    for value, level in all_parts:
+    for k, (value, level, part_power) in enumerate(everything):
         share = jnp.exp(level - top)
         total = total + share
-        mean = mean + value.astype(jnp.float32) * share
-    return mean / total, top + jnp.log(total)
-
-
-def packed(part):
-    return part[0].astype(jnp.float16), part[1]
+        scale = part_power if k < len(all_parts) else 0.0
+        mean = mean + value.astype(jnp.float32) * (share * jnp.exp2(scale - power))
+    return mean / total, top + jnp.log(total), power
+
+
+def packed(mean, level, power):
+    at = lax.broadcasted_iota(jnp.int32, (2, mean.shape[0]), 0)
+    stats = jnp.where(at == 0, level[:, 0][None], power[:, 0][None])
+    return mean.astype(jnp.float16), stats
 
 
 def program(queries, corpus, attributions):
@@ -146,9 +162,8 @@
         return lax.ppermute(value, axis, pairs)
 
     def move_part(part, pairs, axis="blk"):
-        mean, level = part
-        mean_there = move(mean, pairs, axis)
-        return mean_there, move(after(level[:, 0], mean), pairs, axis)[:, None]
+        mean, stats = part
+        return move(mean, pairs, axis), move(after(stats, mean), pairs, axis)
 
     def edges(c):
         rows = queries.shape[0]
@@ -169,27 +184,32 @@
     def window(near):
         far = move(near, pair)
         near_part, far_part = parts([near, far], keys_1, values_1)
-        far_back = move_part(packed(far_part), pair)
-        mine = packed(joined([near_part, far_back]))
+        far_back = move_part((far_part[0].astype(jnp.float16), far_part[1]), pair)
+        mine = packed(*joined([near_part, far_back]))
         return mine, move_part(mine, two_back)
 
-    def exchange(all_parts):
-        mine = packed(joined(all_parts))
+    def cut_part(part, c):
+        lo, hi = edges(c)
+        return part[0][lo:hi], part[1][:, lo:hi]
+
+    def exchange(all_parts, own):
+        mine = packed(*joined(all_parts, own))
         return mine, move_part(mine, [(0, 1), (1, 0)], "rep")
 
     def finish(outs, mine, theirs, c):
-        attributed, log_total = joined([mine, theirs])
+        mean, log_total, power = joined([mine, theirs])
+        attributed = mean * jnp.exp2(power)
         at = edges(c)[0]
         shape = (queries.shape[0], attributed.shape[1])
         return store(outs, shape, attributed.astype(jnp.bfloat16), log_total[:, 0][None], at)
 
     mine_1, back_1 = window(after(near_1, own))
     (other_part,) = parts([after(other, mine_1)], keys_1, values_1)
-    other_part = packed(other_part)
+    other_part = other_part[0].astype(jnp.float16), other_part[1]
     other_back = move_part(other_part, fourth_back)
     mine_2, back_2 = window(after(near_2, other_part))
-    own_1, theirs_1 = exchange([cut(own, 0), cut(other_back, 0), after(back_1, mine_2)])
-    own_2, theirs_2 = exchange([cut(own, 1), cut(other_back, 1), after(back_2, own_1)])
+    own_1, theirs_1 = exchange([cut_part(other_back, 0), after(back_1, mine_2)], cut(own, 0))
+    own_2, theirs_2 = exchange([cut_part(other_back, 1), after(back_2, own_1)], cut(own, 1))
     outs = ()
     outs = finish(outs, own_1, after(theirs_1, own_2), 0)
     outs = finish(outs, own_2, theirs_2, 1)

time: 61.8 us -> 71.1 us (1.15)
  waiting for transfers between devices: 25.1 us -> 31.9 us
  starting transfers between devices: 17.9 us -> 19.4 us
    ppermute x19, waiting for transfers between devices: 25.1 us -> 31.9 us  [move(): return lax.ppermute(value, axis, pairs)]
    ppermute x19, starting transfers between devices: 17.9 us -> 19.4 us  [move(): return lax.ppermute(value, axis, pairs)]
  transfers between devices with their start and end apart: 19 -> 19, of which waited for: 10 -> 10; matrix products, arithmetic and copies ran while one was open for 11% -> 10% of each run, Pallas kernels for 14% -> 9%
where the time goes in v6:
time: 71.1 us; the launch traced here: 70.9 us
  waiting for transfers between devices  31.9 us (45%)
  starting transfers between devices  19.4 us (27%)
  Pallas kernels  10 us (14%)
  matrix products  5.29 us (7%)
  other arithmetic  2.37 us (3%)
  local copies, waits for them, and re-layouts  1.08 us (2%)
  between operations  0.84 us (1%)
    ppermute x19, waiting for transfers between devices, move(): return lax.ppermute(value, axis, pairs)  31.9 us
    ppermute x19, starting transfers between devices, move(): return lax.ppermute(value, axis, pairs)  19.4 us
    pallas_call x3, Pallas kernels, parts(): pl.pallas_call(parts_kernel, out_shape=tuple(shapes), in_specs=[vmem] * (...  8.56 us
    dot_general x1, matrix products, plain_part(): jnp.dot(block_queries, keys.T, preferred_element_type=jnp.float32)  3.86 us
    pallas_call x2, Pallas kernels, store(): pl.pallas_call(kernel, out_shape=(jax.ShapeDtypeStruct(shape, attributed....  1.45 us
    dot_general x1, matrix products, plain_part(): jnp.dot(weights.astype(jnp.bfloat16), values, preferred_element_type=jnp....  1.43 us
  transfers between devices with their start and end apart: 19, of which 10 were waited for; matrix products, arithmetic and copies ran while one was open for 10% of the time, Pallas kernels for 9%

profile of v6, /device:TPU:0, one launch (start us, length us, event | category | flops | bytes accessed | tf_op | source)
XLA Modules:
  0.0 70.9 jit_solution(180578940101476428)
XLA Ops:
  0.6 1.1 %fusion.56 = (bf16[128,1024]{1,0:T(8,128)(2,1)S(1)}, bf16[128,1024]{1,0:T(8,128)(2,1)S(1)}) fusion(bf16[256,1024]{1,0:T(8,128)(2,1)} %param.3), kind=kLoop, calls=%fused_computation.134 | loop fusion | bytes 1048576 | tf_op jit(solution)/shard_map/slice | solution.py:174
  1.7 3.0 %collective-permute-start.1 = (bf16[128,1024]{1,0:T(8,128)(2,1)S(1)}, bf16[128,1024]{1,0:T(8,128)(2,1)S(1)}, u32[]{:S(2)}, u32[]{:S(2)}) collective-permute-start(bf16[128,1024]{1,0:T(8,128)(2,1)S(1)} %get-tuple-element.72), channel_id=1, source_target_pairs={{0,4},{2,6},{4,8},{6,10},{8,12},{10,14},{12,16},{14,18},{16,20},{1... | collective-permute-start | bytes 786440 | tf_op jit(solution)/shard_map/ppermute | solution.py:162
  4.7 3.9 %fusion.57 = (f32[256]{0:T(256)S(1)}, f32[256,2048]{1,0:T(8,128)S(1)}) fusion(bf16[256,1024]{1,0:T(8,128)(2,1)} %param.3, bf16[1,2048,1024]{2,1,0:T(8,128)(2,1)} %param.4), kind=kOutput, calls=%fused_computation.135 | convolution fusion | flops 1074790144 | bytes 6816768 | tf_op jit(solution)/shard_map/dot_general | solution.py:25
  8.6 0.4 fusion
  9.1 1.4 %abs_reduce_fusion = (f32[256]{0:T(256)S(1)}, f32[256,1024]{1,0:T(8,128)S(1)}) fusion(f32[256]{0:T(256)S(1)} %fusion, bf16[1,2048,1024]{2,1,0:T(8,128)(2,1)S(1)} %copy-done.1, f32[256,2048]{1,0:T(8,128)S(1)} %get-tuple-element.97, f32[256]{0:T(256)S(1)} %get-tuple-element.96), kind=kOutput, calls=%fused_computation.5 | convolution fusion | flops 1075576576 | bytes 7343104 | tf_op jit(solution)/shard_map/dot_general | solution.py:31
  10.5 3.6 %collective-permute-done.1.refs_0_ = bf16[128,1024]{1,0:T(8,128)(2,1)S(1)} collective-permute-done((bf16[128,1024]{1,0:T(8,128)(2,1)S(1)}, bf16[128,1024]{1,0:T(8,128)(2,1)S(1)}, u32[]{:S(2)}, u32[]{:S(2)}) %collective-permute-start.1) | collective-permute-done | bytes 262176 | tf_op jit(solution)/shard_map/ppermute | solution.py:162
  14.1 0.5 collective-permute-start
  14.6 1.0 %collective-permute-done.2.refs_1_ = bf16[128,1024]{1,0:T(8,128)(2,1)S(1)} collective-permute-done((bf16[128,1024]{1,0:T(8,128)(2,1)S(1)}, bf16[128,1024]{1,0:T(8,128)(2,1)S(1)}, u32[]{:S(2)}, u32[]{:S(2)}) %collective-permute-start.2) | collective-permute-done | bytes 262176 | tf_op jit(solution)/shard_map/ppermute | solution.py:162
  15.6 2.9 %parts.3 = (f32[128,1024]{1,0:T(8,128)S(1)}, f32[8,128]{1,0:T(8,128)S(1)}, f32[128,1024]{1,0:T(8,128)S(1)}, f32[8,128]{1,0:T(8,128)S(1)}) custom-call(bf16[128,1024]{1,0:T(8,128)(2,1)S(1)} %collective-permute-done.1.refs_0_, bf16[128,1024]{1,0:T(8,128)(2,1)S(1)} %collective-permute-done.2.refs_1_, bf16[2048,1024]{1,0:T(8,128)(2,1)S(1)} %bitcast.336, ...), custom_call_target="tpu_custom_call" | custom-call | tf_op jit(solution)/shard_map/parts/pallas_call | solution.py:87
  19.1 0.7 collective-permute-done.3
  19.9 0.4 collective-permute-done.4
  20.5 4.0 %collective-permute-done.refs_0_ = bf16[256,1024]{1,0:T(8,128)(2,1)S(1)} collective-permute-done((bf16[256,1024]{1,0:T(8,128)(2,1)S(1)}, bf16[256,1024]{1,0:T(8,128)(2,1)S(1)}, u32[]{:S(2)}, u32[]{:S(2)}) %collective-permute-start) | collective-permute-done | bytes 524320 | tf_op jit(solution)/shard_map/ppermute | solution.py:162
  24.5 2.9 %parts.4 = (f32[256,1024]{1,0:T(8,128)S(1)}, f32[8,256]{1,0:T(8,128)S(1)}) custom-call(bf16[256,1024]{1,0:T(8,128)(2,1)S(1)} %collective-permute-done.refs_0_, bf16[2048,1024]{1,0:T(8,128)(2,1)S(1)} %bitcast.337, bf16[2048,1024]{1,0:T(8,128)(2,1)S(1)} %bitcast.340), custom_call_target="tpu_custom_call" | custom-call | tf_op jit(solution)/shard_map/parts/pallas_call | solution.py:87
  27.4 0.8 %collective-permute-start.8 = (bf16[128,1024]{1,0:T(8,128)(2,1)S(1)}, bf16[128,1024]{1,0:T(8,128)(2,1)S(1)}, u32[]{:S(2)}, u32[]{:S(2)}) collective-permute-start(bf16[128,1024]{1,0:T(8,128)(2,1)S(1)} %collective-permute-done.7.refs_0_), channel_id=1, source_target_pairs={{0,2},{2,0},{4,6},{6,4},{8,10},{10,8},{12,14},{14,12},{16,18},{18,... | collective-permute-start | bytes 786440 | tf_op jit(solution)/shard_map/ppermute | solution.py:162
  28.3 1.2 %collective-permute-done.8.refs_1_ = bf16[128,1024]{1,0:T(8,128)(2,1)S(1)} collective-permute-done((bf16[128,1024]{1,0:T(8,128)(2,1)S(1)}, bf16[128,1024]{1,0:T(8,128)(2,1)S(1)}, u32[]{:S(2)}, u32[]{:S(2)}) %collective-permute-start.8) | collective-permute-done | bytes 262176 | tf_op jit(solution)/shard_map/ppermute | solution.py:162
  29.4 2.9 %parts.5 = (f32[128,1024]{1,0:T(8,128)S(1)}, f32[8,128]{1,0:T(8,128)S(1)}, f32[128,1024]{1,0:T(8,128)S(1)}, f32[8,128]{1,0:T(8,128)S(1)}) custom-call(bf16[128,1024]{1,0:T(8,128)(2,1)S(1)} %collective-permute-done.7.refs_0_, bf16[128,1024]{1,0:T(8,128)(2,1)S(1)} %collective-permute-done.8.refs_1_, bf16[2048,1024]{1,0:T(8,128)(2,1)S(1)} %bitcast.338, ...), custom_call_target="tpu_custom_call" | custom-call | tf_op jit(solution)/shard_map/parts/pallas_call | solution.py:87
  32.3 0.4 collective-permute-start.9
  32.8 2.2 %collective-permute-start.13 = (f16[128,1024]{1,0:T(8,128)(2,1)S(1)}, f16[128,1024]{1,0:T(8,128)(2,1)S(1)}, u32[]{:S(2)}, u32[]{:S(2)}) collective-permute-start(f16[128,1024]{1,0:T(8,128)(2,1)S(1)} %divide_convert_fusion.1), channel_id=1, source_target_pairs={{4,0},{6,2},{8,4},{10,6},{12,8},{14,10},{16,12},{18,14},{20,16},{2... | collective-permute-start | bytes 786440 | tf_op jit(solution)/shard_map/ppermute | solution.py:162
  35.1 0.4 collective-permute-start.6
  35.5 0.9 %collective-permute-start.14 = (f32[2,128]{1,0:T(2,128)S(1)}, f32[2,128]{1,0:T(2,128)S(1)}, u32[]{:S(2)}, u32[]{:S(2)}) collective-permute-start(f32[2,128]{1,0:T(2,128)S(1)} %broadcast_select_fusion.3), channel_id=1, source_target_pairs={{4,0},{6,2},{8,4},{10,6},{12,8},{14,10},{16,12},{18,14},{20,16},{2... | collective-permute-start | bytes 3080 | tf_op jit(solution)/shard_map/ppermute | solution.py:162
  36.5 1.4 %collective-permute-done.10 = f16[128,1024]{1,0:T(8,128)(2,1)S(1)} collective-permute-done((f16[128,1024]{1,0:T(8,128)(2,1)S(1)}, f16[128,1024]{1,0:T(8,128)(2,1)S(1)}, u32[]{:S(2)}, u32[]{:S(2)}) %collective-permute-start.10) | collective-permute-done | bytes 262176 | tf_op jit(solution)/shard_map/ppermute | solution.py:162
  38.2 1.0 %collective-permute-start.11 = (f16[128,1024]{1,0:T(8,128)(2,1)S(1)}, f16[128,1024]{1,0:T(8,128)(2,1)S(1)}, u32[]{:S(2)}, u32[]{:S(2)}) collective-permute-start(f16[128,1024]{1,0:T(8,128)(2,1)S(1)} %divide_convert_fusion), channel_id=1, source_target_pairs={{4,0},{6,2},{8,4},{10,6},{12,8},{14,10},{16,12},{18,14},{20,16},{2... | collective-permute-start | bytes 786440 | tf_op jit(solution)/shard_map/ppermute | solution.py:162
  39.2 10.4 %collective-permute-done.14 = f32[2,128]{1,0:T(2,128)S(1)} collective-permute-done((f32[2,128]{1,0:T(2,128)S(1)}, f32[2,128]{1,0:T(2,128)S(1)}, u32[]{:S(2)}, u32[]{:S(2)}) %collective-permute-start.14) | collective-permute-done | bytes 1056 | tf_op jit(solution)/shard_map/ppermute | solution.py:162
  49.6 5.2 %collective-permute-start.12 = (f32[2,128]{1,0:T(2,128)S(1)}, f32[2,128]{1,0:T(2,128)S(1)}, u32[]{:S(2)}, u32[]{:S(2)}) collective-permute-start(f32[2,128]{1,0:T(2,128)S(1)} %broadcast_select_fusion.2), channel_id=1, source_target_pairs={{4,0},{6,2},{8,4},{10,6},{12,8},{14,10},{16,12},{18,14},{20,16},{2... | collective-permute-start | bytes 3080 | tf_op jit(solution)/shard_map/ppermute | solution.py:162
  55.1 1.6 %collective-permute-start.17 = (f16[128,1024]{1,0:T(8,128)(2,1)S(1)}, f16[128,1024]{1,0:T(8,128)(2,1)S(1)}, u32[]{:S(2)}, u32[]{:S(2)}) collective-permute-start(f16[128,1024]{1,0:T(8,128)(2,1)S(1)} %fusion.8), channel_id=1, source_target_pairs={{0,1},{1,0},{2,3},{3,2},{4,5},{5,4},{6,7},{7,6},{8,9},{9,8},{10,11... | collective-permute-start | bytes 786440 | tf_op jit(solution)/shard_map/ppermute | solution.py:162
  56.7 0.5 collective-permute-start.18
  57.6 5.8 %collective-permute-done.18 = f32[2,128]{1,0:T(2,128)S(1)} collective-permute-done((f32[2,128]{1,0:T(2,128)S(1)}, f32[2,128]{1,0:T(2,128)S(1)}, u32[]{:S(2)}, u32[]{:S(2)}) %collective-permute-start.18) | collective-permute-done | bytes 1056 | tf_op jit(solution)/shard_map/ppermute | solution.py:162
  63.4 1.6 %collective-permute-start.16 = (f16[128,1024]{1,0:T(8,128)(2,1)S(1)}, f16[128,1024]{1,0:T(8,128)(2,1)S(1)}, u32[]{:S(2)}, u32[]{:S(2)}) collective-permute-start(f16[128,1024]{1,0:T(8,128)(2,1)S(1)} %fusion.9), channel_id=1, source_target_pairs={{0,1},{1,0},{2,3},{3,2},{4,5},{5,4},{6,7},{7,6},{8,9},{9,8},{10,11... | collective-permute-start | bytes 786440 | tf_op jit(solution)/shard_map/ppermute | solution.py:162
  65.0 0.5 collective-permute-start.15
  65.8 0.7 %store.2 = (bf16[256,1024]{1,0:T(8,128)(2,1)}, f32[1,256]{1,0:T(1,128)}) custom-call(bf16[128,1024]{1,0:T(8,128)(2,1)S(1)} %multiply_convert_fusion.attributed_ref, f32[1,128]{1,0:T(1,128)S(1)} %log_add_fusion.1.level_ref), custom_call_target="tpu_custom_call" | custom-call | tf_op jit(solution)/shard_map/store/pallas_call | solution.py:115
  66.5 3.4 %collective-permute-done.15 = f32[2,128]{1,0:T(2,128)S(1)} collective-permute-done((f32[2,128]{1,0:T(2,128)S(1)}, f32[2,128]{1,0:T(2,128)S(1)}, u32[]{:S(2)}, u32[]{:S(2)}) %collective-permute-start.15) | collective-permute-done | bytes 1056 | tf_op jit(solution)/shard_map/ppermute | solution.py:162
  70.2 0.7 %store.3 = (bf16[256,1024]{1,0:T(8,128)(2,1)}, f32[1,256]{1,0:T(1,128)}) custom-call(bf16[128,1024]{1,0:T(8,128)(2,1)S(1)} %multiply_convert_fusion.1.attributed_ref, f32[1,128]{1,0:T(1,128)S(1)} %log_add_fusion.2.level_ref, bf16[256,1024]{1,0:T(8,128)(2,1)} %get-tuple-element.58.refs_0_, ...), custom_call_target="tpu_custom_call", output_to_operand_aliasing={{0}: (2, {}), {1}: (3, {})} | custom-call | tf_op jit(solution)/shard_map/store/pallas_call | solution.py:115
  (51 shorter events, 2.7 us)
Async XLA Ops:
  1.7 12.4 %collective-permute-start.1 = (bf16[128,1024]{1,0:T(8,128)(2,1)S(1)}, bf16[128,1024]{1,0:T(8,128)(2,1)S(1)}, u32[]{:S(2)}, u32[]{:S(2)}) collective-permute-start(bf16[128,1024]{1,0:T(8,128)(2,1)S(1)} %get-tuple-element.72), channel_id=1, source_target_pairs={{0,4},{2,6},{4,8},{6,10},{8,12},{10,14},{12,16},{14,18},{16,20},{1... | collective-permute-start | bytes 786440 | tf_op jit(solution)/shard_map/ppermute | solution.py:162
  4.7 4.3 %copy-start.1 = (bf16[1,2048,1024]{2,1,0:T(8,128)(2,1)S(1)}, bf16[1,2048,1024]{2,1,0:T(8,128)(2,1)}, u32[]{:S(2)}) copy-start(bf16[1,2048,1024]{2,1,0:T(8,128)(2,1)} %param.5) | copy-start | bytes 12582916
  9.1 5.0 %copy-start.2 = (bf16[256,1024]{1,0:T(8,128)(2,1)S(1)}, bf16[256,1024]{1,0:T(8,128)(2,1)}, u32[]{:S(2)}) copy-start(bf16[256,1024]{1,0:T(8,128)(2,1)} %param.3) | copy-start | bytes 1572868
  9.1 6.6 %copy-start = (bf16[1,2048,1024]{2,1,0:T(8,128)(2,1)S(1)}, bf16[1,2048,1024]{2,1,0:T(8,128)(2,1)}, u32[]{:S(2)}) copy-start(bf16[1,2048,1024]{2,1,0:T(8,128)(2,1)} %param.4) | copy-start | bytes 12582916
  14.1 1.5 %collective-permute-start.2 = (bf16[128,1024]{1,0:T(8,128)(2,1)S(1)}, bf16[128,1024]{1,0:T(8,128)(2,1)S(1)}, u32[]{:S(2)}, u32[]{:S(2)}) collective-permute-start(bf16[128,1024]{1,0:T(8,128)(2,1)S(1)} %collective-permute-done.1.refs_0_), channel_id=1, source_target_pairs={{0,2},{2,0},{4,6},{6,4},{8,10},{10,8},{12,14},{14,12},{16,18},{18,... | collective-permute-start | bytes 786440 | tf_op jit(solution)/shard_map/ppermute | solution.py:162
  14.1 10.4 %collective-permute-start = (bf16[256,1024]{1,0:T(8,128)(2,1)S(1)}, bf16[256,1024]{1,0:T(8,128)(2,1)S(1)}, u32[]{:S(2)}, u32[]{:S(2)}) collective-permute-start(bf16[256,1024]{1,0:T(8,128)(2,1)S(1)} %copy-done.2), channel_id=1, source_target_pairs={{0,2},{2,8},{4,6},{6,12},{8,10},{10,16},{12,14},{14,20},{16,18},{1... | collective-permute-start | bytes 1572872 | tf_op jit(solution)/shard_map/ppermute | solution.py:162
  14.6 12.8 %collective-permute-start.7 = (bf16[128,1024]{1,0:T(8,128)(2,1)S(1)}, bf16[128,1024]{1,0:T(8,128)(2,1)S(1)}, u32[]{:S(2)}, u32[]{:S(2)}) collective-permute-start(bf16[128,1024]{1,0:T(8,128)(2,1)S(1)} %get-tuple-element.73), channel_id=1, source_target_pairs={{0,4},{2,6},{4,8},{6,10},{8,12},{10,14},{12,16},{14,18},{16,20},{1... | collective-permute-start | bytes 786440 | tf_op jit(solution)/shard_map/ppermute | solution.py:162
  18.5 1.2 %collective-permute-start.3 = (f32[8,128]{1,0:T(8,128)S(1)}, f32[8,128]{1,0:T(8,128)S(1)}, u32[]{:S(2)}, u32[]{:S(2)}) collective-permute-start(f32[8,128]{1,0:T(8,128)S(1)} %get-tuple-element.37), channel_id=1, source_target_pairs={{0,2},{2,0},{4,6},{6,4},{8,10},{10,8},{12,14},{14,12},{16,18},{18,... | collective-permute-start | bytes 12296 | tf_op jit(solution)/shard_map/ppermute | solution.py:162
  18.7 1.5 %collective-permute-start.4 = (f16[128,1024]{1,0:T(8,128)(2,1)S(1)}, f16[128,1024]{1,0:T(8,128)(2,1)S(1)}, u32[]{:S(2)}, u32[]{:S(2)}) collective-permute-start(f16[128,1024]{1,0:T(8,128)(2,1)S(1)} %convert_element_type.61), channel_id=1, source_target_pairs={{0,2},{2,0},{4,6},{6,4},{8,10},{10,8},{12,14},{14,12},{16,18},{18,... | collective-permute-start | bytes 786440 | tf_op jit(solution)/shard_map/ppermute | solution.py:162
  27.4 2.0 %collective-permute-start.8 = (bf16[128,1024]{1,0:T(8,128)(2,1)S(1)}, bf16[128,1024]{1,0:T(8,128)(2,1)S(1)}, u32[]{:S(2)}, u32[]{:S(2)}) collective-permute-start(bf16[128,1024]{1,0:T(8,128)(2,1)S(1)} %collective-permute-done.7.refs_0_), channel_id=1, source_target_pairs={{0,2},{2,0},{4,6},{6,4},{8,10},{10,8},{12,14},{14,12},{16,18},{18,... | collective-permute-start | bytes 786440 | tf_op jit(solution)/shard_map/ppermute | solution.py:162
  32.3 4.1 %collective-permute-start.9 = (f32[8,128]{1,0:T(8,128)S(1)}, f32[8,128]{1,0:T(8,128)S(1)}, u32[]{:S(2)}, u32[]{:S(2)}) collective-permute-start(f32[8,128]{1,0:T(8,128)S(1)} %get-tuple-element.47), channel_id=1, source_target_pairs={{0,2},{2,0},{4,6},{6,4},{8,10},{10,8},{12,14},{14,12},{16,18},{18,... | collective-permute-start | bytes 12296 | tf_op jit(solution)/shard_map/ppermute | solution.py:162
  32.8 16.8 %collective-permute-start.13 = (f16[128,1024]{1,0:T(8,128)(2,1)S(1)}, f16[128,1024]{1,0:T(8,128)(2,1)S(1)}, u32[]{:S(2)}, u32[]{:S(2)}) collective-permute-start(f16[128,1024]{1,0:T(8,128)(2,1)S(1)} %divide_convert_fusion.1), channel_id=1, source_target_pairs={{4,0},{6,2},{8,4},{10,6},{12,8},{14,10},{16,12},{18,14},{20,16},{2... | collective-permute-start | bytes 786440 | tf_op jit(solution)/shard_map/ppermute | solution.py:162
  34.9 19.9 %collective-permute-start.5 = (f16[256,1024]{1,0:T(8,128)(2,1)S(1)}, f16[256,1024]{1,0:T(8,128)(2,1)S(1)}, u32[]{:S(2)}, u32[]{:S(2)}) collective-permute-start(f16[256,1024]{1,0:T(8,128)(2,1)S(1)} %convert_element_type.64), channel_id=1, source_target_pairs={{2,0},{8,2},{6,4},{12,6},{10,8},{16,10},{14,12},{20,14},{18,16},{2... | collective-permute-start | bytes 1572872 | tf_op jit(solution)/shard_map/ppermute | solution.py:162
  35.1 19.7 %collective-permute-start.6 = (f32[8,256]{1,0:T(8,128)S(1)}, f32[8,256]{1,0:T(8,128)S(1)}, u32[]{:S(2)}, u32[]{:S(2)}) collective-permute-start(f32[8,256]{1,0:T(8,128)S(1)} %get-tuple-element.41), channel_id=1, source_target_pairs={{2,0},{8,2},{6,4},{12,6},{10,8},{16,10},{14,12},{20,14},{18,16},{2... | collective-permute-start | bytes 24584 | tf_op jit(solution)/shard_map/ppermute | solution.py:162
  35.5 14.1 %collective-permute-start.14 = (f32[2,128]{1,0:T(2,128)S(1)}, f32[2,128]{1,0:T(2,128)S(1)}, u32[]{:S(2)}, u32[]{:S(2)}) collective-permute-start(f32[2,128]{1,0:T(2,128)S(1)} %broadcast_select_fusion.3), channel_id=1, source_target_pairs={{4,0},{6,2},{8,4},{10,6},{12,8},{14,10},{16,12},{18,14},{20,16},{2... | collective-permute-start | bytes 3080 | tf_op jit(solution)/shard_map/ppermute | solution.py:162
  36.4 1.5 %collective-permute-start.10 = (f16[128,1024]{1,0:T(8,128)(2,1)S(1)}, f16[128,1024]{1,0:T(8,128)(2,1)S(1)}, u32[]{:S(2)}, u32[]{:S(2)}) collective-permute-start(f16[128,1024]{1,0:T(8,128)(2,1)S(1)} %convert_element_type.66), channel_id=1, source_target_pairs={{0,2},{2,0},{4,6},{6,4},{8,10},{10,8},{12,14},{14,12},{16,18},{18,... | collective-permute-start | bytes 786440 | tf_op jit(solution)/shard_map/ppermute | solution.py:162
  38.2 19.1 %collective-permute-start.11 = (f16[128,1024]{1,0:T(8,128)(2,1)S(1)}, f16[128,1024]{1,0:T(8,128)(2,1)S(1)}, u32[]{:S(2)}, u32[]{:S(2)}) collective-permute-start(f16[128,1024]{1,0:T(8,128)(2,1)S(1)} %divide_convert_fusion), channel_id=1, source_target_pairs={{4,0},{6,2},{8,4},{10,6},{12,8},{14,10},{16,12},{18,14},{20,16},{2... | collective-permute-start | bytes 786440 | tf_op jit(solution)/shard_map/ppermute | solution.py:162
  49.6 7.6 %collective-permute-start.12 = (f32[2,128]{1,0:T(2,128)S(1)}, f32[2,128]{1,0:T(2,128)S(1)}, u32[]{:S(2)}, u32[]{:S(2)}) collective-permute-start(f32[2,128]{1,0:T(2,128)S(1)} %broadcast_select_fusion.2), channel_id=1, source_target_pairs={{4,0},{6,2},{8,4},{10,6},{12,8},{14,10},{16,12},{18,14},{20,16},{2... | collective-permute-start | bytes 3080 | tf_op jit(solution)/shard_map/ppermute | solution.py:162
  55.1 8.3 %collective-permute-start.17 = (f16[128,1024]{1,0:T(8,128)(2,1)S(1)}, f16[128,1024]{1,0:T(8,128)(2,1)S(1)}, u32[]{:S(2)}, u32[]{:S(2)}) collective-permute-start(f16[128,1024]{1,0:T(8,128)(2,1)S(1)} %fusion.8), channel_id=1, source_target_pairs={{0,1},{1,0},{2,3},{3,2},{4,5},{5,4},{6,7},{7,6},{8,9},{9,8},{10,11... | collective-permute-start | bytes 786440 | tf_op jit(solution)/shard_map/ppermute | solution.py:162
  56.7 6.7 %collective-permute-start.18 = (f32[2,128]{1,0:T(2,128)S(1)}, f32[2,128]{1,0:T(2,128)S(1)}, u32[]{:S(2)}, u32[]{:S(2)}) collective-permute-start(f32[2,128]{1,0:T(2,128)S(1)} %broadcast_select_fusion.1), channel_id=1, source_target_pairs={{0,1},{1,0},{2,3},{3,2},{4,5},{5,4},{6,7},{7,6},{8,9},{9,8},{10,11... | collective-permute-start | bytes 3080 | tf_op jit(solution)/shard_map/ppermute | solution.py:162
  63.4 6.5 %collective-permute-start.16 = (f16[128,1024]{1,0:T(8,128)(2,1)S(1)}, f16[128,1024]{1,0:T(8,128)(2,1)S(1)}, u32[]{:S(2)}, u32[]{:S(2)}) collective-permute-start(f16[128,1024]{1,0:T(8,128)(2,1)S(1)} %fusion.9), channel_id=1, source_target_pairs={{0,1},{1,0},{2,3},{3,2},{4,5},{5,4},{6,7},{7,6},{8,9},{9,8},{10,11... | collective-permute-start | bytes 786440 | tf_op jit(solution)/shard_map/ppermute | solution.py:162
  65.0 4.9 %collective-permute-start.15 = (f32[2,128]{1,0:T(2,128)S(1)}, f32[2,128]{1,0:T(2,128)S(1)}, u32[]{:S(2)}, u32[]{:S(2)}) collective-permute-start(f32[2,128]{1,0:T(2,128)S(1)} %broadcast_select_fusion), channel_id=1, source_target_pairs={{0,1},{1,0},{2,3},{3,2},{4,5},{5,4},{6,7},{7,6},{8,9},{9,8},{10,11... | collective-permute-start | bytes 3080 | tf_op jit(solution)/shard_map/ppermute | solution.py:162
